TPU v7x, 512 devices: a 8x2x16 block of a 8x8x16 slice. The times are simulated.
512 devices in a mesh: group: 2 (over y), ha: 16 (over x, core), wa: 16 (over z).
Axes of the slice: x: 8, y: 2, z: 16, core: 2. Of those that a mesh axis runs over, the one named last changes fastest.
The devices are a block of a 8x8x16 slice.
Arguments:
- queries: bfloat16 [4, 128, 128, 1536], P('group', 'ha', 'wa'), parts along dimension 0, may hold values from -6 to 6
- keys: bfloat16 [4, 128, 128, 1536], P('group', 'ha', 'wa'), parts along dimension 0, may hold values from -6 to 6
- values: bfloat16 [4, 128, 128, 1536], P('group', 'ha', 'wa'), parts along dimension 0, may hold values from -6 to 6
- out_grad: bfloat16 [4, 128, 128, 1536], P('group', 'ha', 'wa'), parts along dimension 0, may hold values from -96 to 96
- log_norm: float32 [12, 4, 128, 128], P(None, 'group', 'ha', 'wa'), parts along dimension 1, may hold values from 6.5 to 7.5
- delta_rows: float32 [12, 4, 128, 128], P(None, 'group', 'ha', 'wa'), parts along dimension 1, may hold values from -360 to 360
- text_keys: bfloat16 [64, 1536], P('group'), parts along dimension 0, may hold values from -6 to 6
- text_values: bfloat16 [64, 1536], P('group'), parts along dimension 0, may hold values from -6 to 6
- window_table: int32 [16, 16, 9], replicated, may hold values 0 or 1
Outputs:
- query_grad: bfloat16 [4, 128, 128, 1536], P('group', 'ha', 'wa'), parts along dimension 0
- key_grad: bfloat16 [4, 128, 128, 1536], P('group', 'ha', 'wa'), parts along dimension 0
- value_grad: bfloat16 [4, 128, 128, 1536], P('group', 'ha', 'wa'), parts along dimension 0
- text_key_grad: bfloat16 [64, 1536], P('group'), parts along dimension 0
- text_value_grad: bfloat16 [64, 1536], P('group'), parts along dimension 0
There are 2 independent parts, one for each index of `group`. A program takes and returns all parts, laid end to end along the dimension named above; an argument that names none is the same for every part. Nothing has to cross between parts.
All inputs are finite; a program needn't handle non-finite values.
Results may differ from a plain program's by a relative error of at most 0.001.
The roundings to bfloat16 on the way count: a program that leaves them out, or rounds other values in their place, can miss the bound.
Values may be sent and summed in bfloat16 or wider, within the bound.
No kernel may reach another device: no remote copies, remote signals or barrier semaphores. Data moves between devices by JAX's collectives and lax.ppermute only.
A program may use at most 64 MiB of HBM per device.

v0:
```python
import math

import jax
import jax.numpy as jnp
from jax import lax
from jax.sharding import Mesh
from jax.sharding import PartitionSpec as P

HEADS = 12
HDIM = 128
TILE = 8
HALO = 2
HA = ("ha_0", "ha_1")
HA_WA = ("ha_0", "ha_1", "wa")


def passed_along(value, axis, steps):
    count = lax.axis_size(axis)
    pairs = [(source, (source + steps) % count) for source in range(count)]
    return lax.ppermute(value, axis, pairs)


def with_halo(cells, sides, width):
    for axis, dim in sides:
        count = lax.axis_size(axis)
        head = lax.slice_in_dim(cells, 0, width, axis=dim)
        tail = lax.slice_in_dim(cells, cells.shape[dim] - width, cells.shape[dim], axis=dim)
        cells = jnp.concatenate(
            [
                lax.ppermute(tail, axis, [(i, (i + 1) % count) for i in range(count)]),
                cells,
                lax.ppermute(head, axis, [((i + 1) % count, i) for i in range(count)]),
            ],
            axis=dim,
        )
    return cells


def one_axis_at_a_time(shard, axes):
    for axis in axes:
        shard = lax.psum(shard, axis)
    return shard


def tile_grads(query_rows, cotangent_rows, norm_rows, delta_part, key_rows, value_rows, cell_mask):
    score_scale = 1.0 / math.sqrt(query_rows.shape[-1])
    scores = (
        jnp.einsum("qhd,khd->hqk", query_rows, key_rows, preferred_element_type=jnp.float32)
        * score_scale
    )
    probs = jnp.exp(scores - norm_rows[:, :, None])
    if cell_mask is not None:
        probs = probs * cell_mask[None, None, :]
    probs_half = probs.astype(jnp.bfloat16)
    value_part = jnp.einsum(
        "hqk,qhd->khd", probs_half, cotangent_rows, preferred_element_type=jnp.float32
    )
    prob_grad = jnp.einsum(
        "qhd,khd->hqk", cotangent_rows, value_rows, preferred_element_type=jnp.float32
    )
    score_grad = (probs * (prob_grad - delta_part[:, :, None])).astype(jnp.bfloat16)
    query_part = (
        jnp.einsum("hqk,khd->qhd", score_grad, key_rows, preferred_element_type=jnp.float32)
        * score_scale
    )
    key_part = (
        jnp.einsum("hqk,qhd->khd", score_grad, query_rows, preferred_element_type=jnp.float32)
        * score_scale
    )
    return (query_part, key_part, value_part)


def send_cols(strip, offset):
    return passed_along(strip, "wa", offset)


def send_rows(strip, offset):
    return passed_along(strip, HA, offset)


def fold_band(buffer, along, mover):
    lower = lax.slice_in_dim(buffer, 0, HALO, axis=along)
    middle = lax.slice_in_dim(buffer, HALO, HALO + TILE, axis=along)
    upper = lax.slice_in_dim(buffer, HALO + TILE, TILE + 2 * HALO, axis=along)
    from_before = mover(upper, 1)
    from_after = mover(lower, -1)
    widths_low = [(0, 0)] * buffer.ndim
    widths_high = [(0, 0)] * buffer.ndim
    widths_low[along] = (0, TILE - HALO)
    widths_high[along] = (TILE - HALO, 0)
    return middle + jnp.pad(from_before, widths_low) + jnp.pad(from_after, widths_high)


def local(
    queries, keys, values, out_grad, log_norm, delta_rows, text_keys, text_values, window_table
):
    frames, tile_side, _, width = queries.shape
    window_side = TILE + 2 * HALO
    stacked = jnp.stack((keys, values))
    window = with_halo(stacked, ((HA, 2), ("wa", 3)), HALO)
    row_tile = lax.axis_index(HA)
    col_tile = lax.axis_index("wa")
    anchor = jnp.zeros((), jnp.int32)
    pattern = (
        lax.dynamic_slice(window_table, (row_tile, col_tile, anchor), (1, 1, 9))
        .reshape(3, 3)
        .astype(jnp.float32)
    )
    position = jnp.arange(window_side, dtype=jnp.int32)
    block_of = (position >= HALO).astype(jnp.int32) + (position >= HALO + TILE).astype(jnp.int32)
    one_hot = (block_of[:, None] == jnp.arange(3, dtype=jnp.int32)[None, :]).astype(jnp.float32)
    cell_grid = jnp.dot(
        jnp.dot(one_hot, pattern, precision=lax.Precision.HIGHEST),
        one_hot.T,
        precision=lax.Precision.HIGHEST,
    )
    cell_mask = jnp.broadcast_to(cell_grid[None], (frames, window_side, window_side)).reshape(-1)
    query_rows = queries.reshape(-1, HEADS, HDIM)
    cotangent_rows = out_grad.reshape(-1, HEADS, HDIM)
    norm_rows = log_norm.reshape(HEADS, -1)
    delta_part = delta_rows.reshape(HEADS, -1)
    key_rows = window[0].reshape(-1, HEADS, HDIM)
    value_rows = window[1].reshape(-1, HEADS, HDIM)
    video_query, video_key, video_value = tile_grads(
        query_rows, cotangent_rows, norm_rows, delta_part, key_rows, value_rows, cell_mask
    )
    text_query, text_key, text_value = tile_grads(
        query_rows,
        cotangent_rows,
        norm_rows,
        delta_part,
        text_keys.reshape(-1, HEADS, HDIM),
        text_values.reshape(-1, HEADS, HDIM),
        None,
    )
    query_grad = (
        (video_query + text_query).astype(jnp.bfloat16).reshape(frames, tile_side, tile_side, width)
    )
    text_total = one_axis_at_a_time(jnp.stack((text_key, text_value)), HA_WA)
    buffer = jnp.stack((video_key, video_value)).reshape(2, frames, window_side, window_side, width)
    buffer = fold_band(buffer, 3, send_cols)
    buffer = fold_band(buffer, 2, send_rows)
    text_key_grad = text_total[0].reshape(-1, width).astype(jnp.bfloat16)
    text_value_grad = text_total[1].reshape(-1, width).astype(jnp.bfloat16)
    return (
        query_grad,
        buffer[0].astype(jnp.bfloat16),
        buffer[1].astype(jnp.bfloat16),
        text_key_grad,
        text_value_grad,
    )


def solution(mesh):
    split = Mesh(
        mesh.devices.reshape(mesh.shape["group"], 8, 2, mesh.shape["wa"]),
        ("group", "ha_0", "ha_1", "wa"),
    )
    return jax.shard_map(
        local,
        mesh=split,
        in_specs=(
            P("group", HA, "wa", None),
            P("group", HA, "wa", None),
            P("group", HA, "wa", None),
            P("group", HA, "wa", None),
            P(None, "group", HA, "wa"),
            P(None, "group", HA, "wa"),
            P("group", None),
            P("group", None),
            P(),
        ),
        out_specs=(
            P("group", HA, "wa", None),
            P("group", HA, "wa", None),
            P("group", HA, "wa", None),
            P("group", None),
            P("group", None),
        ),
        check_vma=False,
    )
```

profile of v0, /device:TPU:65, one launch (start us, length us, event | category | flops | bytes accessed | tf_op | source)
XLA Modules:
  0.0 264.9 jit_solution(15022201213251635187)
XLA Ops:
  7.3 1.1 pad_maximum_fusion.7
  8.4 2.7 %collective-permute-start = (bf16[2,2,2,8,1536]{4,3,2,1,0:T(8,128)(2,1)S(1)}, bf16[2,2,2,8,1536]{4,3,2,1,0:T(8,128)(2,1)S(1)}, u32[]{:S(2)}, u32[]{:S(2)}) collective-permute-start(bf16[2,2,2,8,1536]{4,3,2,1,0:T(8,128)(2,1)S(1)} %get-tuple-element.20), channel_id=1, source_target_pairs={{0,16},{16,32},{32,48},{48,64},{64,80},{80,96},{96,112},{112,128},... | collective-permute-start | bytes 589832 | tf_op jit(solution)/shard_map/ppermute | solution.py:30
  11.1 38.8 %collective-permute-start.1 = (bf16[2,2,2,8,1536]{4,3,2,1,0:T(8,128)(2,1)S(1)}, bf16[2,2,2,8,1536]{4,3,2,1,0:T(8,128)(2,1)S(1)}, u32[]{:S(2)}, u32[]{:S(2)}) collective-permute-start(bf16[2,2,2,8,1536]{4,3,2,1,0:T(8,128)(2,1)S(1)} %get-tuple-element.21), channel_id=1, source_target_pairs={{16,0},{32,16},{48,32},{64,48},{80,64},{96,80},{112,96},{128,112},... | collective-permute-start | bytes 589832 | tf_op jit(solution)/shard_map/ppermute | solution.py:32
  50.0 0.9 copy.34
  50.9 0.9 copy.37
  51.8 1.3 reshape.49
  54.5 0.8 pad_maximum_fusion.1
  55.5 1.0 convert_reduce_fusion
  56.6 1.1 pad_maximum_fusion.5
  57.7 1.9 collective-permute-start.2
  59.6 4.9 %collective-permute-start.3 = (bf16[2,2,12,2,1536]{4,3,2,1,0:T(2,128)(2,1)S(1)}, bf16[2,2,12,2,1536]{4,3,2,1,0:T(2,128)(2,1)S(1)}, u32[]{:S(2)}, u32[]{:S(2)}) collective-permute-start(bf16[2,2,12,2,1536]{4,3,2,1,0:T(2,128)(2,1)S(1)} %get-tuple-element.17), channel_id=1, source_target_pairs={{1,0},{2,1},{3,2},{4,3},{5,4},{6,5},{7,6},{8,7},{9,8},{10,9},{11,1... | collective-permute-start | bytes 884744 | tf_op jit(solution)/shard_map/ppermute | solution.py:32
  65.0 67.7 %all-reduce.8.cloned.1.call-done = f32[2,32,12,128]{3,1,2,0:T(8,128)} async-done(((f32[2,32,12,128]{3,1,2,0:T(8,128)}), f32[2,32,12,128]{3,1,2,0:T(8,128)}) %all-reduce.8.cloned.1.call-update) | async-done | bytes 393232 | tf_op jit(solution)/shard_map/psum | solution.py:41
  132.9 1.5 pad_maximum_fusion
  134.5 1.7 reshape_squeeze.9
  136.2 0.8 reshape_squeeze.8
  137.6 1.6 convolution_bitcast_fusion
  141.5 1.0 reshape.53
  142.5 2.5 copy.50
  145.0 2.4 stack.30
  147.4 4.0 %copy.52 = f32[288,12,128]{2,1,0:T(8,128)} copy(f32[288,12,128]{2,0,1:T(8,128)} %convolution_bitcast_fusion) | data formatting | bytes 3538944 | tf_op jit(solution)/shard_map/hqk,qhd->khd/transpose | solution.py:55
  151.3 3.2 %stack.31 = f32[1,2,12,12,1536]{4,3,2,1,0:T(8,128)} reshape(f32[288,12,128]{2,1,0:T(8,128)} %copy.52) | data formatting | bytes 3538944 | tf_op jit(solution)/shard_map/stack | solution.py:140
  154.8 1.4 copy-done.1
  156.4 2.1 copy-done.2
  159.0 3.3 %collective-permute-start.4 = (f32[2,2,12,2,1536]{4,3,2,1,0:T(2,128)S(1)}, f32[2,2,12,2,1536]{4,3,2,1,0:T(2,128)S(1)}, u32[]{:S(2)}, u32[]{:S(2)}) collective-permute-start(f32[2,2,12,2,1536]{4,3,2,1,0:T(2,128)S(1)} %get-tuple-element.10), channel_id=1, source_target_pairs={{0,1},{1,2},{2,3},{3,4},{4,5},{5,6},{6,7},{7,8},{8,9},{9,10},{10,1... | collective-permute-start | bytes 1769480 | tf_op jit(solution)/shard_map/ppermute | solution.py:20
  162.3 5.5 %collective-permute-start.5 = (f32[2,2,12,2,1536]{4,3,2,1,0:T(2,128)S(1)}, f32[2,2,12,2,1536]{4,3,2,1,0:T(2,128)S(1)}, u32[]{:S(2)}, u32[]{:S(2)}) collective-permute-start(f32[2,2,12,2,1536]{4,3,2,1,0:T(2,128)S(1)} %get-tuple-element.11), channel_id=1, source_target_pairs={{0,15},{1,0},{2,1},{3,2},{4,3},{5,4},{6,5},{7,6},{8,7},{9,8},{10,9... | collective-permute-start | bytes 1769480 | tf_op jit(solution)/shard_map/ppermute | solution.py:20
  167.8 17.0 %all-reduce.10.cloned.1.call-done = f32[2,32,12,128]{3,1,2,0:T(8,128)} async-done(((f32[2,32,12,128]{3,1,2,0:T(8,128)}), f32[2,32,12,128]{3,1,2,0:T(8,128)}) %all-reduce.10.cloned.1.call-update) | async-done | bytes 393232 | tf_op jit(solution)/shard_map/psum | solution.py:41
  184.8 46.7 %all-reduce.11 = bf16[2,32,12,128]{3,1,2,0:T(8,128)(2,1)S(1)} all-reduce(f32[2,32,12,128]{3,1,2,0:T(8,128)} %all-reduce.10.cloned.1.call-done), channel_id=1, replica_groups=mesh['group'=2,'ha_0'=8,'ha_1'=2,'wa'=16] {'wa'}, use_global_device_ids=true, to_apply=%region_2.0 | all-reduce | flops 98304 | bytes 589824 | tf_op jit(solution)/shard_map/psum | solution.py:41
  231.7 3.0 %fusion = f32[2,2,12,8,1536]{4,3,2,1,0:T(8,128)S(1)} fusion(f32[2,2,12,12,1536]{4,3,2,1,0:T(8,128)} %copy-done.2, f32[2,2,12,2,1536]{4,3,2,1,0:T(2,128)S(1)} %collective-permute-done.5, f32[2,2,12,2,1536]{4,3,2,1,0:T(2,128)S(1)} %collective-permute-done.4), kind=kLoop, calls=%fused_computation.1 | loop fusion | flops 1179648 | bytes 5898240 | tf_op jit(solution)/shard_map/add | solution.py:91
  234.8 15.0 %collective-permute-start.6 = (f32[2,2,2,8,1536]{4,3,2,1,0:T(8,128)S(1)}, f32[2,2,2,8,1536]{4,3,2,1,0:T(8,128)S(1)}, u32[]{:S(2)}, u32[]{:S(2)}) collective-permute-start(f32[2,2,2,8,1536]{4,3,2,1,0:T(8,128)S(1)} %get-tuple-element.12), channel_id=1, source_target_pairs={{0,16},{16,32},{32,48},{48,64},{64,80},{80,96},{96,112},{112,128},... | collective-permute-start | bytes 1179656 | tf_op jit(solution)/shard_map/ppermute | solution.py:20
  250.4 4.0 %collective-permute-done.6 = f32[2,2,2,8,1536]{4,3,2,1,0:T(8,128)S(1)} collective-permute-done((f32[2,2,2,8,1536]{4,3,2,1,0:T(8,128)S(1)}, f32[2,2,2,8,1536]{4,3,2,1,0:T(8,128)S(1)}, u32[]{:S(2)}, u32[]{:S(2)}) %collective-permute-start.6) | collective-permute-done | bytes 393248 | tf_op jit(solution)/shard_map/ppermute | solution.py:20
  254.4 2.5 collective-permute-done.7
  257.1 0.9 slice_bitcast_fusion
  (56 shorter events, 7.1 us)
Async XLA Ops:
  7.2 46.2 %copy-start = (bf16[32,1536]{1,0:T(8,128)(2,1)S(1)}, bf16[32,1536]{1,0:T(8,128)(2,1)}, u32[]{:S(2)}) copy-start(bf16[32,1536]{1,0:T(8,128)(2,1)} %param.15) | copy-start | bytes 294916
  7.2 45.9 %copy-start.8 = (bf16[2,8,8,1536]{3,2,1,0:T(8,128)(2,1)S(1)}, bf16[2,8,8,1536]{3,2,1,0:T(8,128)(2,1)}, u32[]{:S(2)}) copy-start(bf16[2,8,8,1536]{3,2,1,0:T(8,128)(2,1)} %param.12) | copy-start | bytes 1179652
  7.2 125.6 %all-reduce.8.cloned.1.call-start = ((), (), s32[]{:S(2)}) async-start(), calls=%async_computation | async-start | bytes 786432 | tf_op jit(solution)/shard_map/psum | solution.py:41
  7.3 46.7 %copy-start.9 = (bf16[32,1536]{1,0:T(8,128)(2,1)S(1)}, bf16[32,1536]{1,0:T(8,128)(2,1)}, u32[]{:S(2)}) copy-start(bf16[32,1536]{1,0:T(8,128)(2,1)} %param.16) | copy-start | bytes 294916
  8.4 48.1 %collective-permute-start = (bf16[2,2,2,8,1536]{4,3,2,1,0:T(8,128)(2,1)S(1)}, bf16[2,2,2,8,1536]{4,3,2,1,0:T(8,128)(2,1)S(1)}, u32[]{:S(2)}, u32[]{:S(2)}) collective-permute-start(bf16[2,2,2,8,1536]{4,3,2,1,0:T(8,128)(2,1)S(1)} %get-tuple-element.20), channel_id=1, source_target_pairs={{0,16},{16,32},{32,48},{48,64},{64,80},{80,96},{96,112},{112,128},... | collective-permute-start | bytes 589832 | tf_op jit(solution)/shard_map/ppermute | solution.py:30
  11.1 45.4 %collective-permute-start.1 = (bf16[2,2,2,8,1536]{4,3,2,1,0:T(8,128)(2,1)S(1)}, bf16[2,2,2,8,1536]{4,3,2,1,0:T(8,128)(2,1)S(1)}, u32[]{:S(2)}, u32[]{:S(2)}) collective-permute-start(bf16[2,2,2,8,1536]{4,3,2,1,0:T(8,128)(2,1)S(1)} %get-tuple-element.21), channel_id=1, source_target_pairs={{16,0},{32,16},{48,32},{64,48},{80,64},{96,80},{112,96},{128,112},... | collective-permute-start | bytes 589832 | tf_op jit(solution)/shard_map/ppermute | solution.py:32
  53.4 3.2 %copy-start.4 = (bf16[2,8,8,1536]{3,2,1,0:T(8,128)(2,1)S(1)}, bf16[2,8,8,1536]{3,2,1,0:T(8,128)(2,1)}, u32[]{:S(2)}) copy-start(bf16[2,8,8,1536]{3,2,1,0:T(8,128)(2,1)} %param.11) | copy-start | bytes 1179652
  53.4 3.2 %copy-start.5 = (bf16[2,8,8,1536]{3,2,1,0:T(8,128)(2,1)S(1)}, bf16[2,8,8,1536]{3,2,1,0:T(8,128)(2,1)}, u32[]{:S(2)}) copy-start(bf16[2,8,8,1536]{3,2,1,0:T(8,128)(2,1)} %param.10) | copy-start | bytes 1179652
  54.3 78.5 %copy-start.6 = (bf16[12,128,32]{1,2,0:T(8,128)(2,1)}, bf16[12,128,32]{1,2,0:T(8,128)(2,1)S(1)}, u32[]{:S(2)}) copy-start(bf16[12,128,32]{1,2,0:T(8,128)(2,1)S(1)} %fusion.11) | copy-start | bytes 294916
  55.4 129.4 %all-reduce.10.cloned.1.call-start = ((), (), s32[]{:S(2)}) async-start(), calls=%async_computation.1 | async-start | bytes 786432 | tf_op jit(solution)/shard_map/psum | solution.py:41
  57.7 75.1 %collective-permute-start.2 = (bf16[2,2,12,2,1536]{4,3,2,1,0:T(2,128)(2,1)}, bf16[2,2,12,2,1536]{4,3,2,1,0:T(2,128)(2,1)S(1)}, u32[]{:S(2)}, u32[]{:S(2)}) collective-permute-start(bf16[2,2,12,2,1536]{4,3,2,1,0:T(2,128)(2,1)} %get-tuple-element.16), channel_id=1, source_target_pairs={{0,1},{1,2},{2,3},{3,4},{4,5},{5,6},{6,7},{7,8},{8,9},{9,10},{10,1... | collective-permute-start | bytes 884744 | tf_op jit(solution)/shard_map/ppermute | solution.py:30
  59.6 73.2 %collective-permute-start.3 = (bf16[2,2,12,2,1536]{4,3,2,1,0:T(2,128)(2,1)S(1)}, bf16[2,2,12,2,1536]{4,3,2,1,0:T(2,128)(2,1)S(1)}, u32[]{:S(2)}, u32[]{:S(2)}) collective-permute-start(bf16[2,2,12,2,1536]{4,3,2,1,0:T(2,128)(2,1)S(1)} %get-tuple-element.17), channel_id=1, source_target_pairs={{1,0},{2,1},{3,2},{4,3},{5,4},{6,5},{7,6},{8,7},{9,8},{10,9},{11,1... | collective-permute-start | bytes 884744 | tf_op jit(solution)/shard_map/ppermute | solution.py:32
  137.6 1.6 copy-start.3
  139.7 1.0 copy-start.7
  154.5 1.7 copy-start.1
  156.4 2.1 copy-start.2
  159.0 72.6 %collective-permute-start.4 = (f32[2,2,12,2,1536]{4,3,2,1,0:T(2,128)S(1)}, f32[2,2,12,2,1536]{4,3,2,1,0:T(2,128)S(1)}, u32[]{:S(2)}, u32[]{:S(2)}) collective-permute-start(f32[2,2,12,2,1536]{4,3,2,1,0:T(2,128)S(1)} %get-tuple-element.10), channel_id=1, source_target_pairs={{0,1},{1,2},{2,3},{3,4},{4,5},{5,6},{6,7},{7,8},{8,9},{9,10},{10,1... | collective-permute-start | bytes 1769480 | tf_op jit(solution)/shard_map/ppermute | solution.py:20
  162.3 69.4 %collective-permute-start.5 = (f32[2,2,12,2,1536]{4,3,2,1,0:T(2,128)S(1)}, f32[2,2,12,2,1536]{4,3,2,1,0:T(2,128)S(1)}, u32[]{:S(2)}, u32[]{:S(2)}) collective-permute-start(f32[2,2,12,2,1536]{4,3,2,1,0:T(2,128)S(1)} %get-tuple-element.11), channel_id=1, source_target_pairs={{0,15},{1,0},{2,1},{3,2},{4,3},{5,4},{6,5},{7,6},{8,7},{9,8},{10,9... | collective-permute-start | bytes 1769480 | tf_op jit(solution)/shard_map/ppermute | solution.py:20
  234.8 19.7 %collective-permute-start.6 = (f32[2,2,2,8,1536]{4,3,2,1,0:T(8,128)S(1)}, f32[2,2,2,8,1536]{4,3,2,1,0:T(8,128)S(1)}, u32[]{:S(2)}, u32[]{:S(2)}) collective-permute-start(f32[2,2,2,8,1536]{4,3,2,1,0:T(8,128)S(1)} %get-tuple-element.12), channel_id=1, source_target_pairs={{0,16},{16,32},{32,48},{48,64},{64,80},{80,96},{96,112},{112,128},... | collective-permute-start | bytes 1179656 | tf_op jit(solution)/shard_map/ppermute | solution.py:20
  249.7 7.2 %collective-permute-start.7 = (f32[2,2,2,8,1536]{4,3,2,1,0:T(8,128)S(1)}, f32[2,2,2,8,1536]{4,3,2,1,0:T(8,128)S(1)}, u32[]{:S(2)}, u32[]{:S(2)}) collective-permute-start(f32[2,2,2,8,1536]{4,3,2,1,0:T(8,128)S(1)} %get-tuple-element.13), channel_id=1, source_target_pairs={{0,240},{16,0},{32,16},{48,32},{64,48},{80,64},{96,80},{112,96},{1... | collective-permute-start | bytes 1179656 | tf_op jit(solution)/shard_map/ppermute | solution.py:20
Sparse Core Ops, SparseCore 0:
  55.5 77.2 all-reduce.7
  135.7 49.0 all-reduce.9
where the time goes:
time: 267 us; the launch traced here: 265 us
  waiting for transfers between devices  91.4 us (34%)
  starting transfers between devices  72.2 us (27%)
  blocking collectives  46.7 us (17%)
  local copies, waits for them, and re-layouts  26 us (10%)
  between operations  14.4 us (5%)
  other arithmetic  8.7 us (3%)
  matrix products  5.44 us (2%)
    psum x2, waiting for transfers between devices, one_axis_at_a_time(): shard = lax.psum(shard, axis)  84.8 us
    psum x1, blocking collectives, one_axis_at_a_time(): shard = lax.psum(shard, axis)  46.7 us
    ppermute x2, starting transfers between devices, with_halo(): lax.ppermute(head, axis, [((i + 1) % count, i) for i in range(count)])  43.7 us
    ppermute x4, starting transfers between devices, passed_along(): return lax.ppermute(value, axis, pairs)  23.7 us
    ppermute x4, waiting for transfers between devices, passed_along(): return lax.ppermute(value, axis, pairs)  6.49 us
    another operation x3, local copies, waits for them, and re-layouts, local(): jnp.stack((video_key, video_value))  5.77 us
  transfers between devices with their start and end apart: 10, of which 4 were waited for; matrix products, arithmetic and copies ran while one was open for 12% of the time, Pallas kernels for 0%

commit v1 on v0

v1 whole, which is shorter than its diff:
```python
import functools
import math

import jax
import jax.numpy as jnp
import numpy as np
from jax import lax
from jax.experimental import pallas as pl
from jax.experimental.pallas import tpu as pltpu
from jax.sharding import Mesh
from jax.sharding import PartitionSpec as P

HEADS = 12
HDIM = 128
TILE = 8
HALO = 2
HA = ("ha_0", "ha_1")
F32 = jnp.float32
BF16 = jnp.bfloat16
SCALE = 1.0 / math.sqrt(HDIM)

FRAMES = 2
OWN = FRAMES * TILE * TILE
SIDE = FRAMES * TILE * HALO
CORNER = HALO * HALO
BAND = HALO * TILE + 2 * CORNER
ENDS = FRAMES * BAND


def nt(a, b):
    return lax.dot_general(a, b, (((1,), (1,)), ((), ())), preferred_element_type=F32)


def nn(a, b):
    return lax.dot_general(a, b, (((1,), (0,)), ((), ())), preferred_element_type=F32)


def tn(a, b):
    return lax.dot_general(a, b, (((0,), (0,)), ((), ())), preferred_element_type=F32)


def exact(a, b):
    return lax.dot_general(
        a, b, (((1,), (0,)), ((), ())), precision=lax.Precision.HIGHEST, preferred_element_type=F32
    )


def own_row(frame, row, col):
    return frame * TILE * TILE + row * TILE + col


def side_row(frame, row, col):
    return (frame * TILE + row) * HALO + col


def select_sides():
    out = np.zeros((2, SIDE, OWN), np.float32)
    for side, first in enumerate((0, TILE - HALO)):
        for frame in range(FRAMES):
            for row in range(TILE):
                for col in range(HALO):
                    out[side, side_row(frame, row, col), own_row(frame, row, first + col)] = 1
    return out


def select_ends():
    out = np.zeros((2, ENDS, OWN + 2 * SIDE), np.float32)
    for end, first in enumerate((0, TILE - HALO)):
        for frame in range(FRAMES):
            at = frame * BAND
            for row in range(HALO):
                for col in range(TILE):
                    out[end, at, own_row(frame, first + row, col)] = 1
                    at += 1
            for side in range(2):
                for row in range(HALO):
                    for col in range(HALO):
                        out[end, at, OWN + side * SIDE + side_row(frame, first + row, col)] = 1
                        at += 1
    return out


SIDES = select_sides()
BANDS = select_ends()


def sides_kernel(select_ref, keys_ref, values_ref, left_ref, right_ref):
    for part, ref in enumerate((keys_ref, values_ref)):
        rows = ref[...]
        at = pl.ds(part * SIDE, SIDE)
        left_ref[at, :] = nn(select_ref[0], rows).astype(BF16)
        right_ref[at, :] = nn(select_ref[1], rows).astype(BF16)


def ends_kernel(select_ref, keys_ref, values_ref, left_ref, right_ref, top_ref, bottom_ref):
    for part, ref in enumerate((keys_ref, values_ref)):
        at = pl.ds(part * SIDE, SIDE)
        rows = jnp.concatenate([ref[...], left_ref[at, :], right_ref[at, :]], axis=0)
        to = pl.ds(part * ENDS, ENDS)
        top_ref[to, :] = nn(select_ref[0], rows).astype(BF16)
        bottom_ref[to, :] = nn(select_ref[1], rows).astype(BF16)


def text_kernel(
    core_ref, norm_ref, delta_ref, query_ref, out_grad_ref, key_ref, value_ref, grad_ref, stats_ref
):
    lane = lax.broadcasted_iota(jnp.int32, (8, 128), 1)
    row = lax.broadcasted_iota(jnp.int32, (8, 128), 0)
    spread = (lax.rem(lane, 8) == row).astype(F32)
    count = HEADS * 16
    wide_lane = lax.broadcasted_iota(jnp.int32, (count, 128), 1)
    wide_row = lax.broadcasted_iota(jnp.int32, (count, 128), 0)
    here = lax.div(wide_lane, 8) == lax.rem(wide_row, 16)
    head = lax.broadcasted_iota(jnp.int32, (16, count), 0)
    of = lax.div(lax.broadcasted_iota(jnp.int32, (16, count), 1), 16)
    gather = (head == of).astype(F32)
    stats = []
    for which, ref in enumerate((norm_ref, delta_ref)):
        wide = exact(ref[...], spread)
        wide = jnp.where(here, wide, 0.0)
        rows = exact(gather, wide)
        stats_ref[pl.ds(which * 16, 16), :] = rows
        stats.append(rows)
    norm, delta = stats
    core = core_ref[0]
    text = key_ref.shape[0]
    for h in range(HEADS):
        cols = slice(h * HDIM, (h + 1) * HDIM)
        q = query_ref[:, cols]
        g = out_grad_ref[:, cols]
        probs = jnp.exp(nt(key_ref[:, cols], q) * SCALE - norm[h : h + 1])
        prob_grad = nt(value_ref[:, cols], g)
        score_grad = (probs * (prob_grad - delta[h : h + 1])).astype(BF16)
        to = pl.ds(h * text, text)
        grad_ref[core, to, :] = nn(score_grad, q) * SCALE
        grad_ref[1 - core, to, :] = nn(probs.astype(BF16), g)


def video_kernel(
    live_ref,
    stats_ref,
    query_ref,
    out_grad_ref,
    keys_ref,
    values_ref,
    left_ref,
    right_ref,
    top_ref,
    bottom_ref,
    text_key_ref,
    text_value_ref,
    query_grad_ref,
    own_ref,
    left_grad_ref,
    right_grad_ref,
    top_grad_ref,
    bottom_grad_ref,
    mask_ref,
):
    text = text_key_ref.shape[0]
    parts = ((OWN, None), (SIDE, None), (SIDE, None), (ENDS, None), (ENDS, None))

    def live(block):
        return live_ref[block].astype(F32)

    mask_ref[pl.ds(0, OWN), :] = jnp.full((OWN, HDIM), live(4), F32)
    mask_ref[pl.ds(OWN, SIDE), :] = jnp.full((SIDE, HDIM), live(3), F32)
    mask_ref[pl.ds(OWN + SIDE, SIDE), :] = jnp.full((SIDE, HDIM), live(5), F32)
    band = lax.rem(lax.broadcasted_iota(jnp.int32, (ENDS, HDIM), 0), BAND)
    for end, first in ((0, 0), (1, 6)):
        at = OWN + 2 * SIDE + end * ENDS
        mask_ref[pl.ds(at, ENDS), :] = jnp.where(
            band < HALO * TILE,
            live(first + 1),
            jnp.where(band < HALO * TILE + CORNER, live(first), live(first + 2)),
        )
    window = OWN + 2 * SIDE + 2 * ENDS
    mask_ref[pl.ds(window, text), :] = jnp.ones((text, HDIM), F32)

    def rows_of(part, cols):
        side = slice(part * SIDE, (part + 1) * SIDE)
        ends = slice(part * ENDS, (part + 1) * ENDS)
        own, words = ((keys_ref, text_key_ref), (values_ref, text_value_ref))[part]
        return jnp.concatenate(
            [
                own[:, cols],
                left_ref[side, cols],
                right_ref[side, cols],
                top_ref[ends, cols],
                bottom_ref[ends, cols],
                words[:, cols],
            ],
            axis=0,
        )

    for h in range(HEADS):
        cols = slice(h * HDIM, (h + 1) * HDIM)
        q = query_ref[:, cols]
        g = out_grad_ref[:, cols]
        k = rows_of(0, cols)
        v = rows_of(1, cols)
        norm = stats_ref[h : h + 1, :]
        delta = stats_ref[16 + h : 17 + h, :]
        probs = jnp.exp(nt(k, q) * SCALE - norm) * mask_ref[...]
        score_grad = (probs * (nt(v, g) - delta)).astype(BF16)
        query_grad_ref[:, cols] = (tn(score_grad, k) * SCALE).astype(BF16)
        grads = (
            nn(score_grad[:window], q) * SCALE,
            nn(probs[:window].astype(BF16), g),
        )
        for part, grad in enumerate(grads):
            at = 0
            for ref, rows in (
                (own_ref, OWN),
                (left_grad_ref, SIDE),
                (right_grad_ref, SIDE),
                (top_grad_ref, ENDS),
                (bottom_grad_ref, ENDS),
            ):
                ref[part * rows : (part + 1) * rows, cols] = grad[at : at + rows]
                at += rows


def corners_kernel(
    select_ref, left_ref, right_ref, above_ref, below_ref, left_out_ref, right_out_ref
):
    for part in range(2):
        side = pl.ds(part * SIDE, SIDE)
        ends = pl.ds(part * ENDS, ENDS)
        bands = jnp.concatenate([above_ref[ends, :], below_ref[ends, :]], axis=0)
        left_out_ref[side, :] = left_ref[side, :] + exact(select_ref[0], bands)
        right_out_ref[side, :] = right_ref[side, :] + exact(select_ref[1], bands)


def sum_kernel(
    select_ref, own_ref, left_ref, right_ref, above_ref, below_ref, key_ref, value_ref
):
    for part, out in enumerate((key_ref, value_ref)):
        side = pl.ds(part * SIDE, SIDE)
        ends = pl.ds(part * ENDS, ENDS)
        rows = jnp.concatenate(
            [left_ref[side, :], right_ref[side, :], above_ref[ends, :], below_ref[ends, :]], axis=0
        )
        total = own_ref[pl.ds(part * OWN, OWN), :] + exact(select_ref[...], rows)
        out[...] = total.astype(BF16)


def words_kernel(parts_ref, key_ref, value_ref):
    text = key_ref.shape[0]
    rows = parts_ref.shape[1]
    for part, out in enumerate((key_ref, value_ref)):
        for h in range(HEADS):
            for at in range(0, text, 16):
                row = h * text + at
                piece = parts_ref[2 * (row // rows) + part, pl.ds(row % rows, 16), :]
                out[at : at + 16, h * HDIM : (h + 1) * HDIM] = piece


def call(kernel, outs, *args, smem=0, scratch=(), flops=1000000):
    whole = pl.BlockSpec(memory_space=pltpu.VMEM)
    scalars = pl.BlockSpec(memory_space=pltpu.SMEM)
    return pl.pallas_call(
        kernel,
        out_shape=[jax.ShapeDtypeStruct(shape, dtype) for shape, dtype in outs],
        in_specs=[scalars] * smem + [whole] * (len(args) - smem),
        out_specs=[whole] * len(outs),
        scratch_shapes=list(scratch),
        compiler_params=pltpu.CompilerParams(vmem_limit_bytes=12 * 1024 * 1024),
        cost_estimate=pl.CostEstimate(flops=flops, bytes_accessed=1000000, transcendentals=0),
        name=kernel.__name__,
    )(*args)


def shifted(value, axis, steps):
    count = lax.axis_size(axis)
    return lax.ppermute(value, axis, [(i, (i + steps) % count) for i in range(count)])


def to_first(value, axis):
    count = lax.axis_size(axis)
    step = 1
    while step < count:
        pairs = [(i, (i + step) % count) for i in range(step, count, 2 * step)]
        value = value + lax.ppermute(value, axis, pairs)
        step *= 2
    return value


def from_first(value, axis):
    count = lax.axis_size(axis)
    value = jnp.where(lax.axis_index(axis) == 0, value, jnp.zeros_like(value))
    step = count // 2
    while step:
        pairs = [(i, i + step) for i in range(0, count, 2 * step)]
        value = value + lax.ppermute(value, axis, pairs)
        step //= 2
    return value


def local(
    queries, keys, values, out_grad, log_norm, delta_rows, text_keys, text_values, window_table
):
    shape = queries.shape
    width = shape[-1]
    text = text_keys.shape[0]
    q = queries.reshape(OWN, width)
    g = out_grad.reshape(OWN, width)
    k = keys.reshape(OWN, width)
    v = values.reshape(OWN, width)
    anchor = jnp.zeros((), jnp.int32)
    live = lax.dynamic_slice(
        window_table, (lax.axis_index(HA), lax.axis_index("wa"), anchor), (1, 1, 9)
    ).reshape(9)
    core = lax.axis_index("ha_1").reshape(1)

    words, stats = call(
        text_kernel,
        [((2, HEADS * text, HDIM), F32), ((32, HDIM), F32)],
        core,
        log_norm.reshape(-1, TILE),
        delta_rows.reshape(-1, TILE),
        q,
        g,
        text_keys,
        text_values,
        smem=1,
    )

    left, right = call(
        sides_kernel,
        [((2 * SIDE, width), BF16)] * 2,
        jnp.asarray(SIDES, BF16),
        k,
        v,
    )
    from_right = shifted(left, "wa", -1)
    from_left = shifted(right, "wa", 1)

    half = words[0] + shifted(words[1], "ha_1", 1)
    pieces = lax.all_to_all(half, "ha_0", 0, 0, tiled=True)
    piece = pieces.reshape(lax.axis_size("ha_0"), -1, HDIM).sum(axis=0)
    piece = to_first(piece, "wa")

    top, bottom = call(
        ends_kernel,
        [((2 * ENDS, width), BF16)] * 2,
        jnp.asarray(BANDS, BF16),
        k,
        v,
        from_left,
        from_right,
    )
    from_below = shifted(top, HA, -1)
    from_above = shifted(bottom, HA, 1)
    query_grad, own, left_grad, right_grad, top_grad, bottom_grad = call(
        video_kernel,
        [
            ((OWN, width), BF16),
            ((2 * OWN, width), F32),
            ((2 * SIDE, width), F32),
            ((2 * SIDE, width), F32),
            ((2 * ENDS, width), F32),
            ((2 * ENDS, width), F32),
        ],
        live,
        stats,
        q,
        g,
        k,
        v,
        from_left,
        from_right,
        from_above,
        from_below,
        text_keys,
        text_values,
        smem=1,
        scratch=[pltpu.VMEM((OWN + 2 * SIDE + 2 * ENDS + text, HDIM), F32)],
    )
    above = shifted(bottom_grad, HA, 1)
    below = shifted(top_grad, HA, -1)
    back = np.concatenate([BANDS[0].T, BANDS[1].T], axis=1)
    left_grad, right_grad = call(
        corners_kernel,
        [((2 * SIDE, width), F32)] * 2,
        jnp.asarray(np.stack([back[OWN : OWN + SIDE], back[OWN + SIDE :]]), F32),
        left_grad,
        right_grad,
        above,
        below,
    )
    after = shifted(left_grad, "wa", -1)
    before = shifted(right_grad, "wa", 1)
    back = np.concatenate([SIDES[0].T, SIDES[1].T, back[:OWN]], axis=1)
    key_grad, value_grad = call(
        sum_kernel,
        [((OWN, width), BF16)] * 2,
        jnp.asarray(back, F32),
        own,
        before,
        after,
        above,
        below,
    )

    piece = from_first(piece.astype(BF16), "wa")
    count = lax.axis_size(HA)
    pieces = lax.all_to_all(jnp.tile(piece, (count, 1)), HA, 0, 0, tiled=True)
    text_key_grad, text_value_grad = call(
        words_kernel,
        [((text, width), BF16)] * 2,
        pieces.reshape(count, -1, HDIM),
    )
    return (
        query_grad.reshape(shape),
        key_grad.reshape(shape),
        value_grad.reshape(shape),
        text_key_grad,
        text_value_grad,
    )


def solution(mesh):
    split = Mesh(
        mesh.devices.reshape(mesh.shape["group"], 8, 2, mesh.shape["wa"]),
        ("group", "ha_0", "ha_1", "wa"),
    )
    return jax.shard_map(
        local,
        mesh=split,
        in_specs=(
            P("group", HA, "wa", None),
            P("group", HA, "wa", None),
            P("group", HA, "wa", None),
            P("group", HA, "wa", None),
            P(None, "group", HA, "wa"),
            P(None, "group", HA, "wa"),
            P("group", None),
            P("group", None),
            P(),
        ),
        out_specs=(
            P("group", HA, "wa", None),
            P("group", HA, "wa", None),
            P("group", HA, "wa", None),
            P("group", None),
            P("group", None),
        ),
        check_vma=False,
    )
```

time: 267 us -> 172 us (0.64)
  waiting for transfers between devices: 91.4 us -> 31.8 us
  blocking collectives: 46.7 us -> 25.2 us
  Pallas kernels: 0 us -> 13.6 us
  between operations: 14.4 us -> 0.97 us
  local copies, waits for them, and re-layouts: 26 us -> 18.3 us
  other arithmetic: 8.7 us -> 1.71 us
  starting transfers between devices: 72.2 us -> 78.8 us
  matrix products: 5.44 us -> 0 us
    psum x2 -> x0, waiting for transfers between devices: 84.8 us -> none  [one_axis_at_a_time(): shard = lax.psum(shard, axis)]
    psum x1 -> x0, blocking collectives: 46.7 us -> none  [one_axis_at_a_time(): shard = lax.psum(shard, axis)]
    ppermute x8 -> x17, waiting for transfers between devices: 6.5 us -> 31.8 us  [the longest x4 29.4 us: to_first(): value = value + lax.ppermute(value, axis, pairs)]
    all_to_all x0 -> x1, blocking collectives: none -> 25.2 us  [local(): pieces = lax.all_to_all(jnp.tile(piece, (count, 1)), HA, 0, 0, tiled=True)]
    unnamed x21 -> x60, local copies, waits for them, and re-layouts: 3.81 us -> 18 us
    pallas_call x0 -> x7, Pallas kernels: none -> 13.6 us  [call(): pl.pallas_call(kernel, out_shape=[jax.ShapeDtypeStruct(shape, dtype) for...]
    another operation x5 -> x1, local copies, waits for them, and re-layouts: 8.24 us -> 0.03 us  [local(): pieces = lax.all_to_all(jnp.tile(piece, (count, 1)), HA, 0, 0, tiled=True)]
    all_to_all x0 -> x1, starting transfers between devices: none -> 5.89 us  [local(): pieces = lax.all_to_all(half, 'ha_0', 0, 0, tiled=True)]
  transfers between devices with their start and end apart: 10 -> 18, of which waited for: 4 -> 7; matrix products, arithmetic and copies ran while one was open for 12% -> 2% of each run, Pallas kernels for 0% -> 6%
where the time goes in v1:
time: 172 us; the launch traced here: 170 us
  starting transfers between devices  78.8 us (46%)
  waiting for transfers between devices  31.8 us (18%)
  blocking collectives  25.2 us (15%)
  local copies, waits for them, and re-layouts  18.3 us (11%)
  Pallas kernels  13.6 us (8%)
    ppermute x9, starting transfers between devices, shifted(): lax.ppermute(value, axis, [(i, (i + steps) % count) for i in range(count)])  62 us
    ppermute x4, waiting for transfers between devices, to_first(): value = value + lax.ppermute(value, axis, pairs)  29.4 us
    all_to_all x1, blocking collectives, local(): pieces = lax.all_to_all(jnp.tile(piece, (count, 1)), HA, 0, 0, tiled=True)  25.2 us
    unnamed x60, local copies, waits for them, and re-layouts  18 us
    pallas_call x7, Pallas kernels, call(): pl.pallas_call(kernel, out_shape=[jax.ShapeDtypeStruct(shape, dtype) for...  13.6 us
    all_to_all x1, starting transfers between devices, local(): pieces = lax.all_to_all(half, 'ha_0', 0, 0, tiled=True)  5.89 us
    ppermute x4, starting transfers between devices, from_first(): value = value + lax.ppermute(value, axis, pairs)  5.55 us
    ppermute x4, starting transfers between devices, to_first(): value = value + lax.ppermute(value, axis, pairs)  5.34 us
  transfers between devices with their start and end apart: 18, of which 7 were waited for; matrix products, arithmetic and copies ran while one was open for 2% of the time, Pallas kernels for 6%

profile of v1, /device:TPU:65, one launch (start us, length us, event | category | flops | bytes accessed | tf_op | source)
XLA Modules:
  0.0 170.5 jit_solution(1540323685973063359)
XLA Ops:
  0.7 1.0 copy-done.1
  1.7 1.0 copy-done.3
  3.7 6.6 %collective-permute-start = (bf16[64,1536]{1,0:T(8,128)(2,1)S(1)}, bf16[64,1536]{1,0:T(8,128)(2,1)S(1)}, u32[]{:S(2)}, u32[]{:S(2)}) collective-permute-start(bf16[64,1536]{1,0:T(8,128)(2,1)S(1)} %get-tuple-element.24), channel_id=1, source_target_pairs={{0,1},{1,2},{2,3},{3,4},{4,5},{5,6},{6,7},{7,8},{8,9},{9,10},{10,1... | collective-permute-start | bytes 589832 | tf_op jit(solution)/shard_map/ppermute | solution.py:276
  10.3 39.9 %collective-permute-start.1 = (bf16[64,1536]{1,0:T(8,128)(2,1)S(1)}, bf16[64,1536]{1,0:T(8,128)(2,1)S(1)}, u32[]{:S(2)}, u32[]{:S(2)}) collective-permute-start(bf16[64,1536]{1,0:T(8,128)(2,1)S(1)} %get-tuple-element.25), channel_id=1, source_target_pairs={{0,15},{1,0},{2,1},{3,2},{4,3},{5,4},{6,5},{7,6},{8,7},{9,8},{10,9... | collective-permute-start | bytes 589832 | tf_op jit(solution)/shard_map/ppermute | solution.py:276
  50.3 1.0 copy.20
  51.3 1.0 copy.21
  52.3 1.0 copy-done.5
  53.3 1.0 copy-done.7
  56.1 2.7 %text_kernel.1 = (f32[2,384,128]{2,1,0:T(8,128)S(1)}, f32[32,128]{1,0:T(8,128)S(1)}) custom-call(s32[1]{0:T(128)} %bitcast.core_ref, f32[192,8]{1,0:T(8,128)S(1)} %bitcast.25, f32[192,8]{1,0:T(8,128)S(1)} %bitcast.26, bf16[128,1536]{1,0:T(8,128)(2,1)S(1)} %bitcast.21, bf16[128,1536]{1,0:T(8,128)(2,1)S(1)} %bitcast.23, bf16[32,1536]{1,0:T(8,128)(2,1)S(1)} %copy-done.11, ...), custom_call_target="tpu_custom_call" | custom-call | flops 1000000 | bytes 1000000 | tf_op jit(solution)/shard_map/text_kernel/pallas_call | solution.py:262
  58.8 4.1 %collective-permute-start.8 = (f32[384,128]{1,0:T(8,128)S(1)}, f32[384,128]{1,0:T(8,128)S(1)}, u32[]{:S(2)}, u32[]{:S(2)}) collective-permute-start(f32[384,128]{1,0:T(8,128)S(1)} %slice_bitcast_fusion), channel_id=1, source_target_pairs={{0,16},{16,0},{1,17},{17,1},{2,18},{18,2},{3,19},{19,3},{4,20},{20... | collective-permute-start | bytes 589832 | tf_op jit(solution)/shard_map/ppermute | solution.py:276
  63.0 1.2 ends_kernel.1
  65.5 5.9 %all-to-all-start = ((f32[8,48,128]{2,1,0:T(8,128)}), f32[8,48,128]{2,1,0:T(8,128)}, u32[]{:S(2)}, u32[]{:S(2)}) async-start(f32[8,48,128]{2,1,0:T(8,128)} %bitcast.27), calls=%async_computation | async-start | bytes 393216 | tf_op jit(solution)/shard_map/all_to_all | solution.py:340
  77.6 5.2 %video_kernel.1 = (bf16[128,1536]{1,0:T(8,128)(2,1)}, f32[256,1536]{1,0:T(8,128)S(1)}, f32[64,1536]{1,0:T(8,128)S(1)}, f32[64,1536]{1,0:T(8,128)S(1)}, f32[96,1536]{1,0:T(8,128)}, /*index=5*/f32[96,1536]{1,0:T(8,128)}) custom-call(s32[9]{0:T(128)S(1)} %dynamic-slice_reduce_fusion.live_ref, f32[32,128]{1,0:T(8,128)S(1)} %copy-done.27, ...), custom_call_target="tpu_custom_call" | custom-call | flops 1000000 | bytes 1000000 | tf_op jit(solution)/shard_map/video_kernel/pallas_call | solution.py:262
  84.3 4.4 %collective-permute-start.4 = (f32[96,1536]{1,0:T(8,128)}, f32[96,1536]{1,0:T(8,128)S(1)}, u32[]{:S(2)}, u32[]{:S(2)}) collective-permute-start(f32[96,1536]{1,0:T(8,128)} %get-tuple-element.32), channel_id=1, source_target_pairs={{0,16},{16,32},{32,48},{48,64},{64,80},{80,96},{96,112},{112,128},... | collective-permute-start | bytes 1769480 | tf_op jit(solution)/shard_map/ppermute | solution.py:276
  89.6 1.3 collective-permute-start.9
  91.0 4.8 %collective-permute-done.9 = f32[48,128]{1,0:T(8,128)S(1)} collective-permute-done((f32[48,128]{1,0:T(8,128)S(1)}, f32[48,128]{1,0:T(8,128)S(1)}, u32[]{:S(2)}, u32[]{:S(2)}) %collective-permute-start.9) | collective-permute-done | bytes 24608 | tf_op jit(solution)/shard_map/ppermute | solution.py:284
  95.8 1.4 collective-permute-start.10
  97.2 5.4 %collective-permute-done.10 = f32[48,128]{1,0:T(8,128)S(1)} collective-permute-done((f32[48,128]{1,0:T(8,128)S(1)}, f32[48,128]{1,0:T(8,128)S(1)}, u32[]{:S(2)}, u32[]{:S(2)}) %collective-permute-start.10) | collective-permute-done | bytes 24608 | tf_op jit(solution)/shard_map/ppermute | solution.py:284
  102.6 1.3 collective-permute-start.11
  103.9 7.2 %collective-permute-done.11 = f32[48,128]{1,0:T(8,128)S(1)} collective-permute-done((f32[48,128]{1,0:T(8,128)S(1)}, f32[48,128]{1,0:T(8,128)S(1)}, u32[]{:S(2)}, u32[]{:S(2)}) %collective-permute-start.11) | collective-permute-done | bytes 24608 | tf_op jit(solution)/shard_map/ppermute | solution.py:284
  111.1 1.3 collective-permute-start.12
  112.4 12.0 %collective-permute-done.12 = f32[48,128]{1,0:T(8,128)S(1)} collective-permute-done((f32[48,128]{1,0:T(8,128)S(1)}, f32[48,128]{1,0:T(8,128)S(1)}, u32[]{:S(2)}, u32[]{:S(2)}) %collective-permute-start.12) | collective-permute-done | bytes 24608 | tf_op jit(solution)/shard_map/ppermute | solution.py:284
  124.4 1.7 collective-permute-start.13
  126.9 1.3 collective-permute-start.14
  129.0 1.3 collective-permute-start.15
  131.4 1.0 copy-done.18
  132.4 1.1 corners_kernel.1
  133.5 1.9 %collective-permute-start.6 = (f32[64,1536]{1,0:T(8,128)S(1)}, f32[64,1536]{1,0:T(8,128)S(1)}, u32[]{:S(2)}, u32[]{:S(2)}) collective-permute-start(f32[64,1536]{1,0:T(8,128)S(1)} %get-tuple-element.34), channel_id=1, source_target_pairs={{0,1},{1,2},{2,3},{3,4},{4,5},{5,6},{6,7},{7,8},{8,9},{9,10},{10,1... | collective-permute-start | bytes 1179656 | tf_op jit(solution)/shard_map/ppermute | solution.py:276
  135.5 4.6 %collective-permute-start.7 = (f32[64,1536]{1,0:T(8,128)S(1)}, f32[64,1536]{1,0:T(8,128)S(1)}, u32[]{:S(2)}, u32[]{:S(2)}) collective-permute-start(f32[64,1536]{1,0:T(8,128)S(1)} %get-tuple-element.35), channel_id=1, source_target_pairs={{0,15},{1,0},{2,1},{3,2},{4,3},{5,4},{6,5},{7,6},{8,7},{9,8},{10,9... | collective-permute-start | bytes 1179656 | tf_op jit(solution)/shard_map/ppermute | solution.py:276
  140.1 1.3 collective-permute-start.16
  142.3 25.2 %all_to_all.15.parts_ref = bf16[16,48,128]{2,1,0:T(8,128)(2,1)S(1)} all-to-all(bf16[16,48,128]{2,1,0:T(8,128)(2,1)S(1)} %tile.2), channel_id=1, replica_groups=mesh['group'=2,'ha_0'=8,'ha_1'=2,'wa'=16] {'ha_0','ha_1'}, dimensions={0} | all-to-all | bytes 393216 | tf_op jit(solution)/shard_map/all_to_all | solution.py:408
  168.2 2.3 %sum_kernel.1 = (bf16[128,1536]{1,0:T(8,128)(2,1)}, bf16[128,1536]{1,0:T(8,128)(2,1)}) custom-call(f32[128,160]{1,0:T(8,128)S(1)} %copy-done.23, f32[256,1536]{1,0:T(8,128)S(1)} %get-tuple-element.29.own_ref, f32[64,1536]{1,0:T(8,128)S(1)} %collective-permute-done.6.left_ref, f32[64,1536]{1,0:T(8,128)S(1)} %collective-permute-done.7.right_ref, ...), custom_call_target="tpu_custom_call" | custom-call | flops 1000000 | bytes 1000000 | tf_op jit(solution)/shard_map/sum_kernel/pallas_call | solution.py:262
  (85 shorter events, 17.0 us)
Async XLA Ops:
  0.6 70.7 %copy-start = (s32[16,16,9]{1,0,2:T(8,128)S(1)}, s32[16,16,9]{1,0,2:T(8,128)}, u32[]{:S(2)}) copy-start(s32[16,16,9]{1,0,2:T(8,128)} %param.21) | copy-start | bytes 27652
  0.6 1.0 copy-start.1
  3.4 59.6 %copy-start.2 = (bf16[2,8,8,1536]{3,2,1,0:T(8,128)(2,1)S(1)}, bf16[2,8,8,1536]{3,2,1,0:T(8,128)(2,1)}, u32[]{:S(2)}) copy-start(bf16[2,8,8,1536]{3,2,1,0:T(8,128)(2,1)} %param.14) | copy-start | bytes 1179652
  3.4 59.6 %copy-start.4 = (bf16[2,8,8,1536]{3,2,1,0:T(8,128)(2,1)S(1)}, bf16[2,8,8,1536]{3,2,1,0:T(8,128)(2,1)}, u32[]{:S(2)}) copy-start(bf16[2,8,8,1536]{3,2,1,0:T(8,128)(2,1)} %param.15) | copy-start | bytes 1179652
  3.4 59.6 %copy-start.24 = (bf16[2,48,192]{2,1,0:T(8,128)(2,1)S(1)}, bf16[2,48,192]{2,1,0:T(8,128)(2,1)}, u32[]{:S(2)}) copy-start(bf16[2,48,192]{2,1,0:T(8,128)(2,1)} %constant.34.clone.select_ref) | copy-start | bytes 110596
  3.7 59.2 %collective-permute-start = (bf16[64,1536]{1,0:T(8,128)(2,1)S(1)}, bf16[64,1536]{1,0:T(8,128)(2,1)S(1)}, u32[]{:S(2)}, u32[]{:S(2)}) collective-permute-start(bf16[64,1536]{1,0:T(8,128)(2,1)S(1)} %get-tuple-element.24), channel_id=1, source_target_pairs={{0,1},{1,2},{2,3},{3,4},{4,5},{5,6},{6,7},{7,8},{8,9},{9,10},{10,1... | collective-permute-start | bytes 589832 | tf_op jit(solution)/shard_map/ppermute | solution.py:276
  10.3 52.6 %collective-permute-start.1 = (bf16[64,1536]{1,0:T(8,128)(2,1)S(1)}, bf16[64,1536]{1,0:T(8,128)(2,1)S(1)}, u32[]{:S(2)}, u32[]{:S(2)}) collective-permute-start(bf16[64,1536]{1,0:T(8,128)(2,1)S(1)} %get-tuple-element.25), channel_id=1, source_target_pairs={{0,15},{1,0},{2,1},{3,2},{4,3},{5,4},{6,5},{7,6},{8,7},{9,8},{10,9... | collective-permute-start | bytes 589832 | tf_op jit(solution)/shard_map/ppermute | solution.py:276
  52.3 1.0 copy-start.5
  58.8 6.7 %copy-start.26 = (f32[32,128]{1,0:T(8,128)}, f32[32,128]{1,0:T(8,128)S(1)}, u32[]{:S(2)}) copy-start(f32[32,128]{1,0:T(8,128)S(1)} %get-tuple-element.23.stats_ref) | copy-start | bytes 49156
  58.8 14.4 %copy-start.6 = (bf16[2,8,8,1536]{3,2,1,0:T(8,128)(2,1)S(1)}, bf16[2,8,8,1536]{3,2,1,0:T(8,128)(2,1)}, u32[]{:S(2)}) copy-start(bf16[2,8,8,1536]{3,2,1,0:T(8,128)(2,1)} %param.13) | copy-start | bytes 1179652
  58.8 14.4 %copy-start.8 = (bf16[2,8,8,1536]{3,2,1,0:T(8,128)(2,1)S(1)}, bf16[2,8,8,1536]{3,2,1,0:T(8,128)(2,1)}, u32[]{:S(2)}) copy-start(bf16[2,8,8,1536]{3,2,1,0:T(8,128)(2,1)} %param.16) | copy-start | bytes 1179652
  58.8 14.4 %copy-start.12 = (bf16[32,1536]{1,0:T(8,128)(2,1)S(1)}, bf16[32,1536]{1,0:T(8,128)(2,1)}, u32[]{:S(2)}) copy-start(bf16[32,1536]{1,0:T(8,128)(2,1)} %text_key_ref.1) | copy-start | bytes 294916
  58.8 5.9 %collective-permute-start.8 = (f32[384,128]{1,0:T(8,128)S(1)}, f32[384,128]{1,0:T(8,128)S(1)}, u32[]{:S(2)}, u32[]{:S(2)}) collective-permute-start(f32[384,128]{1,0:T(8,128)S(1)} %slice_bitcast_fusion), channel_id=1, source_target_pairs={{0,16},{16,0},{1,17},{17,1},{2,18},{18,2},{3,19},{19,3},{4,20},{20... | collective-permute-start | bytes 589832 | tf_op jit(solution)/shard_map/ppermute | solution.py:276
  63.0 9.4 %copy-start.9 = (bf16[64,1536]{1,0:T(8,128)(2,1)}, bf16[64,1536]{1,0:T(8,128)(2,1)S(1)}, u32[]{:S(2)}) copy-start(bf16[64,1536]{1,0:T(8,128)(2,1)S(1)} %collective-permute-done.1.right_ref) | copy-start | bytes 589828
  64.2 7.5 %collective-permute-start.2 = (bf16[96,1536]{1,0:T(8,128)(2,1)}, bf16[96,1536]{1,0:T(8,128)(2,1)S(1)}, u32[]{:S(2)}, u32[]{:S(2)}) collective-permute-start(bf16[96,1536]{1,0:T(8,128)(2,1)} %get-tuple-element.26), channel_id=1, source_target_pairs={{0,16},{16,32},{32,48},{48,64},{64,80},{80,96},{96,112},{112,128},... | collective-permute-start | bytes 884744 | tf_op jit(solution)/shard_map/ppermute | solution.py:276
  64.3 8.1 %collective-permute-start.3 = (bf16[96,1536]{1,0:T(8,128)(2,1)S(1)}, bf16[96,1536]{1,0:T(8,128)(2,1)S(1)}, u32[]{:S(2)}, u32[]{:S(2)}) collective-permute-start(bf16[96,1536]{1,0:T(8,128)(2,1)S(1)} %get-tuple-element.27), channel_id=1, source_target_pairs={{0,240},{16,0},{32,16},{48,32},{64,48},{80,64},{96,80},{112,96},{1... | collective-permute-start | bytes 884744 | tf_op jit(solution)/shard_map/ppermute | solution.py:276
  65.5 23.2 %all-to-all-start = ((f32[8,48,128]{2,1,0:T(8,128)}), f32[8,48,128]{2,1,0:T(8,128)}, u32[]{:S(2)}, u32[]{:S(2)}) async-start(f32[8,48,128]{2,1,0:T(8,128)} %bitcast.27), calls=%async_computation | async-start | bytes 393216 | tf_op jit(solution)/shard_map/all_to_all | solution.py:340
  77.6 52.7 %copy-start.25 = (f32[2,32,96]{2,1,0:T(8,128)S(1)}, f32[2,32,96]{2,1,0:T(8,128)}, u32[]{:S(2)}) copy-start(f32[2,32,96]{2,1,0:T(8,128)} %constant.35.clone.select_ref) | copy-start | bytes 73732
  84.3 46.0 %collective-permute-start.4 = (f32[96,1536]{1,0:T(8,128)}, f32[96,1536]{1,0:T(8,128)S(1)}, u32[]{:S(2)}, u32[]{:S(2)}) collective-permute-start(f32[96,1536]{1,0:T(8,128)} %get-tuple-element.32), channel_id=1, source_target_pairs={{0,16},{16,32},{32,48},{48,64},{64,80},{80,96},{96,112},{112,128},... | collective-permute-start | bytes 1769480 | tf_op jit(solution)/shard_map/ppermute | solution.py:276
  88.7 41.7 %collective-permute-start.5 = (f32[96,1536]{1,0:T(8,128)}, f32[96,1536]{1,0:T(8,128)S(1)}, u32[]{:S(2)}, u32[]{:S(2)}) collective-permute-start(f32[96,1536]{1,0:T(8,128)} %get-tuple-element.33), channel_id=1, source_target_pairs={{0,240},{16,0},{32,16},{48,32},{64,48},{80,64},{96,80},{112,96},{1... | collective-permute-start | bytes 1769480 | tf_op jit(solution)/shard_map/ppermute | solution.py:276
  89.6 6.1 %collective-permute-start.9 = (f32[48,128]{1,0:T(8,128)S(1)}, f32[48,128]{1,0:T(8,128)S(1)}, u32[]{:S(2)}, u32[]{:S(2)}) collective-permute-start(f32[48,128]{1,0:T(8,128)S(1)} %reduce_sum.9), channel_id=1, source_target_pairs={{1,2},{3,4},{5,6},{7,8},{9,10},{11,12},{13,14},{15,0},{17,18},{19,... | collective-permute-start | bytes 73736 | tf_op jit(solution)/shard_map/ppermute | solution.py:284
  95.8 72.5 %copy-start.23 = (f32[128,160]{1,0:T(8,128)S(1)}, f32[128,160]{1,0:T(8,128)}, u32[]{:S(2)}) copy-start(f32[128,160]{1,0:T(8,128)} %constant.36.clone.select_ref) | copy-start | bytes 245764
  95.8 6.8 %collective-permute-start.10 = (f32[48,128]{1,0:T(8,128)S(1)}, f32[48,128]{1,0:T(8,128)S(1)}, u32[]{:S(2)}, u32[]{:S(2)}) collective-permute-start(f32[48,128]{1,0:T(8,128)S(1)} %add.40), channel_id=1, source_target_pairs={{2,4},{6,8},{10,12},{14,0},{18,20},{22,24},{26,28},{30,16},{34,36}... | collective-permute-start | bytes 73736 | tf_op jit(solution)/shard_map/ppermute | solution.py:284
  102.6 8.5 %collective-permute-start.11 = (f32[48,128]{1,0:T(8,128)S(1)}, f32[48,128]{1,0:T(8,128)S(1)}, u32[]{:S(2)}, u32[]{:S(2)}) collective-permute-start(f32[48,128]{1,0:T(8,128)S(1)} %add.41), channel_id=1, source_target_pairs={{4,8},{12,0},{20,24},{28,16},{36,40},{44,32},{52,56},{60,48},{68,7... | collective-permute-start | bytes 73736 | tf_op jit(solution)/shard_map/ppermute | solution.py:284
  111.1 13.3 %collective-permute-start.12 = (f32[48,128]{1,0:T(8,128)S(1)}, f32[48,128]{1,0:T(8,128)S(1)}, u32[]{:S(2)}, u32[]{:S(2)}) collective-permute-start(f32[48,128]{1,0:T(8,128)S(1)} %add.42), channel_id=1, source_target_pairs={{8,0},{24,16},{40,32},{56,48},{72,64},{88,80},{104,96},{120,112},{... | collective-permute-start | bytes 73736 | tf_op jit(solution)/shard_map/ppermute | solution.py:284
  124.4 2.5 %collective-permute-start.13 = (bf16[48,128]{1,0:T(8,128)(2,1)S(1)}, bf16[48,128]{1,0:T(8,128)(2,1)S(1)}, u32[]{:S(2)}, u32[]{:S(2)}) collective-permute-start(bf16[48,128]{1,0:T(8,128)(2,1)S(1)} %fusion), channel_id=1, source_target_pairs={{0,8},{16,24},{32,40},{48,56},{64,72},{80,88},{96,104},{112,120},{... | collective-permute-start | bytes 36872 | tf_op jit(solution)/shard_map/ppermute | solution.py:295
  126.9 2.1 %collective-permute-start.14 = (bf16[48,128]{1,0:T(8,128)(2,1)S(1)}, bf16[48,128]{1,0:T(8,128)(2,1)S(1)}, u32[]{:S(2)}, u32[]{:S(2)}) collective-permute-start(bf16[48,128]{1,0:T(8,128)(2,1)S(1)} %add.44), channel_id=1, source_target_pairs={{0,4},{8,12},{16,20},{24,28},{32,36},{40,44},{48,52},{56,60},{64,6... | collective-permute-start | bytes 36872 | tf_op jit(solution)/shard_map/ppermute | solution.py:295
  129.0 11.0 %collective-permute-start.15 = (bf16[48,128]{1,0:T(8,128)(2,1)S(1)}, bf16[48,128]{1,0:T(8,128)(2,1)S(1)}, u32[]{:S(2)}, u32[]{:S(2)}) collective-permute-start(bf16[48,128]{1,0:T(8,128)(2,1)S(1)} %add.45), channel_id=1, source_target_pairs={{0,2},{4,6},{8,10},{12,14},{16,18},{20,22},{24,26},{28,30},{32,34}... | collective-permute-start | bytes 36872 | tf_op jit(solution)/shard_map/ppermute | solution.py:295
  130.4 1.0 copy-start.16
  133.5 34.7 %collective-permute-start.6 = (f32[64,1536]{1,0:T(8,128)S(1)}, f32[64,1536]{1,0:T(8,128)S(1)}, u32[]{:S(2)}, u32[]{:S(2)}) collective-permute-start(f32[64,1536]{1,0:T(8,128)S(1)} %get-tuple-element.34), channel_id=1, source_target_pairs={{0,1},{1,2},{2,3},{3,4},{4,5},{5,6},{6,7},{7,8},{8,9},{9,10},{10,1... | collective-permute-start | bytes 1179656 | tf_op jit(solution)/shard_map/ppermute | solution.py:276
  135.5 32.7 %collective-permute-start.7 = (f32[64,1536]{1,0:T(8,128)S(1)}, f32[64,1536]{1,0:T(8,128)S(1)}, u32[]{:S(2)}, u32[]{:S(2)}) collective-permute-start(f32[64,1536]{1,0:T(8,128)S(1)} %get-tuple-element.35), channel_id=1, source_target_pairs={{0,15},{1,0},{2,1},{3,2},{4,3},{5,4},{6,5},{7,6},{8,7},{9,8},{10,9... | collective-permute-start | bytes 1179656 | tf_op jit(solution)/shard_map/ppermute | solution.py:276
  140.1 2.1 %collective-permute-start.16 = (bf16[48,128]{1,0:T(8,128)(2,1)S(1)}, bf16[48,128]{1,0:T(8,128)(2,1)S(1)}, u32[]{:S(2)}, u32[]{:S(2)}) collective-permute-start(bf16[48,128]{1,0:T(8,128)(2,1)S(1)} %add.46), channel_id=1, source_target_pairs={{0,1},{2,3},{4,5},{6,7},{8,9},{10,11},{12,13},{14,15},{16,17},{18,... | collective-permute-start | bytes 36872 | tf_op jit(solution)/shard_map/ppermute | solution.py:295
  (15 other events, 12.9 us)

commit v2 on v1

v2 whole, which is shorter than its diff:
```python
import math

import jax
import jax.numpy as jnp
import numpy as np
from jax import lax
from jax.experimental import pallas as pl
from jax.experimental.pallas import tpu as pltpu
from jax.sharding import Mesh
from jax.sharding import PartitionSpec as P


HEADS = 12
HDIM = 128
TILE = 8
HALO = 2
HA = ("ha_0", "ha_1")
F32 = jnp.float32
BF16 = jnp.bfloat16
SCALE = 1.0 / math.sqrt(HDIM)

FRAMES = 2
OWN = FRAMES * TILE * TILE
SIDE = FRAMES * TILE * HALO
CORNER = HALO * HALO
BAND = HALO * TILE + 2 * CORNER
ENDS = FRAMES * BAND


def nt(a, b):
    return lax.dot_general(a, b, (((1,), (1,)), ((), ())), preferred_element_type=F32)


def nn(a, b):
    return lax.dot_general(a, b, (((1,), (0,)), ((), ())), preferred_element_type=F32)


def tn(a, b):
    return lax.dot_general(a, b, (((0,), (0,)), ((), ())), preferred_element_type=F32)


def exact(a, b):
    return lax.dot_general(
        a, b, (((1,), (0,)), ((), ())), precision=lax.Precision.HIGHEST, preferred_element_type=F32
    )


def own_row(frame, row, col):
    return frame * TILE * TILE + row * TILE + col


def side_row(frame, row, col):
    return (frame * TILE + row) * HALO + col


def select_sides():
    out = np.zeros((2, SIDE, OWN), np.float32)
    for side, first in enumerate((0, TILE - HALO)):
        for frame in range(FRAMES):
            for row in range(TILE):
                for col in range(HALO):
                    out[side, side_row(frame, row, col), own_row(frame, row, first + col)] = 1
    return out


def select_ends():
    out = np.zeros((2, ENDS, OWN + 2 * SIDE), np.float32)
    for end, first in enumerate((0, TILE - HALO)):
        for frame in range(FRAMES):
            at = frame * BAND
            for row in range(HALO):
                for col in range(TILE):
                    out[end, at, own_row(frame, first + row, col)] = 1
                    at += 1
            for side in range(2):
                for row in range(HALO):
                    for col in range(HALO):
                        out[end, at, OWN + side * SIDE + side_row(frame, first + row, col)] = 1
                        at += 1
    return out


SIDES = select_sides()
BANDS = select_ends()


GROUP = 4


def sides_kernel(ready, done, select_ref, keys_ref, values_ref, left_ref, right_ref):
    for h in range(0, HEADS, GROUP):
        ready(h)
        cols = slice(h * HDIM, (h + GROUP) * HDIM)
        for part, ref in enumerate((keys_ref, values_ref)):
            rows = ref[:, cols]
            at = slice(part * SIDE, (part + 1) * SIDE)
            left_ref[at, cols] = nn(select_ref[0], rows).astype(BF16)
            right_ref[at, cols] = nn(select_ref[1], rows).astype(BF16)
        done(h)


def ends_kernel(
    ready, done, select_ref, keys_ref, values_ref, left_ref, right_ref, top_ref, bottom_ref
):
    for h in range(0, HEADS, GROUP):
        ready(h)
        cols = slice(h * HDIM, (h + GROUP) * HDIM)
        for part, ref in enumerate((keys_ref, values_ref)):
            at = slice(part * SIDE, (part + 1) * SIDE)
            rows = jnp.concatenate([ref[:, cols], left_ref[at, cols], right_ref[at, cols]], axis=0)
            to = slice(part * ENDS, (part + 1) * ENDS)
            top_ref[to, cols] = nn(select_ref[0], rows).astype(BF16)
            bottom_ref[to, cols] = nn(select_ref[1], rows).astype(BF16)
        done(h)


def text_kernel(
    ready, done, norm_ref, delta_ref, query_ref, out_grad_ref, key_ref, value_ref, grad_ref, stats_ref
):
    heads = lax.broadcasted_iota(jnp.int32, (16, HEADS), 1)
    identity = (heads == lax.broadcasted_iota(jnp.int32, (16, HEADS), 0)).astype(F32)
    stats = []
    for which, ref in enumerate((norm_ref, delta_ref)):
        rows = lax.dot_general(
            identity,
            ref[...],
            (((1,), (1,)), ((), ())),
            precision=lax.Precision.HIGHEST,
            preferred_element_type=F32,
        )
        stats_ref[which * 16 : (which + 1) * 16, :] = rows
        stats.append(rows)
    norm, delta = stats
    text = key_ref.shape[0]
    piece = grad_ref.shape[0] // 16
    for h in range(HEADS):
        ready(h)
        cols = slice(h * HDIM, (h + 1) * HDIM)
        q = query_ref[:, cols]
        g = out_grad_ref[:, cols]
        probs = jnp.exp(nt(key_ref[:, cols], q) * SCALE - norm[h : h + 1])
        prob_grad = nt(value_ref[:, cols], g)
        score_grad = (probs * (prob_grad - delta[h : h + 1])).astype(BF16)
        for part, grad in enumerate((nn(score_grad, q) * SCALE, nn(probs.astype(BF16), g))):
            for at in range(0, text, 16):
                chip, within = divmod(h * text + at, piece)
                to = (2 * chip + part) * piece + within
                grad_ref[to : to + 16, :] = grad[at : at + 16]


def backward(q, g, k, v, norm, delta, live):
    probs = jnp.exp(nt(k, q) * SCALE - norm)
    if live is not None:
        probs = probs * live
    score_grad = (probs * (nt(v, g) - delta)).astype(BF16)
    return probs.astype(BF16), score_grad


def own_kernel(
    ready,
    done,
    live_ref,
    stats_ref,
    query_ref,
    out_grad_ref,
    keys_ref,
    values_ref,
    text_key_ref,
    text_value_ref,
    query_grad_ref,
    own_ref,
):
    text = text_key_ref.shape[0]
    rows = lax.broadcasted_iota(jnp.int32, (OWN + text, HDIM), 0)
    live = jnp.where(rows < OWN, live_ref[4].astype(F32), 1.0)
    for h in range(HEADS):
        ready(h)
        cols = slice(h * HDIM, (h + 1) * HDIM)
        q = query_ref[:, cols]
        g = out_grad_ref[:, cols]
        k = jnp.concatenate([keys_ref[:, cols], text_key_ref[:, cols]], axis=0)
        v = jnp.concatenate([values_ref[:, cols], text_value_ref[:, cols]], axis=0)
        norm = stats_ref[h : h + 1, :]
        delta = stats_ref[16 + h : 17 + h, :]
        probs, score_grad = backward(q, g, k, v, norm, delta, live)
        query_grad_ref[:, cols] = tn(score_grad, k)
        own_ref[:OWN, cols] = nn(score_grad[:OWN], q) * SCALE
        own_ref[OWN:, cols] = nn(probs[:OWN], g)
        done(h)


def halo_kernel(
    ready,
    done,
    live_ref,
    stats_ref,
    query_ref,
    out_grad_ref,
    left_ref,
    right_ref,
    top_ref,
    bottom_ref,
    part_ref,
    top_grad_ref,
    bottom_grad_ref,
    left_grad_ref,
    right_grad_ref,
    query_grad_ref,
    mask_ref,
):
    def live(block):
        return live_ref[block].astype(F32)

    band = lax.rem(lax.broadcasted_iota(jnp.int32, (ENDS, HDIM), 0), BAND)
    for end, first in ((0, 0), (1, 6)):
        mask_ref[end * ENDS : (end + 1) * ENDS, :] = jnp.where(
            band < HALO * TILE,
            live(first + 1),
            jnp.where(band < HALO * TILE + CORNER, live(first), live(first + 2)),
        )
    at = 2 * ENDS
    mask_ref[at : at + SIDE, :] = jnp.full((SIDE, HDIM), live(3), F32)
    mask_ref[at + SIDE : at + 2 * SIDE, :] = jnp.full((SIDE, HDIM), live(5), F32)
    for h in range(HEADS):
        ready(h)
        cols = slice(h * HDIM, (h + 1) * HDIM)
        q = query_ref[:, cols]
        g = out_grad_ref[:, cols]
        k, v = (
            jnp.concatenate(
                [
                    top_ref[part * ENDS : (part + 1) * ENDS, cols],
                    bottom_ref[part * ENDS : (part + 1) * ENDS, cols],
                    left_ref[part * SIDE : (part + 1) * SIDE, cols],
                    right_ref[part * SIDE : (part + 1) * SIDE, cols],
                ],
                axis=0,
            )
            for part in range(2)
        )
        norm = stats_ref[h : h + 1, :]
        delta = stats_ref[16 + h : 17 + h, :]
        probs, score_grad = backward(q, g, k, v, norm, delta, mask_ref[...])
        query_grad = (part_ref[:, cols] + tn(score_grad, k)) * SCALE
        query_grad_ref[:, cols] = query_grad.astype(BF16)
        for part, grad in enumerate((nn(score_grad, q) * SCALE, nn(probs, g))):
            at = 0
            for ref, rows in (
                (top_grad_ref, ENDS),
                (bottom_grad_ref, ENDS),
                (left_grad_ref, SIDE),
                (right_grad_ref, SIDE),
            ):
                ref[part * rows : (part + 1) * rows, cols] = grad[at : at + rows]
                at += rows
        done(h)


def corners_kernel(
    ready, done, select_ref, left_ref, right_ref, above_ref, below_ref, left_out_ref, right_out_ref
):
    for h in range(0, HEADS, GROUP):
        ready(h)
        cols = slice(h * HDIM, (h + GROUP) * HDIM)
        for part in range(2):
            side = slice(part * SIDE, (part + 1) * SIDE)
            ends = slice(part * ENDS, (part + 1) * ENDS)
            bands = jnp.concatenate([above_ref[ends, cols], below_ref[ends, cols]], axis=0)
            more = exact(select_ref[...], bands)
            left_out_ref[side, cols] = left_ref[side, cols] + more[:SIDE]
            right_out_ref[side, cols] = right_ref[side, cols] + more[SIDE:]
        done(h)


def bands_kernel(ready, done, own_ref, above_ref, below_ref, out_ref):
    for h in range(0, HEADS, GROUP):
        ready(h)
        cols = slice(h * HDIM, (h + GROUP) * HDIM)
        out_ref[:, cols] = own_ref[:, cols]
        for part in range(2):
            for frame in range(FRAMES):
                to = part * OWN + frame * TILE * TILE
                at = part * ENDS + frame * BAND
                rows = HALO * TILE
                out_ref[to : to + rows, cols] += above_ref[at : at + rows, cols]
                end = to + (TILE - HALO) * TILE
                out_ref[end : end + rows, cols] += below_ref[at : at + rows, cols]
        done(h)


def sum_kernel(ready, done, select_ref, own_ref, left_ref, right_ref, key_ref, value_ref):
    for h in range(0, HEADS, GROUP):
        ready(h)
        cols = slice(h * HDIM, (h + GROUP) * HDIM)
        for part, out in enumerate((key_ref, value_ref)):
            side = slice(part * SIDE, (part + 1) * SIDE)
            rows = jnp.concatenate([left_ref[side, cols], right_ref[side, cols]], axis=0)
            total = own_ref[part * OWN : (part + 1) * OWN, cols] + exact(select_ref[...], rows)
            out[:, cols] = total.astype(BF16)
        done(h)


def words_kernel(ready, done, parts_ref, key_ref, value_ref):
    text = key_ref.shape[0]
    rows = parts_ref.shape[1]
    for part, out in enumerate((key_ref, value_ref)):
        for h in range(HEADS):
            for at in range(0, text, 16):
                chip, within = divmod(h * text + at, rows)
                piece = parts_ref[2 * chip + part, within : within + 16, :]
                out[at : at + 16, h * HDIM : (h + 1) * HDIM] = piece


def call(kernel, outs, ins, scratch=(), us=1.0, room=0.0):
    spaces = {"s": pltpu.SMEM, "v": pltpu.VMEM, "h": pltpu.HBM}
    n_in, n_out = len(ins), len(outs)
    shapes = [(a.shape, a.dtype) for a, _ in ins] + [(shape, dtype) for shape, dtype, _ in outs]
    places = [place for _, place in ins] + [place for _, _, place in outs]
    held = [i for i, place in enumerate(places) if place == "h"]
    groups = HEADS // GROUP

    def pieces(i):
        shape, _ = shapes[i]
        if len(shape) == 2 and shape[1] == HEADS * HDIM:
            step = GROUP * HDIM
            return [(slice(None), slice(n * step, (n + 1) * step)) for n in range(groups)]
        return [(Ellipsis,)]

    def body(*refs):
        here = list(refs[: n_in + n_out])
        buffers = refs[n_in + n_out : n_in + n_out + len(held)]
        semaphores = refs[n_in + n_out + len(held)]
        rest = refs[n_in + n_out + len(held) + 1 :]
        arriving, leaving, started = [], [], []
        for n, i in enumerate(held):
            far, near = here[i], buffers[n]
            for m, at in enumerate(pieces(i)):
                source, target = (far, near) if i < n_in else (near, far)
                copy = pltpu.make_async_copy(source.at[at], target.at[at], semaphores.at[n, m])
                (arriving if i < n_in else leaving).append((m, len(pieces(i)), copy))
            here[i] = near
        for group in range(groups):
            for m, _, copy in arriving:
                if m == group:
                    copy.start()
        for _, count, copy in arriving:
            if count == 1:
                copy.wait()

        def ready(h):
            if h % GROUP == 0:
                for m, count, copy in arriving:
                    if count > 1 and m == h // GROUP:
                        copy.wait()

        def done(h):
            if h % GROUP == GROUP - 1 or h % GROUP == 0 and kernel in whole_groups:
                for m, count, copy in leaving:
                    if count > 1 and m == h // GROUP:
                        copy.start()
                        started.append(copy)

        kernel(ready, done, *here, *rest)
        for _, _, copy in leaving:
            if all(copy is not other for other in started):
                copy.start()
        for _, _, copy in leaving:
            copy.wait()

    return pl.pallas_call(
        body,
        out_shape=[jax.ShapeDtypeStruct(shape, dtype) for shape, dtype, _ in outs],
        in_specs=[pl.BlockSpec(memory_space=spaces[place]) for _, place in ins],
        out_specs=[pl.BlockSpec(memory_space=spaces[place]) for _, _, place in outs],
        scratch_shapes=[
            *(pltpu.VMEM(*shapes[i]) for i in held),
            pltpu.SemaphoreType.DMA((max(len(held), 1), groups)),
            *scratch,
        ],
        compiler_params=pltpu.CompilerParams(vmem_limit_bytes=int((60.5 - room) * 2**20)),
        cost_estimate=pl.CostEstimate(
            flops=int(us * FLOPS_PER_US), bytes_accessed=1000000, transcendentals=0
        ),
    )(*(a for a, _ in ins))


FLOPS_PER_US = 50000000
whole_groups = (sides_kernel, ends_kernel, corners_kernel, bands_kernel, sum_kernel)


def shifted(value, axis, steps):
    count = lax.axis_size(axis)
    return lax.ppermute(value, axis, [(i, (i + steps) % count) for i in range(count)])


def by_query(rows):
    return rows.transpose(1, 2, 3, 0).reshape(OWN, HEADS)


def to_all(value, axis):
    count = lax.axis_size(axis)
    everyone = jnp.broadcast_to(value[None], (count, *value.shape))
    return lax.all_to_all(everyone, axis, 0, 0, tiled=True)


def local(
    queries, keys, values, out_grad, log_norm, delta_rows, text_keys, text_values, window_table
):
    shape = queries.shape
    width = shape[-1]
    text = text_keys.shape[0]
    q = queries.reshape(OWN, width)
    g = out_grad.reshape(OWN, width)
    k = keys.reshape(OWN, width)
    v = values.reshape(OWN, width)
    anchor = jnp.zeros((), jnp.int32)
    live = lax.dynamic_slice(
        window_table, (lax.axis_index(HA), lax.axis_index("wa"), anchor), (1, 1, 9)
    ).reshape(9)

    words, stats = call(
        text_kernel,
        [((2 * HEADS * text, HDIM), F32, "h"), ((32, HDIM), F32, "h")],
        [
            (by_query(log_norm), "h"),
            (by_query(delta_rows), "h"),
            (q, "h"),
            (g, "h"),
            (text_keys, "h"),
            (text_values, "h"),
        ],
        us=3,
    )
    count = lax.axis_size(HA)
    words = lax.all_to_all(words.reshape(count, -1, HDIM), HA, 0, 0, tiled=True)
    piece = words.sum(axis=0)
    pieces = to_all(piece, "wa")
    piece = pieces.sum(axis=0).astype(BF16)
    pieces = to_all(piece, HA)
    text_key_grad, text_value_grad = call(
        words_kernel, [((text, width), BF16, "h")] * 2, [(pieces, "h")]
    )

    left, right = call(
        sides_kernel,
        [((2 * SIDE, width), BF16, "h")] * 2,
        [(jnp.asarray(SIDES, BF16), "h"), (k, "h"), (v, "h")],
    )
    from_right = shifted(left, "wa", -1)
    from_left = shifted(right, "wa", 1)
    part, own = call(
        own_kernel,
        [((OWN, width), F32, "h"), ((2 * OWN, width), F32, "h")],
        [
            (live, "s"),
            (stats, "h"),
            (q, "h"),
            (g, "h"),
            (k, "h"),
            (v, "h"),
            (text_keys, "h"),
            (text_values, "h"),
        ],
        us=3,
    )
    top, bottom = call(
        ends_kernel,
        [((2 * ENDS, width), BF16, "h")] * 2,
        [(jnp.asarray(BANDS, BF16), "h"), (k, "h"), (v, "h"), (from_left, "v"), (from_right, "v")],
        room=2.0,
    )
    from_below = shifted(top, HA, -1)
    from_above = shifted(bottom, HA, 1)
    top_grad, bottom_grad, left_grad, right_grad, query_grad = call(
        halo_kernel,
        [((2 * ENDS, width), F32, "v")] * 2
        + [((2 * SIDE, width), F32, "v")] * 2
        + [((OWN, width), BF16, "h")],
        [
            (live, "s"),
            (stats, "h"),
            (q, "h"),
            (g, "h"),
            (from_left, "h"),
            (from_right, "h"),
            (from_above, "h"),
            (from_below, "h"),
            (part, "h"),
        ],
        scratch=[pltpu.VMEM((2 * ENDS + 2 * SIDE, HDIM), F32)],
        us=3,
        room=6.0,
    )
    above = shifted(bottom_grad, HA, 1)
    below = shifted(top_grad, HA, -1)
    back = np.concatenate([BANDS[0].T, BANDS[1].T], axis=1)
    left_grad, right_grad = call(
        corners_kernel,
        [((2 * SIDE, width), F32, "h")] * 2,
        [
            (jnp.asarray(back[OWN:], F32), "h"),
            (left_grad, "v"),
            (right_grad, "v"),
            (above, "v"),
            (below, "v"),
        ],
        room=6.0,
    )
    after = shifted(left_grad, "wa", -1)
    before = shifted(right_grad, "wa", 1)
    (own,) = call(
        bands_kernel,
        [((2 * OWN, width), F32, "h")],
        [(own, "h"), (above, "v"), (below, "v")],
        room=6.0,
    )
    back = np.concatenate([SIDES[0].T, SIDES[1].T], axis=1)
    key_grad, value_grad = call(
        sum_kernel,
        [((OWN, width), BF16, "h")] * 2,
        [(jnp.asarray(back, F32), "h"), (own, "h"), (before, "h"), (after, "h")],
    )
    return (
        query_grad.reshape(shape),
        key_grad.reshape(shape),
        value_grad.reshape(shape),
        text_key_grad,
        text_value_grad,
    )


def solution(mesh):
    split = Mesh(
        mesh.devices.reshape(mesh.shape["group"], 8, 2, mesh.shape["wa"]),
        ("group", "ha_0", "ha_1", "wa"),
    )
    return jax.shard_map(
        local,
        mesh=split,
        in_specs=(
            P("group", HA, "wa", None),
            P("group", HA, "wa", None),
            P("group", HA, "wa", None),
            P("group", HA, "wa", None),
            P(None, "group", HA, "wa"),
            P(None, "group", HA, "wa"),
            P("group", None),
            P("group", None),
            P(),
        ),
        out_specs=(
            P("group", HA, "wa", None),
            P("group", HA, "wa", None),
            P("group", HA, "wa", None),
            P("group", None),
            P("group", None),
        ),
        check_vma=False,
    )
```

time: 172 us -> 162 us (0.942)
  starting transfers between devices: 78.8 us -> 30.5 us
  blocking collectives: 25.2 us -> 59.5 us
  Pallas kernels: 13.6 us -> 37.1 us
  local copies, waits for them, and re-layouts: 18.3 us -> 7.44 us
  waiting for transfers between devices: 31.8 us -> 25.3 us
    ppermute x9 -> x8, starting transfers between devices: 62 us -> 16.6 us  [shifted(): lax.ppermute(value, axis, [(i, (i + steps) % count) for i in range(count)])]
    all_to_all x1, blocking collectives: 25.2 us -> 59.5 us  [local(): words = lax.all_to_all(words.reshape(count, -1, HDIM), HA, 0, 0, tiled=True)]
    ppermute x8 -> x0, waiting for transfers between devices: 31.8 us -> none  [the longest x4 29.4 us: to_first(): value = value + lax.ppermute(value, axis, pairs)]
    ppermute x9 -> x8, waiting for transfers between devices: 0.02 us -> 24.1 us  [shifted(): lax.ppermute(value, axis, [(i, (i + steps) % count) for i in range(count)])]
    pallas_call x7 -> x9, Pallas kernels: 13.6 us -> 37.1 us  [call(): pl.pallas_call(body, out_shape=[jax.ShapeDtypeStruct(shape, dtype) for sh...]
    unnamed x60 -> x20, local copies, waits for them, and re-layouts: 18 us -> 5.09 us
    ppermute x8 -> x0, starting transfers between devices: 10.9 us -> none  [the longest x4 5.55 us: from_first(): value = value + lax.ppermute(value, axis, pairs)]
    all_to_all x1 -> x2, starting transfers between devices: 5.89 us -> 13.9 us  [to_all(): return lax.all_to_all(everyone, axis, 0, 0, tiled=True)]
  transfers between devices with their start and end apart: 18 -> 10, of which waited for: 7 -> 4; matrix products, arithmetic and copies ran while one was open for 2% -> 1% of each run, Pallas kernels for 6% -> 19%
where the time goes in v2:
time: 162 us; the launch traced here: 161 us
  blocking collectives  59.5 us (37%)
  Pallas kernels  37.1 us (23%)
  starting transfers between devices  30.5 us (19%)
  waiting for transfers between devices  25.3 us (16%)
  local copies, waits for them, and re-layouts  7.44 us (5%)
    all_to_all x1, blocking collectives, local(): words = lax.all_to_all(words.reshape(count, -1, HDIM), HA, 0, 0, tiled=True)  59.5 us
    pallas_call x9, Pallas kernels, call(): pl.pallas_call(body, out_shape=[jax.ShapeDtypeStruct(shape, dtype) for sh...  37.1 us
    ppermute x8, waiting for transfers between devices, shifted(): lax.ppermute(value, axis, [(i, (i + steps) % count) for i in range(count)])  24.1 us
    ppermute x8, starting transfers between devices, shifted(): lax.ppermute(value, axis, [(i, (i + steps) % count) for i in range(count)])  16.6 us
    all_to_all x2, starting transfers between devices, to_all(): return lax.all_to_all(everyone, axis, 0, 0, tiled=True)  13.9 us
    unnamed x20, local copies, waits for them, and re-layouts  5.09 us
  transfers between devices with their start and end apart: 10, of which 4 were waited for; matrix products, arithmetic and copies ran while one was open for 1% of the time, Pallas kernels for 19%

profile of v2, /device:TPU:65, one launch (start us, length us, event | category | flops | bytes accessed | tf_op | source)
XLA Modules:
  0.0 160.8 jit_solution(9033964461462720259)
XLA Ops:
  0.6 4.5 %shard_map.164 = (f32[768,128]{1,0:T(8,128)}, f32[32,128]{1,0:T(8,128)}) custom-call(f32[128,12]{1,0:T(8,128)} %bitcast.27, f32[128,12]{1,0:T(8,128)} %bitcast.28, bf16[128,1536]{1,0:T(8,128)(2,1)} %bitcast.20, bf16[128,1536]{1,0:T(8,128)(2,1)} %bitcast.23, bf16[32,1536]{1,0:T(8,128)(2,1)} %refs_6_.1, bf16[32,1536]{1,0:T(8,128)(2,1)} %refs_7_.1), custom_call_target="tpu_custom_call" | custom-call | flops 150000000 | bytes 1000000 | tf_op jit(solution)/shard_map/pallas_call | solution.py:370
  5.1 59.5 %all_to_all.15 = f32[16,48,128]{2,1,0:T(8,128)S(1)} all-to-all(f32[16,48,128]{2,1,0:T(8,128)} %bitcast.26), channel_id=1, replica_groups=mesh['group'=2,'ha_0'=8,'ha_1'=2,'wa'=16] {'ha_0','ha_1'}, dimensions={0} | all-to-all | bytes 786432 | tf_op jit(solution)/shard_map/all_to_all | solution.py:435
  64.6 0.8 broadcast_in_dim.4
  65.4 7.2 %all-to-all-start.1 = ((f32[16,48,128]{2,1,0:T(8,128)}), f32[16,48,128]{2,1,0:T(8,128)S(1)}, u32[]{:S(2)}, u32[]{:S(2)}) async-start(f32[16,48,128]{2,1,0:T(8,128)} %broadcast_in_dim.4), calls=%async_computation.1 | async-start | bytes 786432 | tf_op jit(solution)/shard_map/all_to_all | solution.py:403
  72.6 2.4 %shard_map.165 = (bf16[64,1536]{1,0:T(8,128)(2,1)}, bf16[64,1536]{1,0:T(8,128)(2,1)}) custom-call(bf16[2,32,128]{2,1,0:T(8,128)(2,1)} %constant.31.clone.refs_0_, bf16[128,1536]{1,0:T(8,128)(2,1)} %bitcast.14, bf16[128,1536]{1,0:T(8,128)(2,1)} %bitcast.17), custom_call_target="tpu_custom_call" | custom-call | flops 50000000 | bytes 1000000 | tf_op jit(solution)/shard_map/pallas_call | solution.py:370
  75.0 3.1 %collective-permute-start = (bf16[64,1536]{1,0:T(8,128)(2,1)}, bf16[64,1536]{1,0:T(8,128)(2,1)S(1)}, u32[]{:S(2)}, u32[]{:S(2)}) collective-permute-start(bf16[64,1536]{1,0:T(8,128)(2,1)} %get-tuple-element.25), channel_id=1, source_target_pairs={{0,1},{1,2},{2,3},{3,4},{4,5},{5,6},{6,7},{7,8},{8,9},{9,10},{10,1... | collective-permute-start | bytes 589832 | tf_op jit(solution)/shard_map/ppermute | solution.py:393
  78.1 3.5 %collective-permute-start.1 = (bf16[64,1536]{1,0:T(8,128)(2,1)}, bf16[64,1536]{1,0:T(8,128)(2,1)S(1)}, u32[]{:S(2)}, u32[]{:S(2)}) collective-permute-start(bf16[64,1536]{1,0:T(8,128)(2,1)} %get-tuple-element.26), channel_id=1, source_target_pairs={{0,15},{1,0},{2,1},{3,2},{4,3},{5,4},{6,5},{7,6},{8,7},{9,8},{10,9... | collective-permute-start | bytes 589832 | tf_op jit(solution)/shard_map/ppermute | solution.py:393
  81.6 15.9 %collective-permute-done.refs_3_.refs_4_ = bf16[64,1536]{1,0:T(8,128)(2,1)S(1)} collective-permute-done((bf16[64,1536]{1,0:T(8,128)(2,1)}, bf16[64,1536]{1,0:T(8,128)(2,1)S(1)}, u32[]{:S(2)}, u32[]{:S(2)}) %collective-permute-start) | collective-permute-done | bytes 196640 | tf_op jit(solution)/shard_map/ppermute | solution.py:393
  97.5 0.7 copy-done.3
  98.1 0.7 copy-done.4
  98.8 3.6 %shard_map.166 = (bf16[96,1536]{1,0:T(8,128)(2,1)}, bf16[96,1536]{1,0:T(8,128)(2,1)}) custom-call(bf16[2,48,192]{2,1,0:T(8,128)(2,1)} %constant.32.clone.refs_0_, bf16[128,1536]{1,0:T(8,128)(2,1)} %bitcast.15, bf16[128,1536]{1,0:T(8,128)(2,1)} %bitcast.18, bf16[64,1536]{1,0:T(8,128)(2,1)} %copy-done.3, bf16[64,1536]{1,0:T(8,128)(2,1)} %copy-done.4), custom_call_target="tpu_custom_call" | custom-call | flops 50000000 | bytes 1000000 | tf_op jit(solution)/shard_map/pallas_call | solution.py:370
  102.9 0.9 dynamic-slice_reduce_fusion.refs_0_
  103.8 6.4 %shard_map.167 = (f32[128,1536]{1,0:T(8,128)}, f32[256,1536]{1,0:T(8,128)}) custom-call(s32[9]{0:T(128)} %dynamic-slice_reduce_fusion.refs_0_, f32[32,128]{1,0:T(8,128)} %get-tuple-element.24.refs_1_, bf16[128,1536]{1,0:T(8,128)(2,1)} %bitcast.21, bf16[128,1536]{1,0:T(8,128)(2,1)} %bitcast.24, bf16[128,1536]{1,0:T(8,128)(2,1)} %bitcast.16, ...), custom_call_target="tpu_custom_call" | custom-call | flops 150000000 | bytes 1000000 | tf_op jit(solution)/shard_map/pallas_call | solution.py:370
  110.3 0.7 copy-done.8
  111.1 7.6 %shard_map.168 = (f32[96,1536]{1,0:T(8,128)}, f32[96,1536]{1,0:T(8,128)}, f32[64,1536]{1,0:T(8,128)}, f32[64,1536]{1,0:T(8,128)}, bf16[128,1536]{1,0:T(8,128)(2,1)}) custom-call(s32[9]{0:T(128)} %dynamic-slice_reduce_fusion.refs_0_, f32[32,128]{1,0:T(8,128)} %get-tuple-element.24.refs_1_, bf16[128,1536]{1,0:T(8,128)(2,1)} %bitcast.22, ...), custom_call_target="tpu_custom_call" | custom-call | flops 150000000 | bytes 1000000 | tf_op jit(solution)/shard_map/pallas_call | solution.py:370
  118.7 1.4 collective-permute-start.4
  120.0 1.6 %collective-permute-start.5 = (f32[96,1536]{1,0:T(8,128)}, f32[96,1536]{1,0:T(8,128)S(1)}, u32[]{:S(2)}, u32[]{:S(2)}) collective-permute-start(f32[96,1536]{1,0:T(8,128)} %get-tuple-element.33), channel_id=1, source_target_pairs={{0,240},{16,0},{32,16},{48,32},{64,48},{80,64},{96,80},{112,96},{1... | collective-permute-start | bytes 1769480 | tf_op jit(solution)/shard_map/ppermute | solution.py:393
  121.6 5.5 %collective-permute-done.4.refs_1_.refs_3_ = f32[96,1536]{1,0:T(8,128)S(1)} collective-permute-done((f32[96,1536]{1,0:T(8,128)}, f32[96,1536]{1,0:T(8,128)S(1)}, u32[]{:S(2)}, u32[]{:S(2)}) %collective-permute-start.4) | collective-permute-done | bytes 589856 | tf_op jit(solution)/shard_map/ppermute | solution.py:393
  127.2 2.7 %collective-permute-done.5.refs_2_.refs_4_ = f32[96,1536]{1,0:T(8,128)S(1)} collective-permute-done((f32[96,1536]{1,0:T(8,128)}, f32[96,1536]{1,0:T(8,128)S(1)}, u32[]{:S(2)}, u32[]{:S(2)}) %collective-permute-start.5) | collective-permute-done | bytes 589856 | tf_op jit(solution)/shard_map/ppermute | solution.py:393
  129.8 0.8 copy-done.2
  130.6 3.8 %shard_map.170 = (f32[64,1536]{1,0:T(8,128)}, f32[64,1536]{1,0:T(8,128)}) custom-call(f32[64,96]{1,0:T(8,128)} %constant.33.clone.refs_0_, f32[64,1536]{1,0:T(8,128)} %get-tuple-element.34.refs_1_, f32[64,1536]{1,0:T(8,128)} %get-tuple-element.35.refs_2_, f32[96,1536]{1,0:T(8,128)} %copy-done.1, f32[96,1536]{1,0:T(8,128)} %copy-done.2), custom_call_target="tpu_custom_call" | custom-call | flops 50000000 | bytes 1000000 | tf_op jit(solution)/shard_map/pallas_call | solution.py:370
  134.4 2.0 %collective-permute-start.6 = (f32[64,1536]{1,0:T(8,128)}, f32[64,1536]{1,0:T(8,128)S(1)}, u32[]{:S(2)}, u32[]{:S(2)}) collective-permute-start(f32[64,1536]{1,0:T(8,128)} %get-tuple-element.36), channel_id=1, source_target_pairs={{0,1},{1,2},{2,3},{3,4},{4,5},{5,6},{6,7},{7,8},{8,9},{9,10},{10,1... | collective-permute-start | bytes 1179656 | tf_op jit(solution)/shard_map/ppermute | solution.py:393
  136.4 4.6 %collective-permute-start.7 = (f32[64,1536]{1,0:T(8,128)}, f32[64,1536]{1,0:T(8,128)S(1)}, u32[]{:S(2)}, u32[]{:S(2)}) collective-permute-start(f32[64,1536]{1,0:T(8,128)} %get-tuple-element.37), channel_id=1, source_target_pairs={{0,15},{1,0},{2,1},{3,2},{4,3},{5,4},{6,5},{7,6},{8,7},{9,8},{10,9... | collective-permute-start | bytes 1179656 | tf_op jit(solution)/shard_map/ppermute | solution.py:393
  141.0 0.7 broadcast_in_dim.5
  141.8 6.7 %all-to-all-start.2 = ((bf16[16,48,128]{2,1,0:T(8,128)(2,1)}), bf16[16,48,128]{2,1,0:T(8,128)(2,1)S(1)}, u32[]{:S(2)}, u32[]{:S(2)}) async-start(bf16[16,48,128]{2,1,0:T(8,128)(2,1)} %broadcast_in_dim.5), calls=%async_computation.2 | async-start | bytes 393216 | tf_op jit(solution)/shard_map/all_to_all | solution.py:403
  148.5 3.6 %shard_map.169.refs_1_ = f32[256,1536]{1,0:T(8,128)} custom-call(f32[256,1536]{1,0:T(8,128)} %get-tuple-element.31.refs_0_, f32[96,1536]{1,0:T(8,128)} %copy-done.1, f32[96,1536]{1,0:T(8,128)} %copy-done.2), custom_call_target="tpu_custom_call" | custom-call | flops 50000000 | bytes 1000000 | tf_op jit(solution)/shard_map/pallas_call | solution.py:370
  152.1 0.7 copy-done.6
  152.8 0.7 copy-done.7
  153.6 3.7 %shard_map.171 = (bf16[128,1536]{1,0:T(8,128)(2,1)}, bf16[128,1536]{1,0:T(8,128)(2,1)}) custom-call(f32[128,64]{1,0:T(8,128)} %constant.34.clone.refs_0_, f32[256,1536]{1,0:T(8,128)} %shard_map.169.refs_1_, f32[64,1536]{1,0:T(8,128)} %copy-done.6, f32[64,1536]{1,0:T(8,128)} %copy-done.7), custom_call_target="tpu_custom_call" | custom-call | flops 50000000 | bytes 1000000 | tf_op jit(solution)/shard_map/pallas_call | solution.py:370
  157.2 1.2 all-to-all-done.2.refs_0_
  158.4 0.7 copy-done.5
  159.1 1.7 %shard_map.172 = (bf16[32,1536]{1,0:T(8,128)(2,1)}, bf16[32,1536]{1,0:T(8,128)(2,1)}) custom-call(bf16[16,48,128]{2,1,0:T(8,128)(2,1)} %copy-done.5), custom_call_target="tpu_custom_call" | custom-call | flops 50000000 | bytes 1000000 | tf_op jit(solution)/shard_map/pallas_call | solution.py:370
  (23 shorter events, 0.7 us)
Async XLA Ops:
  0.6 102.3 %copy-start = (s32[16,16,9]{1,0,2:T(8,128)S(1)}, s32[16,16,9]{1,0,2:T(8,128)}, u32[]{:S(2)}) copy-start(s32[16,16,9]{1,0,2:T(8,128)} %param.21) | copy-start | bytes 27652
  65.4 75.6 %all-to-all-start.1 = ((f32[16,48,128]{2,1,0:T(8,128)}), f32[16,48,128]{2,1,0:T(8,128)S(1)}, u32[]{:S(2)}, u32[]{:S(2)}) async-start(f32[16,48,128]{2,1,0:T(8,128)} %broadcast_in_dim.4), calls=%async_computation.1 | async-start | bytes 786432 | tf_op jit(solution)/shard_map/all_to_all | solution.py:403
  75.0 22.5 %collective-permute-start = (bf16[64,1536]{1,0:T(8,128)(2,1)}, bf16[64,1536]{1,0:T(8,128)(2,1)S(1)}, u32[]{:S(2)}, u32[]{:S(2)}) collective-permute-start(bf16[64,1536]{1,0:T(8,128)(2,1)} %get-tuple-element.25), channel_id=1, source_target_pairs={{0,1},{1,2},{2,3},{3,4},{4,5},{5,6},{6,7},{7,8},{8,9},{9,10},{10,1... | collective-permute-start | bytes 589832 | tf_op jit(solution)/shard_map/ppermute | solution.py:393
  78.1 19.4 %collective-permute-start.1 = (bf16[64,1536]{1,0:T(8,128)(2,1)}, bf16[64,1536]{1,0:T(8,128)(2,1)S(1)}, u32[]{:S(2)}, u32[]{:S(2)}) collective-permute-start(bf16[64,1536]{1,0:T(8,128)(2,1)} %get-tuple-element.26), channel_id=1, source_target_pairs={{0,15},{1,0},{2,1},{3,2},{4,3},{5,4},{6,5},{7,6},{8,7},{9,8},{10,9... | collective-permute-start | bytes 589832 | tf_op jit(solution)/shard_map/ppermute | solution.py:393
  97.5 0.7 copy-start.3
  98.1 0.7 copy-start.4
  102.4 7.9 %collective-permute-start.2 = (bf16[96,1536]{1,0:T(8,128)(2,1)}, bf16[96,1536]{1,0:T(8,128)(2,1)S(1)}, u32[]{:S(2)}, u32[]{:S(2)}) collective-permute-start(bf16[96,1536]{1,0:T(8,128)(2,1)} %get-tuple-element.27), channel_id=1, source_target_pairs={{0,16},{16,32},{32,48},{48,64},{64,80},{80,96},{96,112},{112,128},... | collective-permute-start | bytes 884744 | tf_op jit(solution)/shard_map/ppermute | solution.py:393
  102.5 7.8 %collective-permute-start.3 = (bf16[96,1536]{1,0:T(8,128)(2,1)}, bf16[96,1536]{1,0:T(8,128)(2,1)S(1)}, u32[]{:S(2)}, u32[]{:S(2)}) collective-permute-start(bf16[96,1536]{1,0:T(8,128)(2,1)} %get-tuple-element.28), channel_id=1, source_target_pairs={{0,240},{16,0},{32,16},{48,32},{64,48},{80,64},{96,80},{112,96},{1... | collective-permute-start | bytes 884744 | tf_op jit(solution)/shard_map/ppermute | solution.py:393
  110.2 0.7 copy-start.8
  110.3 0.8 copy-start.9
  118.7 8.5 %collective-permute-start.4 = (f32[96,1536]{1,0:T(8,128)}, f32[96,1536]{1,0:T(8,128)S(1)}, u32[]{:S(2)}, u32[]{:S(2)}) collective-permute-start(f32[96,1536]{1,0:T(8,128)} %get-tuple-element.32), channel_id=1, source_target_pairs={{0,16},{16,32},{32,48},{48,64},{64,80},{80,96},{96,112},{112,128},... | collective-permute-start | bytes 1769480 | tf_op jit(solution)/shard_map/ppermute | solution.py:393
  120.0 9.8 %collective-permute-start.5 = (f32[96,1536]{1,0:T(8,128)}, f32[96,1536]{1,0:T(8,128)S(1)}, u32[]{:S(2)}, u32[]{:S(2)}) collective-permute-start(f32[96,1536]{1,0:T(8,128)} %get-tuple-element.33), channel_id=1, source_target_pairs={{0,240},{16,0},{32,16},{48,32},{64,48},{80,64},{96,80},{112,96},{1... | collective-permute-start | bytes 1769480 | tf_op jit(solution)/shard_map/ppermute | solution.py:393
  127.2 2.7 %copy-start.1 = (f32[96,1536]{1,0:T(8,128)}, f32[96,1536]{1,0:T(8,128)S(1)}, u32[]{:S(2)}) copy-start(f32[96,1536]{1,0:T(8,128)S(1)} %collective-permute-done.4.refs_1_.refs_3_) | copy-start | bytes 1769476
  129.8 0.8 copy-start.2
  134.4 17.6 %collective-permute-start.6 = (f32[64,1536]{1,0:T(8,128)}, f32[64,1536]{1,0:T(8,128)S(1)}, u32[]{:S(2)}, u32[]{:S(2)}) collective-permute-start(f32[64,1536]{1,0:T(8,128)} %get-tuple-element.36), channel_id=1, source_target_pairs={{0,1},{1,2},{2,3},{3,4},{4,5},{5,6},{6,7},{7,8},{8,9},{9,10},{10,1... | collective-permute-start | bytes 1179656 | tf_op jit(solution)/shard_map/ppermute | solution.py:393
  136.4 15.7 %collective-permute-start.7 = (f32[64,1536]{1,0:T(8,128)}, f32[64,1536]{1,0:T(8,128)S(1)}, u32[]{:S(2)}, u32[]{:S(2)}) collective-permute-start(f32[64,1536]{1,0:T(8,128)} %get-tuple-element.37), channel_id=1, source_target_pairs={{0,15},{1,0},{2,1},{3,2},{4,3},{5,4},{6,5},{7,6},{8,7},{9,8},{10,9... | collective-permute-start | bytes 1179656 | tf_op jit(solution)/shard_map/ppermute | solution.py:393
  141.8 16.6 %all-to-all-start.2 = ((bf16[16,48,128]{2,1,0:T(8,128)(2,1)}), bf16[16,48,128]{2,1,0:T(8,128)(2,1)S(1)}, u32[]{:S(2)}, u32[]{:S(2)}) async-start(bf16[16,48,128]{2,1,0:T(8,128)(2,1)} %broadcast_in_dim.5), calls=%async_computation.2 | async-start | bytes 393216 | tf_op jit(solution)/shard_map/all_to_all | solution.py:403
  152.1 0.8 copy-start.6
  152.8 0.7 copy-start.7
  158.4 0.7 copy-start.5

commit v3 on v2

v3 whole, which is shorter than its diff:
```python
import math

import jax
import jax.numpy as jnp
import numpy as np
from jax import lax
from jax.experimental import pallas as pl
from jax.experimental.pallas import tpu as pltpu
from jax.sharding import Mesh
from jax.sharding import PartitionSpec as P


HEADS = 12
HDIM = 128
TILE = 8
HALO = 2
HA = ("ha_0", "ha_1")
F32 = jnp.float32
BF16 = jnp.bfloat16
SCALE = 1.0 / math.sqrt(HDIM)

FRAMES = 2
OWN = FRAMES * TILE * TILE
SIDE = FRAMES * TILE * HALO
CORNER = HALO * HALO
BAND = HALO * TILE + 2 * CORNER
ENDS = FRAMES * BAND


def nt(a, b):
    return lax.dot_general(a, b, (((1,), (1,)), ((), ())), preferred_element_type=F32)


def nn(a, b):
    return lax.dot_general(a, b, (((1,), (0,)), ((), ())), preferred_element_type=F32)


def tn(a, b):
    return lax.dot_general(a, b, (((0,), (0,)), ((), ())), preferred_element_type=F32)


def exact(a, b):
    return lax.dot_general(
        a, b, (((1,), (0,)), ((), ())), precision=lax.Precision.HIGHEST, preferred_element_type=F32
    )


def own_row(frame, row, col):
    return frame * TILE * TILE + row * TILE + col


def side_row(frame, row, col):
    return (frame * TILE + row) * HALO + col


def select_sides():
    out = np.zeros((2, SIDE, OWN), np.float32)
    for side, first in enumerate((0, TILE - HALO)):
        for frame in range(FRAMES):
            for row in range(TILE):
                for col in range(HALO):
                    out[side, side_row(frame, row, col), own_row(frame, row, first + col)] = 1
    return out


def select_ends():
    out = np.zeros((2, ENDS, OWN + 2 * SIDE), np.float32)
    for end, first in enumerate((0, TILE - HALO)):
        for frame in range(FRAMES):
            at = frame * BAND
            for row in range(HALO):
                for col in range(TILE):
                    out[end, at, own_row(frame, first + row, col)] = 1
                    at += 1
            for side in range(2):
                for row in range(HALO):
                    for col in range(HALO):
                        out[end, at, OWN + side * SIDE + side_row(frame, first + row, col)] = 1
                        at += 1
    return out


SIDES = select_sides()
BANDS = select_ends()


GROUP = 4


def ends_kernel(select_ref, keys_ref, values_ref, left_ref, right_ref, top_ref, bottom_ref):
    for part, ref in enumerate((keys_ref, values_ref)):
        at = slice(part * SIDE, (part + 1) * SIDE)
        rows = jnp.concatenate([ref[...], left_ref[at, :], right_ref[at, :]], axis=0)
        to = slice(part * ENDS, (part + 1) * ENDS)
        top_ref[to, :] = nn(select_ref[0], rows).astype(BF16)
        bottom_ref[to, :] = nn(select_ref[1], rows).astype(BF16)


def first_kernel(
    ready,
    select_ref,
    keys_ref,
    values_ref,
    norm_ref,
    delta_ref,
    query_ref,
    out_grad_ref,
    key_ref,
    value_ref,
    left_ref,
    right_ref,
    grad_ref,
    stats_ref,
):
    for h in range(0, HEADS, GROUP):
        ready(h, 0)
        cols = slice(h * HDIM, (h + GROUP) * HDIM)
        for part, ref in enumerate((keys_ref, values_ref)):
            rows = ref[:, cols]
            at = slice(part * SIDE, (part + 1) * SIDE)
            left_ref[at, cols] = nn(select_ref[0], rows).astype(BF16)
            right_ref[at, cols] = nn(select_ref[1], rows).astype(BF16)
    heads = lax.broadcasted_iota(jnp.int32, (16, HEADS), 1)
    identity = (heads == lax.broadcasted_iota(jnp.int32, (16, HEADS), 0)).astype(F32)
    stats = []
    for which, ref in enumerate((norm_ref, delta_ref)):
        rows = lax.dot_general(
            identity,
            ref[...],
            (((1,), (1,)), ((), ())),
            precision=lax.Precision.HIGHEST,
            preferred_element_type=F32,
        )
        stats_ref[which * 16 : (which + 1) * 16, :] = rows
        stats.append(rows)
    norm, delta = stats
    text = key_ref.shape[0]
    piece = grad_ref.shape[0] // 16
    for h in range(HEADS):
        ready(h, 1)
        cols = slice(h * HDIM, (h + 1) * HDIM)
        q = query_ref[:, cols]
        g = out_grad_ref[:, cols]
        probs = jnp.exp(nt(key_ref[:, cols], q) * SCALE - norm[h : h + 1])
        prob_grad = nt(value_ref[:, cols], g)
        score_grad = (probs * (prob_grad - delta[h : h + 1])).astype(BF16)
        for part, grad in enumerate((nn(score_grad, q) * SCALE, nn(probs.astype(BF16), g))):
            for at in range(0, text, 16):
                chip, within = divmod(h * text + at, piece)
                to = (2 * chip + part) * piece + within
                grad_ref[to : to + 16, :] = grad[at : at + 16]


def backward(q, g, k, v, norm, delta, live):
    probs = jnp.exp(nt(k, q) * SCALE - norm)
    if live is not None:
        probs = probs * live
    score_grad = (probs * (nt(v, g) - delta)).astype(BF16)
    return probs.astype(BF16), score_grad


def own_kernel(
    live_ref,
    stats_ref,
    query_ref,
    out_grad_ref,
    keys_ref,
    values_ref,
    text_key_ref,
    text_value_ref,
    query_grad_ref,
    own_ref,
):
    text = text_key_ref.shape[0]
    rows = lax.broadcasted_iota(jnp.int32, (OWN + text, HDIM), 0)
    live = jnp.where(rows < OWN, live_ref[4].astype(F32), 1.0)
    for h in range(HEADS):
        cols = slice(h * HDIM, (h + 1) * HDIM)
        q = query_ref[:, cols]
        g = out_grad_ref[:, cols]
        k = jnp.concatenate([keys_ref[:, cols], text_key_ref[:, cols]], axis=0)
        v = jnp.concatenate([values_ref[:, cols], text_value_ref[:, cols]], axis=0)
        norm = stats_ref[h : h + 1, :]
        delta = stats_ref[16 + h : 17 + h, :]
        probs, score_grad = backward(q, g, k, v, norm, delta, live)
        query_grad_ref[:, cols] = tn(score_grad, k)
        own_ref[:OWN, cols] = nn(score_grad[:OWN], q) * SCALE
        own_ref[OWN:, cols] = nn(probs[:OWN], g)


def band_kernel(
    live_ref,
    stats_ref,
    query_ref,
    out_grad_ref,
    top_ref,
    bottom_ref,
    part_ref,
    top_grad_ref,
    bottom_grad_ref,
    query_grad_ref,
):
    def live(block):
        return live_ref[block].astype(F32)

    band = lax.rem(lax.broadcasted_iota(jnp.int32, (ENDS, HDIM), 0), BAND)
    lives = [
        jnp.where(
            band < HALO * TILE,
            live(first + 1),
            jnp.where(band < HALO * TILE + CORNER, live(first), live(first + 2)),
        )
        for first in (0, 6)
    ]
    two_halves(
        (stats_ref, query_ref, out_grad_ref, top_ref, bottom_ref, part_ref),
        (top_grad_ref, bottom_grad_ref, query_grad_ref),
        jnp.concatenate(lives, axis=0),
        1.0,
    )


def side_kernel(
    live_ref,
    stats_ref,
    query_ref,
    out_grad_ref,
    left_ref,
    right_ref,
    part_ref,
    left_grad_ref,
    right_grad_ref,
    query_grad_ref,
):
    rows = lax.broadcasted_iota(jnp.int32, (2 * SIDE, HDIM), 0)
    lives = jnp.where(rows < SIDE, live_ref[3].astype(F32), live_ref[5].astype(F32))
    two_halves(
        (stats_ref, query_ref, out_grad_ref, left_ref, right_ref, part_ref),
        (left_grad_ref, right_grad_ref, query_grad_ref),
        lives,
        SCALE,
    )


def two_halves(given, made, live, scale):
    stats_ref, query_ref, out_grad_ref, first_ref, second_ref, part_ref = given
    first_grad_ref, second_grad_ref, query_grad_ref = made
    rows = first_ref.shape[0] // 2
    for h in range(HEADS):
        cols = slice(h * HDIM, (h + 1) * HDIM)
        q = query_ref[:, cols]
        g = out_grad_ref[:, cols]
        k, v = (
            jnp.concatenate([first_ref[at, cols], second_ref[at, cols]], axis=0)
            for at in (slice(0, rows), slice(rows, 2 * rows))
        )
        norm = stats_ref[h : h + 1, :]
        delta = stats_ref[16 + h : 17 + h, :]
        probs, score_grad = backward(q, g, k, v, norm, delta, live)
        query_grad = part_ref[:, cols] + tn(score_grad, k)
        query_grad_ref[:, cols] = (query_grad * scale).astype(query_grad_ref.dtype)
        for at, grad in ((slice(0, rows), nn(score_grad, q) * SCALE), (slice(rows, 2 * rows), nn(probs, g))):
            first_grad_ref[at, cols] = grad[:rows]
            second_grad_ref[at, cols] = grad[rows:]


def corners_kernel(
    select_ref, left_ref, right_ref, above_ref, below_ref, left_out_ref, right_out_ref
):
    for part in range(2):
        side = slice(part * SIDE, (part + 1) * SIDE)
        ends = slice(part * ENDS, (part + 1) * ENDS)
        bands = jnp.concatenate([above_ref[ends, :], below_ref[ends, :]], axis=0)
        more = exact(select_ref[...], bands)
        left_out_ref[side, :] = left_ref[side, :] + more[:SIDE]
        right_out_ref[side, :] = right_ref[side, :] + more[SIDE:]


def sum_kernel(
    select_ref, own_ref, left_ref, right_ref, above_ref, below_ref, key_ref, value_ref
):
    edge = HALO * TILE
    for part, out in enumerate((key_ref, value_ref)):
        side = slice(part * SIDE, (part + 1) * SIDE)
        rows = jnp.concatenate([left_ref[side, :], right_ref[side, :]], axis=0)
        total = own_ref[part * OWN : (part + 1) * OWN, :] + exact(select_ref[...], rows)
        for frame in range(FRAMES):
            at = part * ENDS + frame * BAND
            top = frame * TILE * TILE
            bottom = top + TILE * TILE - edge
            end = top + TILE * TILE
            out[top : top + edge, :] = (
                total[top : top + edge] + above_ref[at : at + edge, :]
            ).astype(BF16)
            out[top + edge : bottom, :] = total[top + edge : bottom].astype(BF16)
            out[bottom:end, :] = (total[bottom:end] + below_ref[at : at + edge, :]).astype(BF16)


def words_kernel(parts_ref, key_ref, value_ref):
    text = key_ref.shape[0]
    rows = parts_ref.shape[1]
    for part, out in enumerate((key_ref, value_ref)):
        for h in range(HEADS):
            for at in range(0, text, 16):
                chip, within = divmod(h * text + at, rows)
                piece = parts_ref[2 * chip + part, within : within + 16, :]
                out[at : at + 16, h * HDIM : (h + 1) * HDIM] = piece


def call(kernel, outs, ins, us=1.0, smem=0, early=None):
    groups = HEADS // GROUP
    step = GROUP * HDIM

    def body(*refs):
        n = len(ins)
        outputs = refs[n : n + len(outs)]
        buffers = refs[n + len(outs) : -1]
        semaphores = refs[-1]
        small, wide = [], {}
        for i, (far, near) in enumerate(zip(refs[:n], buffers)):
            if ins[i].ndim == 2 and ins[i].shape[1] == groups * step:
                for m in range(groups):
                    at = (slice(None), slice(m * step, (m + 1) * step))
                    copy = pltpu.make_async_copy(far.at[at], near.at[at], semaphores.at[i, m])
                    wide.setdefault((int(i >= early), m), []).append(copy)
            else:
                small.append(pltpu.make_async_copy(far, near, semaphores.at[i, 0]))
        for copies in (small, *(wide[key] for key in sorted(wide))):
            for copy in copies:
                copy.start()
        for copy in small:
            copy.wait()

        def ready(h, part):
            if h % GROUP == 0:
                for copy in wide[part, h // GROUP]:
                    copy.wait()

        kernel(ready, *buffers, *outputs)

    here = pl.BlockSpec(memory_space=pltpu.VMEM)
    scalars = pl.BlockSpec(memory_space=pltpu.SMEM)
    if early is None:
        function, specs, scratch, limit = kernel, [scalars] * smem + [here] * (len(ins) - smem), [], 16
    else:
        function, specs, limit = body, [pl.BlockSpec(memory_space=pltpu.HBM)] * len(ins), 56
        scratch = [pltpu.VMEM(a.shape, a.dtype) for a in ins]
        scratch.append(pltpu.SemaphoreType.DMA((len(ins), groups)))
    return pl.pallas_call(
        function,
        out_shape=[jax.ShapeDtypeStruct(shape, dtype) for shape, dtype in outs],
        in_specs=specs,
        out_specs=[here] * len(outs),
        scratch_shapes=scratch,
        compiler_params=pltpu.CompilerParams(vmem_limit_bytes=limit * 2**20),
        cost_estimate=pl.CostEstimate(
            flops=int(us * 50000000), bytes_accessed=1000000, transcendentals=0
        ),
    )(*ins)


def shifted(value, axis, steps):
    count = lax.axis_size(axis)
    return lax.ppermute(value, axis, [(i, (i + steps) % count) for i in range(count)])


def by_query(rows):
    return rows.transpose(1, 2, 3, 0).reshape(OWN, HEADS)


def to_all(value, axis):
    count = lax.axis_size(axis)
    everyone = jnp.broadcast_to(value[None], (count, *value.shape))
    return lax.all_to_all(everyone, axis, 0, 0, tiled=True)


def local(
    queries, keys, values, out_grad, log_norm, delta_rows, text_keys, text_values, window_table
):
    shape = queries.shape
    width = shape[-1]
    text = text_keys.shape[0]
    q = queries.reshape(OWN, width)
    g = out_grad.reshape(OWN, width)
    k = keys.reshape(OWN, width)
    v = values.reshape(OWN, width)
    anchor = jnp.zeros((), jnp.int32)
    live = lax.dynamic_slice(
        window_table, (lax.axis_index(HA), lax.axis_index("wa"), anchor), (1, 1, 9)
    ).reshape(9)

    left, right, words, stats = call(
        first_kernel,
        [
            ((2 * SIDE, width), BF16),
            ((2 * SIDE, width), BF16),
            ((2 * HEADS * text, HDIM), F32),
            ((32, HDIM), F32),
        ],
        [
            jnp.asarray(SIDES, BF16),
            k,
            v,
            by_query(log_norm),
            by_query(delta_rows),
            q,
            g,
            text_keys,
            text_values,
        ],
        us=3,
        early=3,
    )
    count = lax.axis_size(HA)
    words = lax.all_to_all(words.reshape(count, -1, HDIM), HA, 0, 0, tiled=True)
    piece = words.sum(axis=0)
    pieces = to_all(piece, "wa")
    piece = pieces.sum(axis=0).astype(BF16)
    pieces = to_all(piece, HA)
    text_key_grad, text_value_grad = call(
        words_kernel, [((text, width), BF16)] * 2, [pieces]
    )

    from_right = shifted(left, "wa", -1)
    from_left = shifted(right, "wa", 1)
    part, own = call(
        own_kernel,
        [((OWN, width), F32), ((2 * OWN, width), F32)],
        [live, stats, q, g, k, v, text_keys, text_values],
        us=3,
        smem=1,
    )
    top, bottom = call(
        ends_kernel,
        [((2 * ENDS, width), BF16)] * 2,
        [jnp.asarray(BANDS, BF16), k, v, from_left, from_right],
    )
    from_below = shifted(top, HA, -1)
    from_above = shifted(bottom, HA, 1)
    top_grad, bottom_grad, part = call(
        band_kernel,
        [((2 * ENDS, width), F32)] * 2 + [((OWN, width), F32)],
        [live, stats, q, g, from_above, from_below, part],
        us=2,
        smem=1,
    )
    above = shifted(bottom_grad, HA, 1)
    below = shifted(top_grad, HA, -1)
    left_grad, right_grad, query_grad = call(
        side_kernel,
        [((2 * SIDE, width), F32)] * 2 + [((OWN, width), BF16)],
        [live, stats, q, g, from_left, from_right, part],
        us=2,
        smem=1,
    )
    back = np.concatenate([BANDS[0].T, BANDS[1].T], axis=1)
    left_grad, right_grad = call(
        corners_kernel,
        [((2 * SIDE, width), F32)] * 2,
        [jnp.asarray(back[OWN:], F32), left_grad, right_grad, above, below],
    )
    after = shifted(left_grad, "wa", -1)
    before = shifted(right_grad, "wa", 1)
    back = np.concatenate([SIDES[0].T, SIDES[1].T], axis=1)
    key_grad, value_grad = call(
        sum_kernel,
        [((OWN, width), BF16)] * 2,
        [jnp.asarray(back, F32), own, before, after, above, below],
    )
    return (
        query_grad.reshape(shape),
        key_grad.reshape(shape),
        value_grad.reshape(shape),
        text_key_grad,
        text_value_grad,
    )


def solution(mesh):
    split = Mesh(
        mesh.devices.reshape(mesh.shape["group"], 8, 2, mesh.shape["wa"]),
        ("group", "ha_0", "ha_1", "wa"),
    )
    return jax.shard_map(
        local,
        mesh=split,
        in_specs=(
            P("group", HA, "wa", None),
            P("group", HA, "wa", None),
            P("group", HA, "wa", None),
            P("group", HA, "wa", None),
            P(None, "group", HA, "wa"),
            P(None, "group", HA, "wa"),
            P("group", None),
            P("group", None),
            P(),
        ),
        out_specs=(
            P("group", HA, "wa", None),
            P("group", HA, "wa", None),
            P("group", HA, "wa", None),
            P("group", None),
            P("group", None),
        ),
        check_vma=False,
    )
```

time: 162 us -> 147 us (0.907)
  Pallas kernels: 37.1 us -> 21.5 us
  waiting for transfers between devices: 25.3 us -> 29.1 us
  local copies, waits for them, and re-layouts: 7.44 us -> 4.47 us
    pallas_call x9 -> x8, Pallas kernels: 37.1 us -> 21.5 us  [call(): pl.pallas_call(function, out_shape=[jax.ShapeDtypeStruct(shape, dtype) fo...]
    all_to_all x2, waiting for transfers between devices: 1.19 us -> 6.62 us  [to_all(): return lax.all_to_all(everyone, axis, 0, 0, tiled=True)]
    unnamed x20 -> x30, local copies, waits for them, and re-layouts: 5.09 us -> 2.65 us
  transfers between devices with their start and end apart: 10 -> 10, of which waited for: 4 -> 5; matrix products, arithmetic and copies ran while one was open for 1% -> 1% of each run, Pallas kernels for 19% -> 11%
where the time goes in v3:
time: 147 us
  blocking collectives  59.6 us (41%)
  starting transfers between devices  30.1 us (20%)
  waiting for transfers between devices  29.1 us (20%)
  Pallas kernels  21.5 us (15%)
  local copies, waits for them, and re-layouts  4.47 us (3%)
    all_to_all x1, blocking collectives, local(): words = lax.all_to_all(words.reshape(count, -1, HDIM), HA, 0, 0, tiled=True)  59.6 us
    ppermute x8, waiting for transfers between devices, shifted(): lax.ppermute(value, axis, [(i, (i + steps) % count) for i in range(count)])  22.5 us
    pallas_call x8, Pallas kernels, call(): pl.pallas_call(function, out_shape=[jax.ShapeDtypeStruct(shape, dtype) fo...  21.5 us
    ppermute x8, starting transfers between devices, shifted(): lax.ppermute(value, axis, [(i, (i + steps) % count) for i in range(count)])  16.1 us
    all_to_all x2, starting transfers between devices, to_all(): return lax.all_to_all(everyone, axis, 0, 0, tiled=True)  14 us
    all_to_all x2, waiting for transfers between devices, to_all(): return lax.all_to_all(everyone, axis, 0, 0, tiled=True)  6.62 us
  transfers between devices with their start and end apart: 10, of which 5 were waited for; matrix products, arithmetic and copies ran while one was open for 1% of the time, Pallas kernels for 11%

profile of v3, /device:TPU:65, one launch (start us, length us, event | category | flops | bytes accessed | tf_op | source)
XLA Modules:
  0.0 146.7 jit_solution(13357477303709529120)
XLA Ops:
  0.6 0.0 copy-start
  0.6 5.2 %shard_map.164 = (bf16[64,1536]{1,0:T(8,128)(2,1)}, bf16[64,1536]{1,0:T(8,128)(2,1)}, f32[768,128]{1,0:T(8,128)}, f32[32,128]{1,0:T(8,128)}) custom-call(bf16[2,32,128]{2,1,0:T(8,128)(2,1)} %constant.31.clone.refs_0_, bf16[128,1536]{1,0:T(8,128)(2,1)} %bitcast.22, bf16[128,1536]{1,0:T(8,128)(2,1)} %bitcast.25, f32[128,12]{1,0:T(8,128)} %bitcast.29, ...), custom_call_target="tpu_custom_call" | custom-call | flops 150000000 | bytes 1000000 | tf_op jit(solution)/shard_map/pallas_call | solution.py:349
  5.9 0.0 copy-start.3
  5.9 0.0 copy-start.11
  5.9 59.6 %all_to_all.15 = f32[16,48,128]{2,1,0:T(8,128)S(1)} all-to-all(f32[16,48,128]{2,1,0:T(8,128)} %bitcast.28), channel_id=1, replica_groups=mesh['group'=2,'ha_0'=8,'ha_1'=2,'wa'=16] {'ha_0','ha_1'}, dimensions={0} | all-to-all | bytes 786432 | tf_op jit(solution)/shard_map/all_to_all | solution.py:415
  65.6 0.8 broadcast_in_dim.4
  66.3 7.2 %all-to-all-start.1 = ((f32[16,48,128]{2,1,0:T(8,128)}), f32[16,48,128]{2,1,0:T(8,128)}, u32[]{:S(2)}, u32[]{:S(2)}) async-start(f32[16,48,128]{2,1,0:T(8,128)} %broadcast_in_dim.4), calls=%async_computation.1 | async-start | bytes 786432 | tf_op jit(solution)/shard_map/all_to_all | solution.py:374
  73.5 3.1 %collective-permute-start = (bf16[64,1536]{1,0:T(8,128)(2,1)S(1)}, bf16[64,1536]{1,0:T(8,128)(2,1)S(1)}, u32[]{:S(2)}, u32[]{:S(2)}) collective-permute-start(bf16[64,1536]{1,0:T(8,128)(2,1)S(1)} %copy-done.14), channel_id=1, source_target_pairs={{0,1},{1,2},{2,3},{3,4},{4,5},{5,6},{6,7},{7,8},{8,9},{9,10},{10,1... | collective-permute-start | bytes 589832 | tf_op jit(solution)/shard_map/ppermute | solution.py:364
  76.7 3.5 %collective-permute-start.1 = (bf16[64,1536]{1,0:T(8,128)(2,1)S(1)}, bf16[64,1536]{1,0:T(8,128)(2,1)S(1)}, u32[]{:S(2)}, u32[]{:S(2)}) collective-permute-start(bf16[64,1536]{1,0:T(8,128)(2,1)S(1)} %copy-done.13), channel_id=1, source_target_pairs={{0,15},{1,0},{2,1},{3,2},{4,3},{5,4},{6,5},{7,6},{8,7},{9,8},{10,9... | collective-permute-start | bytes 589832 | tf_op jit(solution)/shard_map/ppermute | solution.py:364
  80.2 18.2 %collective-permute-done.left_ref = bf16[64,1536]{1,0:T(8,128)(2,1)S(1)} collective-permute-done((bf16[64,1536]{1,0:T(8,128)(2,1)S(1)}, bf16[64,1536]{1,0:T(8,128)(2,1)S(1)}, u32[]{:S(2)}, u32[]{:S(2)}) %collective-permute-start) | collective-permute-done | bytes 196640 | tf_op jit(solution)/shard_map/ppermute | solution.py:364
  98.4 1.2 shard_map.165
  99.7 0.5 collective-permute-start.3
  100.2 0.3 dynamic-slice_reduce_fusion.live_ref
  100.6 3.8 %shard_map.166 = (f32[128,1536]{1,0:T(8,128)S(1)}, f32[256,1536]{1,0:T(8,128)S(1)}) custom-call(s32[9]{0:T(128)S(1)} %dynamic-slice_reduce_fusion.live_ref, f32[32,128]{1,0:T(8,128)S(1)} %copy-done.9, bf16[128,1536]{1,0:T(8,128)(2,1)S(1)} %bitcast.15, bf16[128,1536]{1,0:T(8,128)(2,1)S(1)} %bitcast.19, bf16[128,1536]{1,0:T(8,128)(2,1)S(1)} %bitcast.24, ...), custom_call_target="tpu_custom_call" | custom-call | flops 150000000 | bytes 1000000 | tf_op jit(solution)/shard_map/pallas_call | solution.py:349
  104.4 1.2 copy-done.5
  105.6 0.5 collective-permute-done.3.bottom_ref
  106.1 3.4 %shard_map.167 = (f32[96,1536]{1,0:T(8,128)S(1)}, f32[96,1536]{1,0:T(8,128)S(1)}, f32[128,1536]{1,0:T(8,128)S(1)}) custom-call(s32[9]{0:T(128)S(1)} %dynamic-slice_reduce_fusion.live_ref, f32[32,128]{1,0:T(8,128)S(1)} %copy-done.9, bf16[128,1536]{1,0:T(8,128)(2,1)S(1)} %bitcast.16, bf16[128,1536]{1,0:T(8,128)(2,1)S(1)} %bitcast.20, ...), custom_call_target="tpu_custom_call" | custom-call | flops 100000000 | bytes 1000000 | tf_op jit(solution)/shard_map/pallas_call | solution.py:349
  109.5 0.8 collective-permute-start.4
  110.3 1.7 %collective-permute-start.5 = (f32[96,1536]{1,0:T(8,128)S(1)}, f32[96,1536]{1,0:T(8,128)S(1)}, u32[]{:S(2)}, u32[]{:S(2)}) collective-permute-start(f32[96,1536]{1,0:T(8,128)S(1)} %get-tuple-element.37), channel_id=1, source_target_pairs={{0,240},{16,0},{32,16},{48,32},{64,48},{80,64},{96,80},{112,96},{1... | collective-permute-start | bytes 1769480 | tf_op jit(solution)/shard_map/ppermute | solution.py:364
  112.0 4.2 %shard_map.168 = (f32[64,1536]{1,0:T(8,128)S(1)}, f32[64,1536]{1,0:T(8,128)S(1)}, bf16[128,1536]{1,0:T(8,128)(2,1)}) custom-call(s32[9]{0:T(128)S(1)} %dynamic-slice_reduce_fusion.live_ref, f32[32,128]{1,0:T(8,128)S(1)} %copy-done.9, bf16[128,1536]{1,0:T(8,128)(2,1)S(1)} %bitcast.17, bf16[128,1536]{1,0:T(8,128)(2,1)S(1)} %bitcast.21, ...), custom_call_target="tpu_custom_call" | custom-call | flops 100000000 | bytes 1000000 | tf_op jit(solution)/shard_map/pallas_call | solution.py:349
  116.1 1.0 collective-permute-done.4.above_ref
  117.1 2.8 %collective-permute-done.5.below_ref = f32[96,1536]{1,0:T(8,128)S(1)} collective-permute-done((f32[96,1536]{1,0:T(8,128)S(1)}, f32[96,1536]{1,0:T(8,128)S(1)}, u32[]{:S(2)}, u32[]{:S(2)}) %collective-permute-start.5) | collective-permute-done | bytes 589856 | tf_op jit(solution)/shard_map/ppermute | solution.py:364
  119.9 0.8 shard_map.169
  120.7 2.0 %collective-permute-start.6 = (f32[64,1536]{1,0:T(8,128)S(1)}, f32[64,1536]{1,0:T(8,128)S(1)}, u32[]{:S(2)}, u32[]{:S(2)}) collective-permute-start(f32[64,1536]{1,0:T(8,128)S(1)} %get-tuple-element.38), channel_id=1, source_target_pairs={{0,1},{1,2},{2,3},{3,4},{4,5},{5,6},{6,7},{7,8},{8,9},{9,10},{10,1... | collective-permute-start | bytes 1179656 | tf_op jit(solution)/shard_map/ppermute | solution.py:364
  122.7 4.6 %collective-permute-start.7 = (f32[64,1536]{1,0:T(8,128)S(1)}, f32[64,1536]{1,0:T(8,128)S(1)}, u32[]{:S(2)}, u32[]{:S(2)}) collective-permute-start(f32[64,1536]{1,0:T(8,128)S(1)} %get-tuple-element.39), channel_id=1, source_target_pairs={{0,15},{1,0},{2,1},{3,2},{4,3},{5,4},{6,5},{7,6},{8,7},{9,8},{10,9... | collective-permute-start | bytes 1179656 | tf_op jit(solution)/shard_map/ppermute | solution.py:364
  127.3 1.0 reduce_sum.19
  128.3 0.7 broadcast_in_dim.5
  129.0 6.8 %all-to-all-start.2 = ((bf16[16,48,128]{2,1,0:T(8,128)(2,1)}), bf16[16,48,128]{2,1,0:T(8,128)(2,1)S(1)}, u32[]{:S(2)}, u32[]{:S(2)}) async-start(bf16[16,48,128]{2,1,0:T(8,128)(2,1)} %broadcast_in_dim.5), calls=%async_computation.2 | async-start | bytes 393216 | tf_op jit(solution)/shard_map/all_to_all | solution.py:374
  135.8 1.4 copy-done.6
  137.2 2.1 %shard_map.170 = (bf16[128,1536]{1,0:T(8,128)(2,1)}, bf16[128,1536]{1,0:T(8,128)(2,1)}) custom-call(f32[128,64]{1,0:T(8,128)S(1)} %copy-done.10, f32[256,1536]{1,0:T(8,128)S(1)} %copy-done.6, f32[64,1536]{1,0:T(8,128)S(1)} %collective-permute-done.6.left_ref, f32[64,1536]{1,0:T(8,128)S(1)} %collective-permute-done.7.right_ref, ...), custom_call_target="tpu_custom_call" | custom-call | flops 50000000 | bytes 1000000 | tf_op jit(solution)/shard_map/pallas_call | solution.py:349
  139.4 6.6 %all-to-all-done.2.parts_ref = bf16[16,48,128]{2,1,0:T(8,128)(2,1)S(1)} async-done(((bf16[16,48,128]{2,1,0:T(8,128)(2,1)}), bf16[16,48,128]{2,1,0:T(8,128)(2,1)S(1)}, u32[]{:S(2)}, u32[]{:S(2)}) %all-to-all-start.2) | async-done | bytes 196640 | tf_op jit(solution)/shard_map/all_to_all | solution.py:374
  146.0 0.7 shard_map.171
  (32 shorter events, 0.1 us)
Async XLA Ops:
  0.6 99.5 %copy-start = (s32[16,16,9]{1,0,2:T(8,128)S(1)}, s32[16,16,9]{1,0,2:T(8,128)}, u32[]{:S(2)}) copy-start(s32[16,16,9]{1,0,2:T(8,128)} %param.21) | copy-start | bytes 27652
  5.8 67.7 %copy-start.14 = (bf16[64,1536]{1,0:T(8,128)(2,1)S(1)}, bf16[64,1536]{1,0:T(8,128)(2,1)}, u32[]{:S(2)}) copy-start(bf16[64,1536]{1,0:T(8,128)(2,1)} %get-tuple-element.26) | copy-start | bytes 589828
  5.9 70.8 %copy-start.13 = (bf16[64,1536]{1,0:T(8,128)(2,1)S(1)}, bf16[64,1536]{1,0:T(8,128)(2,1)}, u32[]{:S(2)}) copy-start(bf16[64,1536]{1,0:T(8,128)(2,1)} %get-tuple-element.27) | copy-start | bytes 589828
  5.9 92.5 %copy-start.3 = (bf16[2,8,8,1536]{3,2,1,0:T(8,128)(2,1)S(1)}, bf16[2,8,8,1536]{3,2,1,0:T(8,128)(2,1)}, u32[]{:S(2)}) copy-start(bf16[2,8,8,1536]{3,2,1,0:T(8,128)(2,1)} %param.14) | copy-start | bytes 1179652
  5.9 92.5 %copy-start.4 = (bf16[2,8,8,1536]{3,2,1,0:T(8,128)(2,1)S(1)}, bf16[2,8,8,1536]{3,2,1,0:T(8,128)(2,1)}, u32[]{:S(2)}) copy-start(bf16[2,8,8,1536]{3,2,1,0:T(8,128)(2,1)} %param.15) | copy-start | bytes 1179652
  5.9 92.5 %copy-start.11 = (bf16[2,48,192]{2,1,0:T(8,128)(2,1)S(1)}, bf16[2,48,192]{2,1,0:T(8,128)(2,1)}, u32[]{:S(2)}) copy-start(bf16[2,48,192]{2,1,0:T(8,128)(2,1)} %constant.32.clone.select_ref) | copy-start | bytes 110596
  65.5 35.0 %copy-start.1 = (bf16[2,8,8,1536]{3,2,1,0:T(8,128)(2,1)S(1)}, bf16[2,8,8,1536]{3,2,1,0:T(8,128)(2,1)}, u32[]{:S(2)}) copy-start(bf16[2,8,8,1536]{3,2,1,0:T(8,128)(2,1)} %param.13) | copy-start | bytes 1179652
  65.5 35.0 %copy-start.2 = (bf16[2,8,8,1536]{3,2,1,0:T(8,128)(2,1)S(1)}, bf16[2,8,8,1536]{3,2,1,0:T(8,128)(2,1)}, u32[]{:S(2)}) copy-start(bf16[2,8,8,1536]{3,2,1,0:T(8,128)(2,1)} %param.16) | copy-start | bytes 1179652
  65.5 35.0 %copy-start.7 = (bf16[32,1536]{1,0:T(8,128)(2,1)S(1)}, bf16[32,1536]{1,0:T(8,128)(2,1)}, u32[]{:S(2)}) copy-start(bf16[32,1536]{1,0:T(8,128)(2,1)} %text_key_ref.1) | copy-start | bytes 294916
  65.5 35.0 %copy-start.8 = (bf16[32,1536]{1,0:T(8,128)(2,1)S(1)}, bf16[32,1536]{1,0:T(8,128)(2,1)}, u32[]{:S(2)}) copy-start(bf16[32,1536]{1,0:T(8,128)(2,1)} %text_value_ref.1) | copy-start | bytes 294916
  65.5 35.0 %copy-start.9 = (f32[32,128]{1,0:T(8,128)S(1)}, f32[32,128]{1,0:T(8,128)}, u32[]{:S(2)}) copy-start(f32[32,128]{1,0:T(8,128)} %get-tuple-element.25.stats_ref) | copy-start | bytes 49156
  66.3 60.9 %all-to-all-start.1 = ((f32[16,48,128]{2,1,0:T(8,128)}), f32[16,48,128]{2,1,0:T(8,128)}, u32[]{:S(2)}, u32[]{:S(2)}) async-start(f32[16,48,128]{2,1,0:T(8,128)} %broadcast_in_dim.4), calls=%async_computation.1 | async-start | bytes 786432 | tf_op jit(solution)/shard_map/all_to_all | solution.py:374
  73.5 24.9 %collective-permute-start = (bf16[64,1536]{1,0:T(8,128)(2,1)S(1)}, bf16[64,1536]{1,0:T(8,128)(2,1)S(1)}, u32[]{:S(2)}, u32[]{:S(2)}) collective-permute-start(bf16[64,1536]{1,0:T(8,128)(2,1)S(1)} %copy-done.14), channel_id=1, source_target_pairs={{0,1},{1,2},{2,3},{3,4},{4,5},{5,6},{6,7},{7,8},{8,9},{9,10},{10,1... | collective-permute-start | bytes 589832 | tf_op jit(solution)/shard_map/ppermute | solution.py:364
  76.7 21.8 %collective-permute-start.1 = (bf16[64,1536]{1,0:T(8,128)(2,1)S(1)}, bf16[64,1536]{1,0:T(8,128)(2,1)S(1)}, u32[]{:S(2)}, u32[]{:S(2)}) collective-permute-start(bf16[64,1536]{1,0:T(8,128)(2,1)S(1)} %copy-done.13), channel_id=1, source_target_pairs={{0,15},{1,0},{2,1},{3,2},{4,3},{5,4},{6,5},{7,6},{8,7},{9,8},{10,9... | collective-permute-start | bytes 589832 | tf_op jit(solution)/shard_map/ppermute | solution.py:364
  99.7 5.9 %collective-permute-start.2 = (bf16[96,1536]{1,0:T(8,128)(2,1)}, bf16[96,1536]{1,0:T(8,128)(2,1)S(1)}, u32[]{:S(2)}, u32[]{:S(2)}) collective-permute-start(bf16[96,1536]{1,0:T(8,128)(2,1)} %get-tuple-element.28), channel_id=1, source_target_pairs={{0,16},{16,32},{32,48},{48,64},{64,80},{80,96},{96,112},{112,128},... | collective-permute-start | bytes 884744 | tf_op jit(solution)/shard_map/ppermute | solution.py:364
  99.7 6.4 %collective-permute-start.3 = (bf16[96,1536]{1,0:T(8,128)(2,1)S(1)}, bf16[96,1536]{1,0:T(8,128)(2,1)S(1)}, u32[]{:S(2)}, u32[]{:S(2)}) collective-permute-start(bf16[96,1536]{1,0:T(8,128)(2,1)S(1)} %get-tuple-element.29), channel_id=1, source_target_pairs={{0,240},{16,0},{32,16},{48,32},{64,48},{80,64},{96,80},{112,96},{1... | collective-permute-start | bytes 884744 | tf_op jit(solution)/shard_map/ppermute | solution.py:364
  104.4 1.2 copy-start.5
  106.1 13.8 %copy-start.12 = (f32[64,96]{1,0:T(8,128)S(1)}, f32[64,96]{1,0:T(8,128)}, u32[]{:S(2)}) copy-start(f32[64,96]{1,0:T(8,128)} %constant.33.clone.select_ref) | copy-start | bytes 73732
  109.5 7.6 %collective-permute-start.4 = (f32[96,1536]{1,0:T(8,128)S(1)}, f32[96,1536]{1,0:T(8,128)S(1)}, u32[]{:S(2)}, u32[]{:S(2)}) collective-permute-start(f32[96,1536]{1,0:T(8,128)S(1)} %get-tuple-element.36), channel_id=1, source_target_pairs={{0,16},{16,32},{32,48},{48,64},{64,80},{80,96},{96,112},{112,128},... | collective-permute-start | bytes 1769480 | tf_op jit(solution)/shard_map/ppermute | solution.py:364
  110.3 9.6 %collective-permute-start.5 = (f32[96,1536]{1,0:T(8,128)S(1)}, f32[96,1536]{1,0:T(8,128)S(1)}, u32[]{:S(2)}, u32[]{:S(2)}) collective-permute-start(f32[96,1536]{1,0:T(8,128)S(1)} %get-tuple-element.37), channel_id=1, source_target_pairs={{0,240},{16,0},{32,16},{48,32},{64,48},{80,64},{96,80},{112,96},{1... | collective-permute-start | bytes 1769480 | tf_op jit(solution)/shard_map/ppermute | solution.py:364
  116.1 19.7 %copy-start.10 = (f32[128,64]{1,0:T(8,128)S(1)}, f32[128,64]{1,0:T(8,128)}, u32[]{:S(2)}) copy-start(f32[128,64]{1,0:T(8,128)} %constant.34.clone.select_ref) | copy-start | bytes 98308
  120.7 15.1 %collective-permute-start.6 = (f32[64,1536]{1,0:T(8,128)S(1)}, f32[64,1536]{1,0:T(8,128)S(1)}, u32[]{:S(2)}, u32[]{:S(2)}) collective-permute-start(f32[64,1536]{1,0:T(8,128)S(1)} %get-tuple-element.38), channel_id=1, source_target_pairs={{0,1},{1,2},{2,3},{3,4},{4,5},{5,6},{6,7},{7,8},{8,9},{9,10},{10,1... | collective-permute-start | bytes 1179656 | tf_op jit(solution)/shard_map/ppermute | solution.py:364
  122.7 13.1 %collective-permute-start.7 = (f32[64,1536]{1,0:T(8,128)S(1)}, f32[64,1536]{1,0:T(8,128)S(1)}, u32[]{:S(2)}, u32[]{:S(2)}) collective-permute-start(f32[64,1536]{1,0:T(8,128)S(1)} %get-tuple-element.39), channel_id=1, source_target_pairs={{0,15},{1,0},{2,1},{3,2},{4,3},{5,4},{6,5},{7,6},{8,7},{9,8},{10,9... | collective-permute-start | bytes 1179656 | tf_op jit(solution)/shard_map/ppermute | solution.py:364
  129.0 17.0 %all-to-all-start.2 = ((bf16[16,48,128]{2,1,0:T(8,128)(2,1)}), bf16[16,48,128]{2,1,0:T(8,128)(2,1)S(1)}, u32[]{:S(2)}, u32[]{:S(2)}) async-start(bf16[16,48,128]{2,1,0:T(8,128)(2,1)} %broadcast_in_dim.5), calls=%async_computation.2 | async-start | bytes 393216 | tf_op jit(solution)/shard_map/all_to_all | solution.py:374
  135.8 1.4 copy-start.6

commit v4 on v3

--- a/solution.py
+++ b/solution.py
@@ -84,7 +84,7 @@
 BANDS = select_ends()
 
 
-GROUP = 4
+GROUP = 2
 
 
 def ends_kernel(select_ref, keys_ref, values_ref, left_ref, right_ref, top_ref, bottom_ref):
@@ -96,30 +96,17 @@
         bottom_ref[to, :] = nn(select_ref[1], rows).astype(BF16)
 
 
-def first_kernel(
-    ready,
-    select_ref,
-    keys_ref,
-    values_ref,
-    norm_ref,
-    delta_ref,
-    query_ref,
-    out_grad_ref,
-    key_ref,
-    value_ref,
-    left_ref,
-    right_ref,
-    grad_ref,
-    stats_ref,
-):
-    for h in range(0, HEADS, GROUP):
-        ready(h, 0)
-        cols = slice(h * HDIM, (h + GROUP) * HDIM)
-        for part, ref in enumerate((keys_ref, values_ref)):
-            rows = ref[:, cols]
-            at = slice(part * SIDE, (part + 1) * SIDE)
-            left_ref[at, cols] = nn(select_ref[0], rows).astype(BF16)
-            right_ref[at, cols] = nn(select_ref[1], rows).astype(BF16)
+def sides_kernel(select_ref, keys_ref, values_ref, left_ref, right_ref):
+    for part, ref in enumerate((keys_ref, values_ref)):
+        rows = ref[...]
+        at = slice(part * SIDE, (part + 1) * SIDE)
+        left_ref[at, :] = nn(select_ref[0], rows).astype(BF16)
+        right_ref[at, :] = nn(select_ref[1], rows).astype(BF16)
+
+
+def text_kernel(
+    ready, norm_ref, delta_ref, query_ref, out_grad_ref, key_ref, value_ref, grad_ref, stats_ref
+):
     heads = lax.broadcasted_iota(jnp.int32, (16, HEADS), 1)
     identity = (heads == lax.broadcasted_iota(jnp.int32, (16, HEADS), 0)).astype(F32)
     stats = []
@@ -137,7 +124,7 @@
     text = key_ref.shape[0]
     piece = grad_ref.shape[0] // 16
     for h in range(HEADS):
-        ready(h, 1)
+        ready(h)
         cols = slice(h * HDIM, (h + 1) * HDIM)
         q = query_ref[:, cols]
         g = out_grad_ref[:, cols]
@@ -307,7 +294,7 @@
                 out[at : at + 16, h * HDIM : (h + 1) * HDIM] = piece
 
 
-def call(kernel, outs, ins, us=1.0, smem=0, early=None):
+def call(kernel, outs, ins, us=1.0, smem=0, fetch=False):
     groups = HEADS // GROUP
     step = GROUP * HDIM
 
@@ -316,31 +303,31 @@
         outputs = refs[n : n + len(outs)]
         buffers = refs[n + len(outs) : -1]
         semaphores = refs[-1]
-        small, wide = [], {}
+        small, wide = [], [[] for _ in range(groups)]
         for i, (far, near) in enumerate(zip(refs[:n], buffers)):
             if ins[i].ndim == 2 and ins[i].shape[1] == groups * step:
                 for m in range(groups):
                     at = (slice(None), slice(m * step, (m + 1) * step))
                     copy = pltpu.make_async_copy(far.at[at], near.at[at], semaphores.at[i, m])
-                    wide.setdefault((int(i >= early), m), []).append(copy)
+                    wide[m].append(copy)
             else:
                 small.append(pltpu.make_async_copy(far, near, semaphores.at[i, 0]))
-        for copies in (small, *(wide[key] for key in sorted(wide))):
+        for copies in (small, *wide):
             for copy in copies:
                 copy.start()
         for copy in small:
             copy.wait()
 
-        def ready(h, part):
+        def ready(h):
             if h % GROUP == 0:
-                for copy in wide[part, h // GROUP]:
+                for copy in wide[h // GROUP]:
                     copy.wait()
 
         kernel(ready, *buffers, *outputs)
 
     here = pl.BlockSpec(memory_space=pltpu.VMEM)
     scalars = pl.BlockSpec(memory_space=pltpu.SMEM)
-    if early is None:
+    if not fetch:
         function, specs, scratch, limit = kernel, [scalars] * smem + [here] * (len(ins) - smem), [], 16
     else:
         function, specs, limit = body, [pl.BlockSpec(memory_space=pltpu.HBM)] * len(ins), 56
@@ -389,27 +376,12 @@
         window_table, (lax.axis_index(HA), lax.axis_index("wa"), anchor), (1, 1, 9)
     ).reshape(9)
 
-    left, right, words, stats = call(
-        first_kernel,
-        [
-            ((2 * SIDE, width), BF16),
-            ((2 * SIDE, width), BF16),
-            ((2 * HEADS * text, HDIM), F32),
-            ((32, HDIM), F32),
-        ],
-        [
-            jnp.asarray(SIDES, BF16),
-            k,
-            v,
-            by_query(log_norm),
-            by_query(delta_rows),
-            q,
-            g,
-            text_keys,
-            text_values,
-        ],
+    words, stats = call(
+        text_kernel,
+        [((2 * HEADS * text, HDIM), F32), ((32, HDIM), F32)],
+        [by_query(log_norm), by_query(delta_rows), q, g, text_keys, text_values],
         us=3,
-        early=3,
+        fetch=True,
     )
     count = lax.axis_size(HA)
     words = lax.all_to_all(words.reshape(count, -1, HDIM), HA, 0, 0, tiled=True)
@@ -421,6 +393,9 @@
         words_kernel, [((text, width), BF16)] * 2, [pieces]
     )
 
+    left, right = call(
+        sides_kernel, [((2 * SIDE, width), BF16)] * 2, [jnp.asarray(SIDES, BF16), k, v]
+    )
     from_right = shifted(left, "wa", -1)
     from_left = shifted(right, "wa", 1)
     part, own = call(

time: 147 us -> 147 us (level)
    pallas_call x8 -> x9, Pallas kernels: 21.5 us -> 21.6 us  [call(): pl.pallas_call(function, out_shape=[jax.ShapeDtypeStruct(shape, dtype) fo...]
where the time goes in v4:
time: 147 us
  blocking collectives  59.6 us (41%)
  starting transfers between devices  30.1 us (20%)
  waiting for transfers between devices  28.8 us (20%)
  Pallas kernels  21.6 us (15%)
  local copies, waits for them, and re-layouts  4.47 us (3%)
    all_to_all x1, blocking collectives, local(): words = lax.all_to_all(words.reshape(count, -1, HDIM), HA, 0, 0, tiled=True)  59.6 us
    ppermute x8, waiting for transfers between devices, shifted(): lax.ppermute(value, axis, [(i, (i + steps) % count) for i in range(count)])  22.2 us
    pallas_call x9, Pallas kernels, call(): pl.pallas_call(function, out_shape=[jax.ShapeDtypeStruct(shape, dtype) fo...  21.6 us
    ppermute x8, starting transfers between devices, shifted(): lax.ppermute(value, axis, [(i, (i + steps) % count) for i in range(count)])  16.1 us
    all_to_all x2, starting transfers between devices, to_all(): return lax.all_to_all(everyone, axis, 0, 0, tiled=True)  14 us
    all_to_all x2, waiting for transfers between devices, to_all(): return lax.all_to_all(everyone, axis, 0, 0, tiled=True)  6.62 us
  transfers between devices with their start and end apart: 10, of which 5 were waited for; matrix products, arithmetic and copies ran while one was open for 1% of the time, Pallas kernels for 11%

profile of v4, /device:TPU:65, one launch (start us, length us, event | category | flops | bytes accessed | tf_op | source)
XLA Modules:
  0.0 146.5 jit_solution(10228809314888838561)
XLA Ops:
  0.6 0.0 copy-start
  0.7 0.0 copy-start.13
  0.7 5.0 %shard_map.164 = (f32[768,128]{1,0:T(8,128)}, f32[32,128]{1,0:T(8,128)}) custom-call(f32[128,12]{1,0:T(8,128)} %bitcast.29, f32[128,12]{1,0:T(8,128)} %bitcast.30, bf16[128,1536]{1,0:T(8,128)(2,1)} %bitcast.14, bf16[128,1536]{1,0:T(8,128)(2,1)} %bitcast.18, bf16[32,1536]{1,0:T(8,128)(2,1)} %text_key_ref.1, bf16[32,1536]{1,0:T(8,128)(2,1)} %text_value_ref.1), custom_call_target="tpu_custom_call" | custom-call | flops 150000000 | bytes 1000000 | tf_op jit(solution)/shard_map/pallas_call | solution.py:336
  5.7 59.6 %all_to_all.15 = f32[16,48,128]{2,1,0:T(8,128)S(1)} all-to-all(f32[16,48,128]{2,1,0:T(8,128)} %bitcast.28), channel_id=1, replica_groups=mesh['group'=2,'ha_0'=8,'ha_1'=2,'wa'=16] {'ha_0','ha_1'}, dimensions={0} | all-to-all | bytes 786432 | tf_op jit(solution)/shard_map/all_to_all | solution.py:387
  65.4 0.8 broadcast_in_dim.4
  66.2 7.2 %all-to-all-start.1 = ((f32[16,48,128]{2,1,0:T(8,128)}), f32[16,48,128]{2,1,0:T(8,128)}, u32[]{:S(2)}, u32[]{:S(2)}) async-start(f32[16,48,128]{2,1,0:T(8,128)} %broadcast_in_dim.4), calls=%async_computation.1 | async-start | bytes 786432 | tf_op jit(solution)/shard_map/all_to_all | solution.py:361
  73.4 0.3 shard_map.165
  73.7 3.1 %collective-permute-start = (bf16[64,1536]{1,0:T(8,128)(2,1)S(1)}, bf16[64,1536]{1,0:T(8,128)(2,1)S(1)}, u32[]{:S(2)}, u32[]{:S(2)}) collective-permute-start(bf16[64,1536]{1,0:T(8,128)(2,1)S(1)} %get-tuple-element.26), channel_id=1, source_target_pairs={{0,1},{1,2},{2,3},{3,4},{4,5},{5,6},{6,7},{7,8},{8,9},{9,10},{10,1... | collective-permute-start | bytes 589832 | tf_op jit(solution)/shard_map/ppermute | solution.py:351
  76.8 3.5 %collective-permute-start.1 = (bf16[64,1536]{1,0:T(8,128)(2,1)S(1)}, bf16[64,1536]{1,0:T(8,128)(2,1)S(1)}, u32[]{:S(2)}, u32[]{:S(2)}) collective-permute-start(bf16[64,1536]{1,0:T(8,128)(2,1)S(1)} %get-tuple-element.27), channel_id=1, source_target_pairs={{0,15},{1,0},{2,1},{3,2},{4,3},{5,4},{6,5},{7,6},{8,7},{9,8},{10,9... | collective-permute-start | bytes 589832 | tf_op jit(solution)/shard_map/ppermute | solution.py:351
  80.3 17.9 %collective-permute-done.left_ref = bf16[64,1536]{1,0:T(8,128)(2,1)S(1)} collective-permute-done((bf16[64,1536]{1,0:T(8,128)(2,1)S(1)}, bf16[64,1536]{1,0:T(8,128)(2,1)S(1)}, u32[]{:S(2)}, u32[]{:S(2)}) %collective-permute-start) | collective-permute-done | bytes 196640 | tf_op jit(solution)/shard_map/ppermute | solution.py:351
  98.2 1.2 shard_map.166
  99.5 0.5 collective-permute-start.3
  100.0 0.3 dynamic-slice_reduce_fusion.live_ref
  100.4 3.8 %shard_map.167 = (f32[128,1536]{1,0:T(8,128)S(1)}, f32[256,1536]{1,0:T(8,128)S(1)}) custom-call(s32[9]{0:T(128)S(1)} %dynamic-slice_reduce_fusion.live_ref, f32[32,128]{1,0:T(8,128)S(1)} %copy-done.9, bf16[128,1536]{1,0:T(8,128)(2,1)S(1)} %bitcast.15, bf16[128,1536]{1,0:T(8,128)(2,1)S(1)} %bitcast.19, bf16[128,1536]{1,0:T(8,128)(2,1)S(1)} %bitcast.24, ...), custom_call_target="tpu_custom_call" | custom-call | flops 150000000 | bytes 1000000 | tf_op jit(solution)/shard_map/pallas_call | solution.py:336
  104.2 1.2 copy-done.5
  105.4 0.5 collective-permute-done.3.bottom_ref
  105.9 3.4 %shard_map.168 = (f32[96,1536]{1,0:T(8,128)S(1)}, f32[96,1536]{1,0:T(8,128)S(1)}, f32[128,1536]{1,0:T(8,128)S(1)}) custom-call(s32[9]{0:T(128)S(1)} %dynamic-slice_reduce_fusion.live_ref, f32[32,128]{1,0:T(8,128)S(1)} %copy-done.9, bf16[128,1536]{1,0:T(8,128)(2,1)S(1)} %bitcast.16, bf16[128,1536]{1,0:T(8,128)(2,1)S(1)} %bitcast.20, ...), custom_call_target="tpu_custom_call" | custom-call | flops 100000000 | bytes 1000000 | tf_op jit(solution)/shard_map/pallas_call | solution.py:336
  109.3 0.8 collective-permute-start.4
  110.1 1.7 %collective-permute-start.5 = (f32[96,1536]{1,0:T(8,128)S(1)}, f32[96,1536]{1,0:T(8,128)S(1)}, u32[]{:S(2)}, u32[]{:S(2)}) collective-permute-start(f32[96,1536]{1,0:T(8,128)S(1)} %get-tuple-element.37), channel_id=1, source_target_pairs={{0,240},{16,0},{32,16},{48,32},{64,48},{80,64},{96,80},{112,96},{1... | collective-permute-start | bytes 1769480 | tf_op jit(solution)/shard_map/ppermute | solution.py:351
  111.8 4.2 %shard_map.169 = (f32[64,1536]{1,0:T(8,128)S(1)}, f32[64,1536]{1,0:T(8,128)S(1)}, bf16[128,1536]{1,0:T(8,128)(2,1)}) custom-call(s32[9]{0:T(128)S(1)} %dynamic-slice_reduce_fusion.live_ref, f32[32,128]{1,0:T(8,128)S(1)} %copy-done.9, bf16[128,1536]{1,0:T(8,128)(2,1)S(1)} %bitcast.17, bf16[128,1536]{1,0:T(8,128)(2,1)S(1)} %bitcast.21, ...), custom_call_target="tpu_custom_call" | custom-call | flops 100000000 | bytes 1000000 | tf_op jit(solution)/shard_map/pallas_call | solution.py:336
  115.9 1.0 collective-permute-done.4.above_ref
  116.9 2.8 %collective-permute-done.5.below_ref = f32[96,1536]{1,0:T(8,128)S(1)} collective-permute-done((f32[96,1536]{1,0:T(8,128)S(1)}, f32[96,1536]{1,0:T(8,128)S(1)}, u32[]{:S(2)}, u32[]{:S(2)}) %collective-permute-start.5) | collective-permute-done | bytes 589856 | tf_op jit(solution)/shard_map/ppermute | solution.py:351
  119.7 0.8 shard_map.170
  120.5 2.0 %collective-permute-start.6 = (f32[64,1536]{1,0:T(8,128)S(1)}, f32[64,1536]{1,0:T(8,128)S(1)}, u32[]{:S(2)}, u32[]{:S(2)}) collective-permute-start(f32[64,1536]{1,0:T(8,128)S(1)} %get-tuple-element.38), channel_id=1, source_target_pairs={{0,1},{1,2},{2,3},{3,4},{4,5},{5,6},{6,7},{7,8},{8,9},{9,10},{10,1... | collective-permute-start | bytes 1179656 | tf_op jit(solution)/shard_map/ppermute | solution.py:351
  122.5 4.6 %collective-permute-start.7 = (f32[64,1536]{1,0:T(8,128)S(1)}, f32[64,1536]{1,0:T(8,128)S(1)}, u32[]{:S(2)}, u32[]{:S(2)}) collective-permute-start(f32[64,1536]{1,0:T(8,128)S(1)} %get-tuple-element.39), channel_id=1, source_target_pairs={{0,15},{1,0},{2,1},{3,2},{4,3},{5,4},{6,5},{7,6},{8,7},{9,8},{10,9... | collective-permute-start | bytes 1179656 | tf_op jit(solution)/shard_map/ppermute | solution.py:351
  127.1 1.0 reduce_sum.19
  128.1 0.7 broadcast_in_dim.5
  128.8 6.8 %all-to-all-start.2 = ((bf16[16,48,128]{2,1,0:T(8,128)(2,1)}), bf16[16,48,128]{2,1,0:T(8,128)(2,1)S(1)}, u32[]{:S(2)}, u32[]{:S(2)}) async-start(bf16[16,48,128]{2,1,0:T(8,128)(2,1)} %broadcast_in_dim.5), calls=%async_computation.2 | async-start | bytes 393216 | tf_op jit(solution)/shard_map/all_to_all | solution.py:361
  135.6 1.4 copy-done.6
  137.0 2.1 %shard_map.171 = (bf16[128,1536]{1,0:T(8,128)(2,1)}, bf16[128,1536]{1,0:T(8,128)(2,1)}) custom-call(f32[128,64]{1,0:T(8,128)S(1)} %copy-done.10, f32[256,1536]{1,0:T(8,128)S(1)} %copy-done.6, f32[64,1536]{1,0:T(8,128)S(1)} %collective-permute-done.6.left_ref, f32[64,1536]{1,0:T(8,128)S(1)} %collective-permute-done.7.right_ref, ...), custom_call_target="tpu_custom_call" | custom-call | flops 50000000 | bytes 1000000 | tf_op jit(solution)/shard_map/pallas_call | solution.py:336
  139.2 6.6 %all-to-all-done.2.parts_ref = bf16[16,48,128]{2,1,0:T(8,128)(2,1)S(1)} async-done(((bf16[16,48,128]{2,1,0:T(8,128)(2,1)}), bf16[16,48,128]{2,1,0:T(8,128)(2,1)S(1)}, u32[]{:S(2)}, u32[]{:S(2)}) %all-to-all-start.2) | async-done | bytes 196640 | tf_op jit(solution)/shard_map/all_to_all | solution.py:361
  145.8 0.7 shard_map.172
  (31 shorter events, 0.1 us)
Async XLA Ops:
  0.6 99.3 %copy-start = (s32[16,16,9]{1,0,2:T(8,128)S(1)}, s32[16,16,9]{1,0,2:T(8,128)}, u32[]{:S(2)}) copy-start(s32[16,16,9]{1,0,2:T(8,128)} %param.21) | copy-start | bytes 27652
  0.6 72.7 %copy-start.3 = (bf16[2,8,8,1536]{3,2,1,0:T(8,128)(2,1)S(1)}, bf16[2,8,8,1536]{3,2,1,0:T(8,128)(2,1)}, u32[]{:S(2)}) copy-start(bf16[2,8,8,1536]{3,2,1,0:T(8,128)(2,1)} %param.14) | copy-start | bytes 1179652
  0.7 72.7 %copy-start.4 = (bf16[2,8,8,1536]{3,2,1,0:T(8,128)(2,1)S(1)}, bf16[2,8,8,1536]{3,2,1,0:T(8,128)(2,1)}, u32[]{:S(2)}) copy-start(bf16[2,8,8,1536]{3,2,1,0:T(8,128)(2,1)} %param.15) | copy-start | bytes 1179652
  0.7 72.7 %copy-start.13 = (bf16[2,32,128]{2,1,0:T(8,128)(2,1)S(1)}, bf16[2,32,128]{2,1,0:T(8,128)(2,1)}, u32[]{:S(2)}) copy-start(bf16[2,32,128]{2,1,0:T(8,128)(2,1)} %constant.31.clone.select_ref) | copy-start | bytes 49156
  5.7 92.5 %copy-start.11 = (bf16[2,48,192]{2,1,0:T(8,128)(2,1)S(1)}, bf16[2,48,192]{2,1,0:T(8,128)(2,1)}, u32[]{:S(2)}) copy-start(bf16[2,48,192]{2,1,0:T(8,128)(2,1)} %constant.32.clone.select_ref) | copy-start | bytes 110596
  65.3 35.0 %copy-start.1 = (bf16[2,8,8,1536]{3,2,1,0:T(8,128)(2,1)S(1)}, bf16[2,8,8,1536]{3,2,1,0:T(8,128)(2,1)}, u32[]{:S(2)}) copy-start(bf16[2,8,8,1536]{3,2,1,0:T(8,128)(2,1)} %param.13) | copy-start | bytes 1179652
  65.3 35.0 %copy-start.2 = (bf16[2,8,8,1536]{3,2,1,0:T(8,128)(2,1)S(1)}, bf16[2,8,8,1536]{3,2,1,0:T(8,128)(2,1)}, u32[]{:S(2)}) copy-start(bf16[2,8,8,1536]{3,2,1,0:T(8,128)(2,1)} %param.16) | copy-start | bytes 1179652
  65.4 35.0 %copy-start.7 = (bf16[32,1536]{1,0:T(8,128)(2,1)S(1)}, bf16[32,1536]{1,0:T(8,128)(2,1)}, u32[]{:S(2)}) copy-start(bf16[32,1536]{1,0:T(8,128)(2,1)} %text_key_ref.1) | copy-start | bytes 294916
  65.4 35.0 %copy-start.8 = (bf16[32,1536]{1,0:T(8,128)(2,1)S(1)}, bf16[32,1536]{1,0:T(8,128)(2,1)}, u32[]{:S(2)}) copy-start(bf16[32,1536]{1,0:T(8,128)(2,1)} %text_value_ref.1) | copy-start | bytes 294916
  65.4 35.0 %copy-start.9 = (f32[32,128]{1,0:T(8,128)S(1)}, f32[32,128]{1,0:T(8,128)}, u32[]{:S(2)}) copy-start(f32[32,128]{1,0:T(8,128)} %get-tuple-element.25.stats_ref) | copy-start | bytes 49156
  66.2 60.9 %all-to-all-start.1 = ((f32[16,48,128]{2,1,0:T(8,128)}), f32[16,48,128]{2,1,0:T(8,128)}, u32[]{:S(2)}, u32[]{:S(2)}) async-start(f32[16,48,128]{2,1,0:T(8,128)} %broadcast_in_dim.4), calls=%async_computation.1 | async-start | bytes 786432 | tf_op jit(solution)/shard_map/all_to_all | solution.py:361
  73.7 24.5 %collective-permute-start = (bf16[64,1536]{1,0:T(8,128)(2,1)S(1)}, bf16[64,1536]{1,0:T(8,128)(2,1)S(1)}, u32[]{:S(2)}, u32[]{:S(2)}) collective-permute-start(bf16[64,1536]{1,0:T(8,128)(2,1)S(1)} %get-tuple-element.26), channel_id=1, source_target_pairs={{0,1},{1,2},{2,3},{3,4},{4,5},{5,6},{6,7},{7,8},{8,9},{9,10},{10,1... | collective-permute-start | bytes 589832 | tf_op jit(solution)/shard_map/ppermute | solution.py:351
  76.8 21.4 %collective-permute-start.1 = (bf16[64,1536]{1,0:T(8,128)(2,1)S(1)}, bf16[64,1536]{1,0:T(8,128)(2,1)S(1)}, u32[]{:S(2)}, u32[]{:S(2)}) collective-permute-start(bf16[64,1536]{1,0:T(8,128)(2,1)S(1)} %get-tuple-element.27), channel_id=1, source_target_pairs={{0,15},{1,0},{2,1},{3,2},{4,3},{5,4},{6,5},{7,6},{8,7},{9,8},{10,9... | collective-permute-start | bytes 589832 | tf_op jit(solution)/shard_map/ppermute | solution.py:351
  99.5 5.9 %collective-permute-start.2 = (bf16[96,1536]{1,0:T(8,128)(2,1)}, bf16[96,1536]{1,0:T(8,128)(2,1)S(1)}, u32[]{:S(2)}, u32[]{:S(2)}) collective-permute-start(bf16[96,1536]{1,0:T(8,128)(2,1)} %get-tuple-element.28), channel_id=1, source_target_pairs={{0,16},{16,32},{32,48},{48,64},{64,80},{80,96},{96,112},{112,128},... | collective-permute-start | bytes 884744 | tf_op jit(solution)/shard_map/ppermute | solution.py:351
  99.5 6.4 %collective-permute-start.3 = (bf16[96,1536]{1,0:T(8,128)(2,1)S(1)}, bf16[96,1536]{1,0:T(8,128)(2,1)S(1)}, u32[]{:S(2)}, u32[]{:S(2)}) collective-permute-start(bf16[96,1536]{1,0:T(8,128)(2,1)S(1)} %get-tuple-element.29), channel_id=1, source_target_pairs={{0,240},{16,0},{32,16},{48,32},{64,48},{80,64},{96,80},{112,96},{1... | collective-permute-start | bytes 884744 | tf_op jit(solution)/shard_map/ppermute | solution.py:351
  104.2 1.2 copy-start.5
  105.9 13.8 %copy-start.12 = (f32[64,96]{1,0:T(8,128)S(1)}, f32[64,96]{1,0:T(8,128)}, u32[]{:S(2)}) copy-start(f32[64,96]{1,0:T(8,128)} %constant.33.clone.select_ref) | copy-start | bytes 73732
  109.3 7.6 %collective-permute-start.4 = (f32[96,1536]{1,0:T(8,128)S(1)}, f32[96,1536]{1,0:T(8,128)S(1)}, u32[]{:S(2)}, u32[]{:S(2)}) collective-permute-start(f32[96,1536]{1,0:T(8,128)S(1)} %get-tuple-element.36), channel_id=1, source_target_pairs={{0,16},{16,32},{32,48},{48,64},{64,80},{80,96},{96,112},{112,128},... | collective-permute-start | bytes 1769480 | tf_op jit(solution)/shard_map/ppermute | solution.py:351
  110.1 9.6 %collective-permute-start.5 = (f32[96,1536]{1,0:T(8,128)S(1)}, f32[96,1536]{1,0:T(8,128)S(1)}, u32[]{:S(2)}, u32[]{:S(2)}) collective-permute-start(f32[96,1536]{1,0:T(8,128)S(1)} %get-tuple-element.37), channel_id=1, source_target_pairs={{0,240},{16,0},{32,16},{48,32},{64,48},{80,64},{96,80},{112,96},{1... | collective-permute-start | bytes 1769480 | tf_op jit(solution)/shard_map/ppermute | solution.py:351
  115.9 19.7 %copy-start.10 = (f32[128,64]{1,0:T(8,128)S(1)}, f32[128,64]{1,0:T(8,128)}, u32[]{:S(2)}) copy-start(f32[128,64]{1,0:T(8,128)} %constant.34.clone.select_ref) | copy-start | bytes 98308
  120.5 15.1 %collective-permute-start.6 = (f32[64,1536]{1,0:T(8,128)S(1)}, f32[64,1536]{1,0:T(8,128)S(1)}, u32[]{:S(2)}, u32[]{:S(2)}) collective-permute-start(f32[64,1536]{1,0:T(8,128)S(1)} %get-tuple-element.38), channel_id=1, source_target_pairs={{0,1},{1,2},{2,3},{3,4},{4,5},{5,6},{6,7},{7,8},{8,9},{9,10},{10,1... | collective-permute-start | bytes 1179656 | tf_op jit(solution)/shard_map/ppermute | solution.py:351
  122.5 13.1 %collective-permute-start.7 = (f32[64,1536]{1,0:T(8,128)S(1)}, f32[64,1536]{1,0:T(8,128)S(1)}, u32[]{:S(2)}, u32[]{:S(2)}) collective-permute-start(f32[64,1536]{1,0:T(8,128)S(1)} %get-tuple-element.39), channel_id=1, source_target_pairs={{0,15},{1,0},{2,1},{3,2},{4,3},{5,4},{6,5},{7,6},{8,7},{9,8},{10,9... | collective-permute-start | bytes 1179656 | tf_op jit(solution)/shard_map/ppermute | solution.py:351
  128.8 17.0 %all-to-all-start.2 = ((bf16[16,48,128]{2,1,0:T(8,128)(2,1)}), bf16[16,48,128]{2,1,0:T(8,128)(2,1)S(1)}, u32[]{:S(2)}, u32[]{:S(2)}) async-start(bf16[16,48,128]{2,1,0:T(8,128)(2,1)} %broadcast_in_dim.5), calls=%async_computation.2 | async-start | bytes 393216 | tf_op jit(solution)/shard_map/all_to_all | solution.py:361
  135.6 1.4 copy-start.6

commit v5 on v4

--- a/solution.py
+++ b/solution.py
@@ -43,6 +43,36 @@
     return lax.dot_general(
         a, b, (((1,), (0,)), ((), ())), precision=lax.Precision.HIGHEST, preferred_element_type=F32
     )
+
+
+STEPS = 128.0
+MOST = 32000.0
+I16 = jnp.int16
+
+
+def scaled(x, level):
+    half = jnp.exp2(level * (0.5 / STEPS))
+    return (x * half) * half
+
+
+def coded(x):
+    most = jnp.maximum(jnp.max(jnp.abs(x), axis=0, keepdims=True), 2.0**-120)
+    level = jnp.ceil(jnp.log2(most) * STEPS)
+    code = jnp.floor(scaled(x, -level) * MOST + 0.5)
+    return code.astype(jnp.int32).astype(I16), level
+
+
+def levels_of(rows):
+    blank = jnp.zeros((8 - len(rows), rows[0].shape[1]), F32)
+    return jnp.concatenate([*rows, blank], axis=0).astype(jnp.int32).astype(I16)
+
+
+def wide(code):
+    return code.astype(jnp.int32).astype(F32)
+
+
+def decoded(code, level):
+    return scaled(wide(code) * (1.0 / MOST), level)
 
 
 def own_row(frame, row, col):
@@ -105,8 +135,18 @@
 
 
 def text_kernel(
-    ready, norm_ref, delta_ref, query_ref, out_grad_ref, key_ref, value_ref, grad_ref, stats_ref
-):
+    ready,
+    norm_ref,
+    delta_ref,
+    query_ref,
+    out_grad_ref,
+    key_ref,
+    value_ref,
+    grad_ref,
+    stats_ref,
+    levels_ref,
+):
+    levels_ref[...] = jnp.zeros(levels_ref.shape, F32)
     heads = lax.broadcasted_iota(jnp.int32, (16, HEADS), 1)
     identity = (heads == lax.broadcasted_iota(jnp.int32, (16, HEADS), 0)).astype(F32)
     stats = []
@@ -122,7 +162,9 @@
         stats.append(rows)
     norm, delta = stats
     text = key_ref.shape[0]
-    piece = grad_ref.shape[0] // 16
+    pieces = levels_ref.shape[0] // 8
+    sent = grad_ref.shape[0] // pieces
+    piece = sent - 8
     for h in range(HEADS):
         ready(h)
         cols = slice(h * HDIM, (h + 1) * HDIM)
@@ -134,8 +176,41 @@
         for part, grad in enumerate((nn(score_grad, q) * SCALE, nn(probs.astype(BF16), g))):
             for at in range(0, text, 16):
                 chip, within = divmod(h * text + at, piece)
-                to = (2 * chip + part) * piece + within
-                grad_ref[to : to + 16, :] = grad[at : at + 16]
+                to = 2 * chip + part
+                code, level = coded(grad[at : at + 16])
+                grad_ref[to * sent + within : to * sent + within + 16, :] = code
+                levels_ref[to * 8 + within // 16 : to * 8 + within // 16 + 1, :] = level
+    for to in range(pieces):
+        levels = levels_ref[to * 8 : (to + 1) * 8, :].astype(jnp.int32).astype(I16)
+        grad_ref[(to + 1) * sent - 8 : (to + 1) * sent, :] = levels
+
+
+def over_chips_kernel(parts_ref, out_ref):
+    count, sent, _ = parts_ref.shape
+    total = 0.0
+    for n in range(count):
+        levels = wide(parts_ref[n, sent - 8 :, :])
+        blocks = [
+            decoded(parts_ref[n, 16 * b : 16 * b + 16, :], levels[b : b + 1])
+            for b in range((sent - 8) // 16)
+        ]
+        total = total + jnp.concatenate(blocks, axis=0)
+    code, level = coded(total)
+    levels = levels_of([level])
+    for n in range(out_ref.shape[0]):
+        out_ref[n, : sent - 8, :] = code
+        out_ref[n, sent - 8 :, :] = levels
+
+
+def over_tiles_kernel(parts_ref, out_ref):
+    count, sent, _ = parts_ref.shape
+    total = 0.0
+    for n in range(count):
+        level = wide(parts_ref[n, sent - 8 :, :])[:1]
+        total = total + decoded(parts_ref[n, : sent - 8, :], level)
+    total = total.astype(BF16)
+    for n in range(out_ref.shape[0]):
+        out_ref[n] = total
 
 
 def backward(q, g, k, v, norm, delta, live):
@@ -204,6 +279,7 @@
         (top_grad_ref, bottom_grad_ref, query_grad_ref),
         jnp.concatenate(lives, axis=0),
         1.0,
+        True,
     )
 
 
@@ -226,10 +302,11 @@
         (left_grad_ref, right_grad_ref, query_grad_ref),
         lives,
         SCALE,
-    )
-
-
-def two_halves(given, made, live, scale):
+        False,
+    )
+
+
+def two_halves(given, made, live, scale, code):
     stats_ref, query_ref, out_grad_ref, first_ref, second_ref, part_ref = given
     first_grad_ref, second_grad_ref, query_grad_ref = made
     rows = first_ref.shape[0] // 2
@@ -246,21 +323,38 @@
         probs, score_grad = backward(q, g, k, v, norm, delta, live)
         query_grad = part_ref[:, cols] + tn(score_grad, k)
         query_grad_ref[:, cols] = (query_grad * scale).astype(query_grad_ref.dtype)
-        for at, grad in ((slice(0, rows), nn(score_grad, q) * SCALE), (slice(rows, 2 * rows), nn(probs, g))):
-            first_grad_ref[at, cols] = grad[:rows]
-            second_grad_ref[at, cols] = grad[rows:]
+        grads = (nn(score_grad, q) * SCALE, nn(probs, g))
+        for n, ref in enumerate((first_grad_ref, second_grad_ref)):
+            levels = []
+            for at, grad in ((slice(0, rows), grads[0]), (slice(rows, 2 * rows), grads[1])):
+                block = grad[n * rows : (n + 1) * rows]
+                if code:
+                    block, level = coded(block)
+                    levels.append(level)
+                ref[at, cols] = block
+            if code:
+                ref[2 * rows :, cols] = levels_of(levels)
+
+
+def received(ref, part, rows):
+    level = wide(ref[2 * rows :, :])[part : part + 1]
+    return decoded(ref[part * rows : (part + 1) * rows, :], level)
 
 
 def corners_kernel(
     select_ref, left_ref, right_ref, above_ref, below_ref, left_out_ref, right_out_ref
 ):
+    levels = ([], [])
     for part in range(2):
         side = slice(part * SIDE, (part + 1) * SIDE)
-        ends = slice(part * ENDS, (part + 1) * ENDS)
-        bands = jnp.concatenate([above_ref[ends, :], below_ref[ends, :]], axis=0)
-        more = exact(select_ref[...], bands)
-        left_out_ref[side, :] = left_ref[side, :] + more[:SIDE]
-        right_out_ref[side, :] = right_ref[side, :] + more[SIDE:]
+        bands = [received(ref, part, ENDS) for ref in (above_ref, below_ref)]
+        more = exact(select_ref[...], jnp.concatenate(bands, axis=0))
+        for n, (ref, out) in enumerate(((left_ref, left_out_ref), (right_ref, right_out_ref))):
+            code, level = coded(ref[side, :] + more[n * SIDE : (n + 1) * SIDE])
+            out[side, :] = code
+            levels[n].append(level)
+    left_out_ref[2 * SIDE :, :] = levels_of(levels[0])
+    right_out_ref[2 * SIDE :, :] = levels_of(levels[1])
 
 
 def sum_kernel(
@@ -268,19 +362,20 @@
 ):
     edge = HALO * TILE
     for part, out in enumerate((key_ref, value_ref)):
-        side = slice(part * SIDE, (part + 1) * SIDE)
-        rows = jnp.concatenate([left_ref[side, :], right_ref[side, :]], axis=0)
+        above, below = received(above_ref, part, ENDS), received(below_ref, part, ENDS)
+        sides = [received(ref, part, SIDE) for ref in (left_ref, right_ref)]
+        rows = jnp.concatenate(sides, axis=0)
         total = own_ref[part * OWN : (part + 1) * OWN, :] + exact(select_ref[...], rows)
         for frame in range(FRAMES):
-            at = part * ENDS + frame * BAND
+            at = frame * BAND
             top = frame * TILE * TILE
             bottom = top + TILE * TILE - edge
             end = top + TILE * TILE
             out[top : top + edge, :] = (
-                total[top : top + edge] + above_ref[at : at + edge, :]
+                total[top : top + edge] + above[at : at + edge]
             ).astype(BF16)
             out[top + edge : bottom, :] = total[top + edge : bottom].astype(BF16)
-            out[bottom:end, :] = (total[bottom:end] + below_ref[at : at + edge, :]).astype(BF16)
+            out[bottom:end, :] = (total[bottom:end] + below[at : at + edge]).astype(BF16)
 
 
 def words_kernel(parts_ref, key_ref, value_ref):
@@ -294,15 +389,15 @@
                 out[at : at + 16, h * HDIM : (h + 1) * HDIM] = piece
 
 
-def call(kernel, outs, ins, us=1.0, smem=0, fetch=False):
+def call(kernel, outs, ins, us=1.0, smem=0, fetch=False, scratch=()):
     groups = HEADS // GROUP
     step = GROUP * HDIM
 
     def body(*refs):
         n = len(ins)
         outputs = refs[n : n + len(outs)]
-        buffers = refs[n + len(outs) : -1]
-        semaphores = refs[-1]
+        buffers = refs[n + len(outs) : 2 * n + len(outs)]
+        semaphores, *rest = refs[2 * n + len(outs) :]
         small, wide = [], [[] for _ in range(groups)]
         for i, (far, near) in enumerate(zip(refs[:n], buffers)):
             if ins[i].ndim == 2 and ins[i].shape[1] == groups * step:
@@ -323,16 +418,16 @@
                 for copy in wide[h // GROUP]:
                     copy.wait()
 
-        kernel(ready, *buffers, *outputs)
+        kernel(ready, *buffers, *outputs, *rest)
 
     here = pl.BlockSpec(memory_space=pltpu.VMEM)
     scalars = pl.BlockSpec(memory_space=pltpu.SMEM)
     if not fetch:
-        function, specs, scratch, limit = kernel, [scalars] * smem + [here] * (len(ins) - smem), [], 16
+        function, specs, scratch, limit = kernel, [scalars] * smem + [here] * (len(ins) - smem), [*scratch], 16
     else:
         function, specs, limit = body, [pl.BlockSpec(memory_space=pltpu.HBM)] * len(ins), 56
-        scratch = [pltpu.VMEM(a.shape, a.dtype) for a in ins]
-        scratch.append(pltpu.SemaphoreType.DMA((len(ins), groups)))
+        buffers = [pltpu.VMEM(a.shape, a.dtype) for a in ins]
+        scratch = [*buffers, pltpu.SemaphoreType.DMA((len(ins), groups)), *scratch]
     return pl.pallas_call(
         function,
         out_shape=[jax.ShapeDtypeStruct(shape, dtype) for shape, dtype in outs],
@@ -355,10 +450,8 @@
     return rows.transpose(1, 2, 3, 0).reshape(OWN, HEADS)
 
 
-def to_all(value, axis):
-    count = lax.axis_size(axis)
-    everyone = jnp.broadcast_to(value[None], (count, *value.shape))
-    return lax.all_to_all(everyone, axis, 0, 0, tiled=True)
+def exchanged(pieces, axis):
+    return lax.all_to_all(pieces, axis, 0, 0, tiled=True)
 
 
 def local(
@@ -376,21 +469,25 @@
         window_table, (lax.axis_index(HA), lax.axis_index("wa"), anchor), (1, 1, 9)
     ).reshape(9)
 
+    count = lax.axis_size(HA)
+    piece = 2 * HEADS * text // count
+    sent = piece + 8
     words, stats = call(
         text_kernel,
-        [((2 * HEADS * text, HDIM), F32), ((32, HDIM), F32)],
+        [((count * sent, HDIM), I16), ((32, HDIM), F32)],
         [by_query(log_norm), by_query(delta_rows), q, g, text_keys, text_values],
         us=3,
         fetch=True,
-    )
-    count = lax.axis_size(HA)
-    words = lax.all_to_all(words.reshape(count, -1, HDIM), HA, 0, 0, tiled=True)
-    piece = words.sum(axis=0)
-    pieces = to_all(piece, "wa")
-    piece = pieces.sum(axis=0).astype(BF16)
-    pieces = to_all(piece, HA)
+        scratch=[pltpu.VMEM((count * 8, HDIM), F32)],
+    )
+    words = exchanged(words.reshape(count, sent, HDIM), HA)
+    tiles = lax.axis_size("wa")
+    (words,) = call(over_chips_kernel, [((tiles, sent, HDIM), I16)], [words])
+    words = exchanged(words, "wa")
+    (words,) = call(over_tiles_kernel, [((count, piece, HDIM), BF16)], [words])
+    words = exchanged(words, HA)
     text_key_grad, text_value_grad = call(
-        words_kernel, [((text, width), BF16)] * 2, [pieces]
+        words_kernel, [((text, width), BF16)] * 2, [words]
     )
 
     left, right = call(
@@ -414,7 +511,7 @@
     from_above = shifted(bottom, HA, 1)
     top_grad, bottom_grad, part = call(
         band_kernel,
-        [((2 * ENDS, width), F32)] * 2 + [((OWN, width), F32)],
+        [((2 * ENDS + 8, width), I16)] * 2 + [((OWN, width), F32)],
         [live, stats, q, g, from_above, from_below, part],
         us=2,
         smem=1,
@@ -431,7 +528,7 @@
     back = np.concatenate([BANDS[0].T, BANDS[1].T], axis=1)
     left_grad, right_grad = call(
         corners_kernel,
-        [((2 * SIDE, width), F32)] * 2,
+        [((2 * SIDE + 8, width), I16)] * 2,
         [jnp.asarray(back[OWN:], F32), left_grad, right_grad, above, below],
     )
     after = shifted(left_grad, "wa", -1)

time: 147 us -> 136 us (0.925)
  waiting for transfers between devices: 28.8 us -> 14.6 us
  local copies, waits for them, and re-layouts: 4.47 us -> 8.64 us
  blocking collectives: 59.6 us -> 56.1 us
  Pallas kernels: 21.6 us -> 24.5 us
    ppermute x8, waiting for transfers between devices: 22.2 us -> 14.6 us  [shifted(): lax.ppermute(value, axis, [(i, (i + steps) % count) for i in range(count)])]
    all_to_all x2, waiting for transfers between devices: 6.62 us -> 0.01 us  [exchanged(): return lax.all_to_all(pieces, axis, 0, 0, tiled=True)]
    unnamed x28 -> x42, local copies, waits for them, and re-layouts: 2.65 us -> 8.3 us
    all_to_all x1, blocking collectives: 59.6 us -> 56.1 us  [exchanged(): return lax.all_to_all(pieces, axis, 0, 0, tiled=True)]
    pallas_call x9 -> x11, Pallas kernels: 21.6 us -> 24.5 us  [call(): pl.pallas_call(function, out_shape=[jax.ShapeDtypeStruct(shape, dtype) fo...]
    broadcast_in_dim x2 -> x0, local copies, waits for them, and re-layouts: 1.48 us -> none  [to_all(): everyone = jnp.broadcast_to(value[None], (count, *value.shape))]
  transfers between devices with their start and end apart: 10 -> 10, of which waited for: 5 -> 4; matrix products, arithmetic and copies ran while one was open for 1% -> 0% of each run, Pallas kernels for 11% -> 13%
where the time goes in v5:
time: 136 us; the launch traced here: 135 us
  blocking collectives  56.1 us (41%)
  starting transfers between devices  29.9 us (22%)
  Pallas kernels  24.5 us (18%)
  waiting for transfers between devices  14.6 us (11%)
  local copies, waits for them, and re-layouts  8.64 us (6%)
    all_to_all x1, blocking collectives, exchanged(): return lax.all_to_all(pieces, axis, 0, 0, tiled=True)  56.1 us
    pallas_call x11, Pallas kernels, call(): pl.pallas_call(function, out_shape=[jax.ShapeDtypeStruct(shape, dtype) fo...  24.5 us
    ppermute x8, starting transfers between devices, shifted(): lax.ppermute(value, axis, [(i, (i + steps) % count) for i in range(count)])  16.6 us
    ppermute x8, waiting for transfers between devices, shifted(): lax.ppermute(value, axis, [(i, (i + steps) % count) for i in range(count)])  14.6 us
    all_to_all x2, starting transfers between devices, exchanged(): return lax.all_to_all(pieces, axis, 0, 0, tiled=True)  13.3 us
    unnamed x42, local copies, waits for them, and re-layouts  8.3 us
  transfers between devices with their start and end apart: 10, of which 4 were waited for; matrix products, arithmetic and copies ran while one was open for 0% of the time, Pallas kernels for 13%

profile of v5, /device:TPU:65, one launch (start us, length us, event | category | flops | bytes accessed | tf_op | source)
XLA Modules:
  0.0 134.6 jit_solution(2383932316832553123)
XLA Ops:
  0.7 5.1 %shard_map.164 = (s16[896,128]{1,0:T(8,128)(2,1)}, f32[32,128]{1,0:T(8,128)}) custom-call(f32[128,12]{1,0:T(8,128)} %bitcast.29, f32[128,12]{1,0:T(8,128)} %bitcast.30, bf16[128,1536]{1,0:T(8,128)(2,1)} %bitcast.14, bf16[128,1536]{1,0:T(8,128)(2,1)} %bitcast.18, bf16[32,1536]{1,0:T(8,128)(2,1)} %text_key_ref.1, bf16[32,1536]{1,0:T(8,128)(2,1)} %text_value_ref.1), custom_call_target="tpu_custom_call" | custom-call | flops 150000000 | bytes 1000000 | tf_op jit(solution)/shard_map/pallas_call | solution.py:431
  5.8 56.1 %all_to_all.15.parts_ref = s16[16,56,128]{2,1,0:T(8,128)(2,1)S(1)} all-to-all(s16[16,56,128]{2,1,0:T(8,128)(2,1)} %bitcast.28), channel_id=1, replica_groups=mesh['group'=2,'ha_0'=8,'ha_1'=2,'wa'=16] {'ha_0','ha_1'}, dimensions={0} | all-to-all | bytes 458752 | tf_op jit(solution)/shard_map/all_to_all | solution.py:454
  61.9 0.8 shard_map.172
  62.7 7.0 %all-to-all-start.1 = ((s16[16,56,128]{2,1,0:T(8,128)(2,1)}), s16[16,56,128]{2,1,0:T(8,128)(2,1)S(1)}, u32[]{:S(2)}, u32[]{:S(2)}) async-start(s16[16,56,128]{2,1,0:T(8,128)(2,1)} %shard_map.172), calls=%async_computation.1 | async-start | bytes 458752 | tf_op jit(solution)/shard_map/all_to_all | solution.py:454
  70.1 3.1 %collective-permute-start = (bf16[64,1536]{1,0:T(8,128)(2,1)S(1)}, bf16[64,1536]{1,0:T(8,128)(2,1)S(1)}, u32[]{:S(2)}, u32[]{:S(2)}) collective-permute-start(bf16[64,1536]{1,0:T(8,128)(2,1)S(1)} %get-tuple-element.26), channel_id=1, source_target_pairs={{0,1},{1,2},{2,3},{3,4},{4,5},{5,6},{6,7},{7,8},{8,9},{9,10},{10,1... | collective-permute-start | bytes 589832 | tf_op jit(solution)/shard_map/ppermute | solution.py:446
  73.2 3.5 %collective-permute-start.1 = (bf16[64,1536]{1,0:T(8,128)(2,1)S(1)}, bf16[64,1536]{1,0:T(8,128)(2,1)S(1)}, u32[]{:S(2)}, u32[]{:S(2)}) collective-permute-start(bf16[64,1536]{1,0:T(8,128)(2,1)S(1)} %get-tuple-element.27), channel_id=1, source_target_pairs={{0,15},{1,0},{2,1},{3,2},{4,3},{5,4},{6,5},{7,6},{8,7},{9,8},{10,9... | collective-permute-start | bytes 589832 | tf_op jit(solution)/shard_map/ppermute | solution.py:446
  76.7 10.4 %collective-permute-done.left_ref = bf16[64,1536]{1,0:T(8,128)(2,1)S(1)} collective-permute-done((bf16[64,1536]{1,0:T(8,128)(2,1)S(1)}, bf16[64,1536]{1,0:T(8,128)(2,1)S(1)}, u32[]{:S(2)}, u32[]{:S(2)}) %collective-permute-start) | collective-permute-done | bytes 196640 | tf_op jit(solution)/shard_map/ppermute | solution.py:446
  87.1 1.2 shard_map.166
  88.3 0.7 copy-done.5
  89.4 0.5 collective-permute-start.3
  90.3 0.9 copy-done.13
  91.2 0.7 copy-done.14
  91.9 3.8 %shard_map.167 = (f32[128,1536]{1,0:T(8,128)S(1)}, f32[256,1536]{1,0:T(8,128)S(1)}) custom-call(s32[9]{0:T(128)S(1)} %dynamic-slice_reduce_fusion.live_ref, f32[32,128]{1,0:T(8,128)S(1)} %copy-done.14, bf16[128,1536]{1,0:T(8,128)(2,1)S(1)} %bitcast.15, bf16[128,1536]{1,0:T(8,128)(2,1)S(1)} %bitcast.19, bf16[128,1536]{1,0:T(8,128)(2,1)S(1)} %bitcast.24, ...), custom_call_target="tpu_custom_call" | custom-call | flops 150000000 | bytes 1000000 | tf_op jit(solution)/shard_map/pallas_call | solution.py:431
  96.1 0.7 copy-done.15
  96.9 4.9 %shard_map.168 = (s16[104,1536]{1,0:T(8,128)(2,1)}, s16[104,1536]{1,0:T(8,128)(2,1)}, f32[128,1536]{1,0:T(8,128)S(1)}) custom-call(s32[9]{0:T(128)S(1)} %dynamic-slice_reduce_fusion.live_ref, f32[32,128]{1,0:T(8,128)S(1)} %copy-done.15, bf16[128,1536]{1,0:T(8,128)(2,1)S(1)} %bitcast.16, bf16[128,1536]{1,0:T(8,128)(2,1)S(1)} %bitcast.20, ...), custom_call_target="tpu_custom_call" | custom-call | flops 100000000 | bytes 1000000 | tf_op jit(solution)/shard_map/pallas_call | solution.py:431
  101.7 0.9 copy-done.9
  102.6 0.8 collective-permute-start.4
  103.4 1.8 %collective-permute-start.5 = (s16[104,1536]{1,0:T(8,128)(2,1)}, s16[104,1536]{1,0:T(8,128)(2,1)S(1)}, u32[]{:S(2)}, u32[]{:S(2)}) collective-permute-start(s16[104,1536]{1,0:T(8,128)(2,1)} %get-tuple-element.37), channel_id=1, source_target_pairs={{0,240},{16,0},{32,16},{48,32},{64,48},{80,64},{96,80},{112,96},{1... | collective-permute-start | bytes 958472 | tf_op jit(solution)/shard_map/ppermute | solution.py:446
  105.3 0.7 copy-done.11
  106.0 6.3 %all-to-all-start.2 = ((bf16[16,48,128]{2,1,0:T(8,128)(2,1)}), bf16[16,48,128]{2,1,0:T(8,128)(2,1)S(1)}, u32[]{:S(2)}, u32[]{:S(2)}) async-start(bf16[16,48,128]{2,1,0:T(8,128)(2,1)} %copy-done.11), calls=%async_computation.2 | async-start | bytes 393216 | tf_op jit(solution)/shard_map/all_to_all | solution.py:454
  112.2 0.9 copy-done.6
  113.2 0.9 copy-done.8
  114.1 1.1 copy-done.10
  115.2 0.7 copy-done.16
  115.9 4.2 %shard_map.169 = (f32[64,1536]{1,0:T(8,128)S(1)}, f32[64,1536]{1,0:T(8,128)S(1)}, bf16[128,1536]{1,0:T(8,128)(2,1)}) custom-call(s32[9]{0:T(128)S(1)} %dynamic-slice_reduce_fusion.live_ref, f32[32,128]{1,0:T(8,128)S(1)} %copy-done.16, bf16[128,1536]{1,0:T(8,128)(2,1)S(1)} %bitcast.17, bf16[128,1536]{1,0:T(8,128)(2,1)S(1)} %bitcast.21, ...), custom_call_target="tpu_custom_call" | custom-call | flops 100000000 | bytes 1000000 | tf_op jit(solution)/shard_map/pallas_call | solution.py:431
  120.1 1.1 shard_map.170
  121.2 2.0 %collective-permute-start.6 = (s16[72,1536]{1,0:T(8,128)(2,1)S(1)}, s16[72,1536]{1,0:T(8,128)(2,1)S(1)}, u32[]{:S(2)}, u32[]{:S(2)}) collective-permute-start(s16[72,1536]{1,0:T(8,128)(2,1)S(1)} %get-tuple-element.38), channel_id=1, source_target_pairs={{0,1},{1,2},{2,3},{3,4},{4,5},{5,6},{6,7},{7,8},{8,9},{9,10},{10,1... | collective-permute-start | bytes 663560 | tf_op jit(solution)/shard_map/ppermute | solution.py:446
  123.2 4.6 %collective-permute-start.7 = (s16[72,1536]{1,0:T(8,128)(2,1)S(1)}, s16[72,1536]{1,0:T(8,128)(2,1)S(1)}, u32[]{:S(2)}, u32[]{:S(2)}) collective-permute-start(s16[72,1536]{1,0:T(8,128)(2,1)S(1)} %get-tuple-element.39), channel_id=1, source_target_pairs={{0,15},{1,0},{2,1},{3,2},{4,3},{5,4},{6,5},{7,6},{8,7},{9,8},{10,9... | collective-permute-start | bytes 663560 | tf_op jit(solution)/shard_map/ppermute | solution.py:446
  127.8 2.9 %collective-permute-done.6.left_ref = s16[72,1536]{1,0:T(8,128)(2,1)S(1)} collective-permute-done((s16[72,1536]{1,0:T(8,128)(2,1)S(1)}, s16[72,1536]{1,0:T(8,128)(2,1)S(1)}, u32[]{:S(2)}, u32[]{:S(2)}) %collective-permute-start.6) | collective-permute-done | bytes 221216 | tf_op jit(solution)/shard_map/ppermute | solution.py:446
  130.7 0.9 collective-permute-done.7.right_ref
  131.7 2.2 %shard_map.171 = (bf16[128,1536]{1,0:T(8,128)(2,1)}, bf16[128,1536]{1,0:T(8,128)(2,1)}) custom-call(f32[128,64]{1,0:T(8,128)S(1)} %copy-done.17, f32[256,1536]{1,0:T(8,128)S(1)} %get-tuple-element.33.own_ref, s16[72,1536]{1,0:T(8,128)(2,1)S(1)} %collective-permute-done.6.left_ref, s16[72,1536]{1,0:T(8,128)(2,1)S(1)} %collective-permute-done.7.right_ref, ...), custom_call_target="tpu_custom_call" | custom-call | flops 50000000 | bytes 1000000 | tf_op jit(solution)/shard_map/pallas_call | solution.py:431
  133.8 0.7 shard_map.174
  (43 shorter events, 1.6 us)
Async XLA Ops:
  0.6 89.3 %copy-start = (s32[16,16,9]{1,0,2:T(8,128)S(1)}, s32[16,16,9]{1,0,2:T(8,128)}, u32[]{:S(2)}) copy-start(s32[16,16,9]{1,0,2:T(8,128)} %param.21) | copy-start | bytes 27652
  0.6 69.1 %copy-start.20 = (bf16[2,32,128]{2,1,0:T(8,128)(2,1)S(1)}, bf16[2,32,128]{2,1,0:T(8,128)(2,1)}, u32[]{:S(2)}) copy-start(bf16[2,32,128]{2,1,0:T(8,128)(2,1)} %constant.29.clone.select_ref) | copy-start | bytes 49156
  0.7 69.1 %copy-start.4 = (bf16[2,8,8,1536]{3,2,1,0:T(8,128)(2,1)S(1)}, bf16[2,8,8,1536]{3,2,1,0:T(8,128)(2,1)}, u32[]{:S(2)}) copy-start(bf16[2,8,8,1536]{3,2,1,0:T(8,128)(2,1)} %param.15) | copy-start | bytes 1179652
  0.7 69.1 %copy-start.3 = (bf16[2,8,8,1536]{3,2,1,0:T(8,128)(2,1)S(1)}, bf16[2,8,8,1536]{3,2,1,0:T(8,128)(2,1)}, u32[]{:S(2)}) copy-start(bf16[2,8,8,1536]{3,2,1,0:T(8,128)(2,1)} %param.14) | copy-start | bytes 1179652
  0.7 86.4 %copy-start.18 = (bf16[2,48,192]{2,1,0:T(8,128)(2,1)S(1)}, bf16[2,48,192]{2,1,0:T(8,128)(2,1)}, u32[]{:S(2)}) copy-start(bf16[2,48,192]{2,1,0:T(8,128)(2,1)} %constant.30.clone.select_ref) | copy-start | bytes 110596
  61.9 28.4 %copy-start.1 = (bf16[2,8,8,1536]{3,2,1,0:T(8,128)(2,1)S(1)}, bf16[2,8,8,1536]{3,2,1,0:T(8,128)(2,1)}, u32[]{:S(2)}) copy-start(bf16[2,8,8,1536]{3,2,1,0:T(8,128)(2,1)} %param.13) | copy-start | bytes 1179652
  61.9 28.4 %copy-start.2 = (bf16[2,8,8,1536]{3,2,1,0:T(8,128)(2,1)S(1)}, bf16[2,8,8,1536]{3,2,1,0:T(8,128)(2,1)}, u32[]{:S(2)}) copy-start(bf16[2,8,8,1536]{3,2,1,0:T(8,128)(2,1)} %param.16) | copy-start | bytes 1179652
  61.9 28.4 %copy-start.12 = (bf16[32,1536]{1,0:T(8,128)(2,1)S(1)}, bf16[32,1536]{1,0:T(8,128)(2,1)}, u32[]{:S(2)}) copy-start(bf16[32,1536]{1,0:T(8,128)(2,1)} %text_key_ref.1) | copy-start | bytes 294916
  62.7 42.4 %all-to-all-start.1 = ((s16[16,56,128]{2,1,0:T(8,128)(2,1)}), s16[16,56,128]{2,1,0:T(8,128)(2,1)S(1)}, u32[]{:S(2)}, u32[]{:S(2)}) async-start(s16[16,56,128]{2,1,0:T(8,128)(2,1)} %shard_map.172), calls=%async_computation.1 | async-start | bytes 458752 | tf_op jit(solution)/shard_map/all_to_all | solution.py:454
  70.1 16.9 %collective-permute-start = (bf16[64,1536]{1,0:T(8,128)(2,1)S(1)}, bf16[64,1536]{1,0:T(8,128)(2,1)S(1)}, u32[]{:S(2)}, u32[]{:S(2)}) collective-permute-start(bf16[64,1536]{1,0:T(8,128)(2,1)S(1)} %get-tuple-element.26), channel_id=1, source_target_pairs={{0,1},{1,2},{2,3},{3,4},{4,5},{5,6},{6,7},{7,8},{8,9},{9,10},{10,1... | collective-permute-start | bytes 589832 | tf_op jit(solution)/shard_map/ppermute | solution.py:446
  73.2 13.8 %collective-permute-start.1 = (bf16[64,1536]{1,0:T(8,128)(2,1)S(1)}, bf16[64,1536]{1,0:T(8,128)(2,1)S(1)}, u32[]{:S(2)}, u32[]{:S(2)}) collective-permute-start(bf16[64,1536]{1,0:T(8,128)(2,1)S(1)} %get-tuple-element.27), channel_id=1, source_target_pairs={{0,15},{1,0},{2,1},{3,2},{4,3},{5,4},{6,5},{7,6},{8,7},{9,8},{10,9... | collective-permute-start | bytes 589832 | tf_op jit(solution)/shard_map/ppermute | solution.py:446
  87.1 1.3 copy-start.7
  88.3 0.7 copy-start.5
  89.0 6.7 %collective-permute-start.2 = (bf16[96,1536]{1,0:T(8,128)(2,1)}, bf16[96,1536]{1,0:T(8,128)(2,1)}, u32[]{:S(2)}, u32[]{:S(2)}) collective-permute-start(bf16[96,1536]{1,0:T(8,128)(2,1)} %get-tuple-element.28), channel_id=1, source_target_pairs={{0,16},{16,32},{32,48},{48,64},{64,80},{80,96},{96,112},{112,128},... | collective-permute-start | bytes 884744 | tf_op jit(solution)/shard_map/ppermute | solution.py:446
  89.4 6.8 %collective-permute-start.3 = (bf16[96,1536]{1,0:T(8,128)(2,1)}, bf16[96,1536]{1,0:T(8,128)(2,1)}, u32[]{:S(2)}, u32[]{:S(2)}) collective-permute-start(bf16[96,1536]{1,0:T(8,128)(2,1)} %get-tuple-element.29), channel_id=1, source_target_pairs={{0,240},{16,0},{32,16},{48,32},{64,48},{80,64},{96,80},{112,96},{1... | collective-permute-start | bytes 884744 | tf_op jit(solution)/shard_map/ppermute | solution.py:446
  90.3 0.9 copy-start.13
  91.2 0.7 copy-start.14
  96.1 0.7 copy-start.15
  101.7 0.9 copy-start.9
  102.6 17.5 %copy-start.19 = (f32[64,96]{1,0:T(8,128)S(1)}, f32[64,96]{1,0:T(8,128)}, u32[]{:S(2)}) copy-start(f32[64,96]{1,0:T(8,128)} %constant.31.clone.select_ref) | copy-start | bytes 73732
  102.6 17.5 %collective-permute-start.4 = (s16[104,1536]{1,0:T(8,128)(2,1)}, s16[104,1536]{1,0:T(8,128)(2,1)S(1)}, u32[]{:S(2)}, u32[]{:S(2)}) collective-permute-start(s16[104,1536]{1,0:T(8,128)(2,1)} %get-tuple-element.36), channel_id=1, source_target_pairs={{0,16},{16,32},{32,48},{48,64},{64,80},{80,96},{96,112},{112,128},... | collective-permute-start | bytes 958472 | tf_op jit(solution)/shard_map/ppermute | solution.py:446
  103.4 16.7 %collective-permute-start.5 = (s16[104,1536]{1,0:T(8,128)(2,1)}, s16[104,1536]{1,0:T(8,128)(2,1)S(1)}, u32[]{:S(2)}, u32[]{:S(2)}) collective-permute-start(s16[104,1536]{1,0:T(8,128)(2,1)} %get-tuple-element.37), channel_id=1, source_target_pairs={{0,240},{16,0},{32,16},{48,32},{64,48},{80,64},{96,80},{112,96},{1... | collective-permute-start | bytes 958472 | tf_op jit(solution)/shard_map/ppermute | solution.py:446
  105.3 0.7 copy-start.11
  106.0 27.9 %all-to-all-start.2 = ((bf16[16,48,128]{2,1,0:T(8,128)(2,1)}), bf16[16,48,128]{2,1,0:T(8,128)(2,1)S(1)}, u32[]{:S(2)}, u32[]{:S(2)}) async-start(bf16[16,48,128]{2,1,0:T(8,128)(2,1)} %copy-done.11), calls=%async_computation.2 | async-start | bytes 393216 | tf_op jit(solution)/shard_map/all_to_all | solution.py:454
  112.2 0.9 copy-start.6
  113.2 0.9 copy-start.8
  114.1 1.1 copy-start.10
  115.2 0.7 copy-start.16
  115.9 15.7 %copy-start.17 = (f32[128,64]{1,0:T(8,128)S(1)}, f32[128,64]{1,0:T(8,128)}, u32[]{:S(2)}) copy-start(f32[128,64]{1,0:T(8,128)} %constant.32.clone.select_ref) | copy-start | bytes 98308
  121.2 9.5 %collective-permute-start.6 = (s16[72,1536]{1,0:T(8,128)(2,1)S(1)}, s16[72,1536]{1,0:T(8,128)(2,1)S(1)}, u32[]{:S(2)}, u32[]{:S(2)}) collective-permute-start(s16[72,1536]{1,0:T(8,128)(2,1)S(1)} %get-tuple-element.38), channel_id=1, source_target_pairs={{0,1},{1,2},{2,3},{3,4},{4,5},{5,6},{6,7},{7,8},{8,9},{9,10},{10,1... | collective-permute-start | bytes 663560 | tf_op jit(solution)/shard_map/ppermute | solution.py:446
  123.2 8.4 %collective-permute-start.7 = (s16[72,1536]{1,0:T(8,128)(2,1)S(1)}, s16[72,1536]{1,0:T(8,128)(2,1)S(1)}, u32[]{:S(2)}, u32[]{:S(2)}) collective-permute-start(s16[72,1536]{1,0:T(8,128)(2,1)S(1)} %get-tuple-element.39), channel_id=1, source_target_pairs={{0,15},{1,0},{2,1},{3,2},{4,3},{5,4},{6,5},{7,6},{8,7},{9,8},{10,9... | collective-permute-start | bytes 663560 | tf_op jit(solution)/shard_map/ppermute | solution.py:446

commit v6 on v5

--- a/solution.py
+++ b/solution.py
@@ -39,10 +39,10 @@
     return lax.dot_general(a, b, (((0,), (0,)), ((), ())), preferred_element_type=F32)
 
 
-def exact(a, b):
-    return lax.dot_general(
-        a, b, (((1,), (0,)), ((), ())), precision=lax.Precision.HIGHEST, preferred_element_type=F32
-    )
+def picked(select, rows):
+    high = rows.astype(BF16)
+    low = (rows - high.astype(F32)).astype(BF16)
+    return nn(select, high) + nn(select, low)
 
 
 STEPS = 128.0
@@ -165,21 +165,23 @@
     pieces = levels_ref.shape[0] // 8
     sent = grad_ref.shape[0] // pieces
     piece = sent - 8
-    for h in range(HEADS):
+
+    def load(h):
         ready(h)
-        cols = slice(h * HDIM, (h + 1) * HDIM)
-        q = query_ref[:, cols]
-        g = out_grad_ref[:, cols]
-        probs = jnp.exp(nt(key_ref[:, cols], q) * SCALE - norm[h : h + 1])
-        prob_grad = nt(value_ref[:, cols], g)
-        score_grad = (probs * (prob_grad - delta[h : h + 1])).astype(BF16)
-        for part, grad in enumerate((nn(score_grad, q) * SCALE, nn(probs.astype(BF16), g))):
+        cols = columns(h)
+        q, g, k, v = (r[:, cols] for r in (query_ref, out_grad_ref, key_ref, value_ref))
+        return q, g, k, v, norm[h : h + 1], delta[h : h + 1]
+
+    def store(h, q, g, k, probs, score_grad):
+        for part, grad in enumerate((nn(score_grad, q) * SCALE, nn(probs, g))):
             for at in range(0, text, 16):
                 chip, within = divmod(h * text + at, piece)
                 to = 2 * chip + part
                 code, level = coded(grad[at : at + 16])
                 grad_ref[to * sent + within : to * sent + within + 16, :] = code
                 levels_ref[to * 8 + within // 16 : to * 8 + within // 16 + 1, :] = level
+
+    backward(load, store, None)
     for to in range(pieces):
         levels = levels_ref[to * 8 : (to + 1) * 8, :].astype(jnp.int32).astype(I16)
         grad_ref[(to + 1) * sent - 8 : (to + 1) * sent, :] = levels
@@ -213,12 +215,27 @@
         out_ref[n] = total
 
 
-def backward(q, g, k, v, norm, delta, live):
-    probs = jnp.exp(nt(k, q) * SCALE - norm)
-    if live is not None:
-        probs = probs * live
-    score_grad = (probs * (nt(v, g) - delta)).astype(BF16)
-    return probs.astype(BF16), score_grad
+BLOCK = 12
+
+
+def backward(load, store, live):
+    for first in range(0, HEADS, BLOCK):
+        heads = range(first, first + BLOCK)
+        given = [load(h) for h in heads]
+        scores = [nt(k, q) for q, _, k, _, _, _ in given]
+        prob_grads = [nt(v, g) for _, g, _, v, _, _ in given]
+        made = []
+        for (_, _, _, _, norm, delta), score, prob_grad in zip(given, scores, prob_grads):
+            probs = jnp.exp(score * SCALE - norm)
+            if live is not None:
+                probs = probs * live
+            made.append((probs.astype(BF16), (probs * (prob_grad - delta)).astype(BF16)))
+        for h, (q, g, k, _, _, _), (probs, score_grad) in zip(heads, given, made):
+            store(h, q, g, k, probs, score_grad)
+
+
+def columns(h):
+    return slice(h * HDIM, (h + 1) * HDIM)
 
 
 def own_kernel(
@@ -230,24 +247,29 @@
     values_ref,
     text_key_ref,
     text_value_ref,
+    part_ref,
     query_grad_ref,
     own_ref,
 ):
     text = text_key_ref.shape[0]
     rows = lax.broadcasted_iota(jnp.int32, (OWN + text, HDIM), 0)
     live = jnp.where(rows < OWN, live_ref[4].astype(F32), 1.0)
-    for h in range(HEADS):
-        cols = slice(h * HDIM, (h + 1) * HDIM)
-        q = query_ref[:, cols]
-        g = out_grad_ref[:, cols]
+
+    def load(h):
+        cols = columns(h)
         k = jnp.concatenate([keys_ref[:, cols], text_key_ref[:, cols]], axis=0)
         v = jnp.concatenate([values_ref[:, cols], text_value_ref[:, cols]], axis=0)
-        norm = stats_ref[h : h + 1, :]
-        delta = stats_ref[16 + h : 17 + h, :]
-        probs, score_grad = backward(q, g, k, v, norm, delta, live)
-        query_grad_ref[:, cols] = tn(score_grad, k)
+        norm, delta = stats_ref[h : h + 1, :], stats_ref[16 + h : 17 + h, :]
+        return query_ref[:, cols], out_grad_ref[:, cols], k, v, norm, delta
+
+    def store(h, q, g, k, probs, score_grad):
+        cols = columns(h)
+        query_grad = part_ref[:, cols] + tn(score_grad, k)
+        query_grad_ref[:, cols] = (query_grad * SCALE).astype(BF16)
         own_ref[:OWN, cols] = nn(score_grad[:OWN], q) * SCALE
         own_ref[OWN:, cols] = nn(probs[:OWN], g)
+
+    backward(load, store, live)
 
 
 def band_kernel(
@@ -278,7 +300,6 @@
         (stats_ref, query_ref, out_grad_ref, top_ref, bottom_ref, part_ref),
         (top_grad_ref, bottom_grad_ref, query_grad_ref),
         jnp.concatenate(lives, axis=0),
-        1.0,
         True,
     )
 
@@ -290,39 +311,37 @@
     out_grad_ref,
     left_ref,
     right_ref,
-    part_ref,
-    left_grad_ref,
-    right_grad_ref,
+    side_grad_ref,
     query_grad_ref,
 ):
     rows = lax.broadcasted_iota(jnp.int32, (2 * SIDE, HDIM), 0)
     lives = jnp.where(rows < SIDE, live_ref[3].astype(F32), live_ref[5].astype(F32))
     two_halves(
-        (stats_ref, query_ref, out_grad_ref, left_ref, right_ref, part_ref),
-        (left_grad_ref, right_grad_ref, query_grad_ref),
+        (stats_ref, query_ref, out_grad_ref, left_ref, right_ref, None),
+        (side_grad_ref.at[: 2 * SIDE], side_grad_ref.at[2 * SIDE :], query_grad_ref),
         lives,
-        SCALE,
         False,
     )
 
 
-def two_halves(given, made, live, scale, code):
+def two_halves(given, made, live, code):
     stats_ref, query_ref, out_grad_ref, first_ref, second_ref, part_ref = given
     first_grad_ref, second_grad_ref, query_grad_ref = made
     rows = first_ref.shape[0] // 2
-    for h in range(HEADS):
-        cols = slice(h * HDIM, (h + 1) * HDIM)
-        q = query_ref[:, cols]
-        g = out_grad_ref[:, cols]
+
+    def load(h):
+        cols = columns(h)
         k, v = (
             jnp.concatenate([first_ref[at, cols], second_ref[at, cols]], axis=0)
             for at in (slice(0, rows), slice(rows, 2 * rows))
         )
-        norm = stats_ref[h : h + 1, :]
-        delta = stats_ref[16 + h : 17 + h, :]
-        probs, score_grad = backward(q, g, k, v, norm, delta, live)
-        query_grad = part_ref[:, cols] + tn(score_grad, k)
-        query_grad_ref[:, cols] = (query_grad * scale).astype(query_grad_ref.dtype)
+        norm, delta = stats_ref[h : h + 1, :], stats_ref[16 + h : 17 + h, :]
+        return query_ref[:, cols], out_grad_ref[:, cols], k, v, norm, delta
+
+    def store(h, q, g, k, probs, score_grad):
+        cols = columns(h)
+        query_grad = tn(score_grad, k)
+        query_grad_ref[:, cols] = query_grad if part_ref is None else part_ref[:, cols] + query_grad
         grads = (nn(score_grad, q) * SCALE, nn(probs, g))
         for n, ref in enumerate((first_grad_ref, second_grad_ref)):
             levels = []
@@ -335,6 +354,8 @@
             if code:
                 ref[2 * rows :, cols] = levels_of(levels)
 
+    backward(load, store, live)
+
 
 def received(ref, part, rows):
     level = wide(ref[2 * rows :, :])[part : part + 1]
@@ -342,15 +363,16 @@
 
 
 def corners_kernel(
-    select_ref, left_ref, right_ref, above_ref, below_ref, left_out_ref, right_out_ref
+    select_ref, sides_ref, above_ref, below_ref, left_out_ref, right_out_ref
 ):
     levels = ([], [])
     for part in range(2):
         side = slice(part * SIDE, (part + 1) * SIDE)
         bands = [received(ref, part, ENDS) for ref in (above_ref, below_ref)]
-        more = exact(select_ref[...], jnp.concatenate(bands, axis=0))
-        for n, (ref, out) in enumerate(((left_ref, left_out_ref), (right_ref, right_out_ref))):
-            code, level = coded(ref[side, :] + more[n * SIDE : (n + 1) * SIDE])
+        more = picked(select_ref[...], jnp.concatenate(bands, axis=0))
+        for n, out in enumerate((left_out_ref, right_out_ref)):
+            here = sides_ref[(2 * n + part) * SIDE : (2 * n + part + 1) * SIDE, :]
+            code, level = coded(here + more[n * SIDE : (n + 1) * SIDE])
             out[side, :] = code
             levels[n].append(level)
     left_out_ref[2 * SIDE :, :] = levels_of(levels[0])
@@ -365,7 +387,7 @@
         above, below = received(above_ref, part, ENDS), received(below_ref, part, ENDS)
         sides = [received(ref, part, SIDE) for ref in (left_ref, right_ref)]
         rows = jnp.concatenate(sides, axis=0)
-        total = own_ref[part * OWN : (part + 1) * OWN, :] + exact(select_ref[...], rows)
+        total = own_ref[part * OWN : (part + 1) * OWN, :] + picked(select_ref[...], rows)
         for frame in range(FRAMES):
             at = frame * BAND
             top = frame * TILE * TILE
@@ -495,13 +517,6 @@
     )
     from_right = shifted(left, "wa", -1)
     from_left = shifted(right, "wa", 1)
-    part, own = call(
-        own_kernel,
-        [((OWN, width), F32), ((2 * OWN, width), F32)],
-        [live, stats, q, g, k, v, text_keys, text_values],
-        us=3,
-        smem=1,
-    )
     top, bottom = call(
         ends_kernel,
         [((2 * ENDS, width), BF16)] * 2,
@@ -509,6 +524,13 @@
     )
     from_below = shifted(top, HA, -1)
     from_above = shifted(bottom, HA, 1)
+    side_grad, part = call(
+        side_kernel,
+        [((4 * SIDE, width), F32), ((OWN, width), F32)],
+        [live, stats, q, g, from_left, from_right],
+        us=2,
+        smem=1,
+    )
     top_grad, bottom_grad, part = call(
         band_kernel,
         [((2 * ENDS + 8, width), I16)] * 2 + [((OWN, width), F32)],
@@ -518,26 +540,26 @@
     )
     above = shifted(bottom_grad, HA, 1)
     below = shifted(top_grad, HA, -1)
-    left_grad, right_grad, query_grad = call(
-        side_kernel,
-        [((2 * SIDE, width), F32)] * 2 + [((OWN, width), BF16)],
-        [live, stats, q, g, from_left, from_right, part],
-        us=2,
-        smem=1,
-    )
     back = np.concatenate([BANDS[0].T, BANDS[1].T], axis=1)
     left_grad, right_grad = call(
         corners_kernel,
         [((2 * SIDE + 8, width), I16)] * 2,
-        [jnp.asarray(back[OWN:], F32), left_grad, right_grad, above, below],
+        [jnp.asarray(back[OWN:], BF16), side_grad, above, below],
     )
     after = shifted(left_grad, "wa", -1)
     before = shifted(right_grad, "wa", 1)
+    query_grad, own = call(
+        own_kernel,
+        [((OWN, width), BF16), ((2 * OWN, width), F32)],
+        [live, stats, q, g, k, v, text_keys, text_values, part],
+        us=3,
+        smem=1,
+    )
     back = np.concatenate([SIDES[0].T, SIDES[1].T], axis=1)
     key_grad, value_grad = call(
         sum_kernel,
         [((OWN, width), BF16)] * 2,
-        [jnp.asarray(back, F32), own, before, after, above, below],
+        [jnp.asarray(back, BF16), own, before, after, above, below],
     )
     return (
         query_grad.reshape(shape),

time: 136 us -> 123 us (0.904)
  Pallas kernels: 24.5 us -> 15.9 us
  local copies, waits for them, and re-layouts: 8.64 us -> 5.76 us
    pallas_call x11, Pallas kernels: 24.5 us -> 15.9 us  [call(): pl.pallas_call(function, out_shape=[jax.ShapeDtypeStruct(shape, dtype) fo...]
    unnamed x42 -> x36, local copies, waits for them, and re-layouts: 8.3 us -> 5.42 us
  transfers between devices with their start and end apart: 10 -> 10, of which waited for: 4 -> 5; matrix products, arithmetic and copies ran while one was open for 0% -> 0% of each run, Pallas kernels for 13% -> 9%
where the time goes in v6:
time: 123 us; the launch traced here: 122 us
  blocking collectives  56.1 us (46%)
  starting transfers between devices  29.7 us (24%)
  Pallas kernels  15.9 us (13%)
  waiting for transfers between devices  14.1 us (11%)
  local copies, waits for them, and re-layouts  5.76 us (5%)
    all_to_all x1, blocking collectives, exchanged(): return lax.all_to_all(pieces, axis, 0, 0, tiled=True)  56.1 us
    ppermute x8, starting transfers between devices, shifted(): lax.ppermute(value, axis, [(i, (i + steps) % count) for i in range(count)])  16.5 us
    pallas_call x11, Pallas kernels, call(): pl.pallas_call(function, out_shape=[jax.ShapeDtypeStruct(shape, dtype) fo...  15.9 us
    ppermute x8, waiting for transfers between devices, shifted(): lax.ppermute(value, axis, [(i, (i + steps) % count) for i in range(count)])  14.1 us
    all_to_all x2, starting transfers between devices, exchanged(): return lax.all_to_all(pieces, axis, 0, 0, tiled=True)  13.3 us
    unnamed x36, local copies, waits for them, and re-layouts  5.42 us
  transfers between devices with their start and end apart: 10, of which 5 were waited for; matrix products, arithmetic and copies ran while one was open for 0% of the time, Pallas kernels for 9%

profile of v6, /device:TPU:65, one launch (start us, length us, event | category | flops | bytes accessed | tf_op | source)
XLA Modules:
  0.0 122.3 jit_solution(5696142227047206399)
XLA Ops:
  0.7 3.2 %shard_map.164 = (s16[896,128]{1,0:T(8,128)(2,1)}, f32[32,128]{1,0:T(8,128)}) custom-call(f32[128,12]{1,0:T(8,128)} %bitcast.29, f32[128,12]{1,0:T(8,128)} %bitcast.30, bf16[128,1536]{1,0:T(8,128)(2,1)} %bitcast.14, bf16[128,1536]{1,0:T(8,128)(2,1)} %bitcast.18, bf16[32,1536]{1,0:T(8,128)(2,1)} %text_key_ref.1, bf16[32,1536]{1,0:T(8,128)(2,1)} %text_value_ref.1), custom_call_target="tpu_custom_call" | custom-call | flops 150000000 | bytes 1000000 | tf_op jit(solution)/shard_map/pallas_call | solution.py:453
  3.9 56.1 %all_to_all.15.parts_ref = s16[16,56,128]{2,1,0:T(8,128)(2,1)S(1)} all-to-all(s16[16,56,128]{2,1,0:T(8,128)(2,1)} %bitcast.28), channel_id=1, replica_groups=mesh['group'=2,'ha_0'=8,'ha_1'=2,'wa'=16] {'ha_0','ha_1'}, dimensions={0} | all-to-all | bytes 458752 | tf_op jit(solution)/shard_map/all_to_all | solution.py:476
  60.0 0.8 shard_map.172
  60.8 7.0 %all-to-all-start.1 = ((s16[16,56,128]{2,1,0:T(8,128)(2,1)}), s16[16,56,128]{2,1,0:T(8,128)(2,1)S(1)}, u32[]{:S(2)}, u32[]{:S(2)}) async-start(s16[16,56,128]{2,1,0:T(8,128)(2,1)} %shard_map.172), calls=%async_computation.1 | async-start | bytes 458752 | tf_op jit(solution)/shard_map/all_to_all | solution.py:476
  68.2 3.1 %collective-permute-start = (bf16[64,1536]{1,0:T(8,128)(2,1)S(1)}, bf16[64,1536]{1,0:T(8,128)(2,1)S(1)}, u32[]{:S(2)}, u32[]{:S(2)}) collective-permute-start(bf16[64,1536]{1,0:T(8,128)(2,1)S(1)} %get-tuple-element.25), channel_id=1, source_target_pairs={{0,1},{1,2},{2,3},{3,4},{4,5},{5,6},{6,7},{7,8},{8,9},{9,10},{10,1... | collective-permute-start | bytes 589832 | tf_op jit(solution)/shard_map/ppermute | solution.py:468
  71.3 3.5 %collective-permute-start.1 = (bf16[64,1536]{1,0:T(8,128)(2,1)S(1)}, bf16[64,1536]{1,0:T(8,128)(2,1)S(1)}, u32[]{:S(2)}, u32[]{:S(2)}) collective-permute-start(bf16[64,1536]{1,0:T(8,128)(2,1)S(1)} %get-tuple-element.26), channel_id=1, source_target_pairs={{0,15},{1,0},{2,1},{3,2},{4,3},{5,4},{6,5},{7,6},{8,7},{9,8},{10,9... | collective-permute-start | bytes 589832 | tf_op jit(solution)/shard_map/ppermute | solution.py:468
  74.8 10.4 %collective-permute-done.left_ref = bf16[64,1536]{1,0:T(8,128)(2,1)S(1)} collective-permute-done((bf16[64,1536]{1,0:T(8,128)(2,1)S(1)}, bf16[64,1536]{1,0:T(8,128)(2,1)S(1)}, u32[]{:S(2)}, u32[]{:S(2)}) %collective-permute-start) | collective-permute-done | bytes 196640 | tf_op jit(solution)/shard_map/ppermute | solution.py:468
  85.2 1.2 %shard_map.166 = (bf16[96,1536]{1,0:T(8,128)(2,1)S(1)}, bf16[96,1536]{1,0:T(8,128)(2,1)}) custom-call(bf16[2,48,192]{2,1,0:T(8,128)(2,1)S(1)} %copy-done.14, bf16[128,1536]{1,0:T(8,128)(2,1)S(1)} %bitcast.23, bf16[128,1536]{1,0:T(8,128)(2,1)S(1)} %bitcast.26, bf16[64,1536]{1,0:T(8,128)(2,1)S(1)} %collective-permute-done.left_ref, ...), custom_call_target="tpu_custom_call" | custom-call | flops 50000000 | bytes 1000000 | tf_op jit(solution)/shard_map/pallas_call | solution.py:453
  86.4 0.4 collective-permute-start.2
  86.8 0.6 collective-permute-start.3
  87.7 1.5 %shard_map.167 = (f32[128,1536]{1,0:T(8,128)S(1)}, f32[128,1536]{1,0:T(8,128)S(1)}) custom-call(s32[9]{0:T(128)S(1)} %dynamic-slice_reduce_fusion.live_ref, f32[32,128]{1,0:T(8,128)S(1)} %copy-done.13, bf16[128,1536]{1,0:T(8,128)(2,1)S(1)} %bitcast.15, bf16[128,1536]{1,0:T(8,128)(2,1)S(1)} %bitcast.19, bf16[64,1536]{1,0:T(8,128)(2,1)S(1)} %collective-permute-done.left_ref, ...), custom_call_target="tpu_custom_call" | custom-call | flops 100000000 | bytes 1000000 | tf_op jit(solution)/shard_map/pallas_call | solution.py:453
  89.2 0.9 copy-done.5
  90.1 0.7 collective-permute-done.2.top_ref
  90.7 0.7 copy-done.9
  91.5 1.7 %collective-permute-done.3.bottom_ref = bf16[96,1536]{1,0:T(8,128)(2,1)S(1)} collective-permute-done((bf16[96,1536]{1,0:T(8,128)(2,1)S(1)}, bf16[96,1536]{1,0:T(8,128)(2,1)S(1)}, u32[]{:S(2)}, u32[]{:S(2)}) %collective-permute-start.3) | collective-permute-done | bytes 294944 | tf_op jit(solution)/shard_map/ppermute | solution.py:468
  93.2 0.7 copy-done.11
  93.9 1.0 copy-done.10
  94.9 1.0 copy-done.12
  95.8 2.6 %shard_map.168 = (s16[104,1536]{1,0:T(8,128)(2,1)}, s16[104,1536]{1,0:T(8,128)(2,1)}, f32[128,1536]{1,0:T(8,128)S(1)}) custom-call(s32[9]{0:T(128)S(1)} %dynamic-slice_reduce_fusion.live_ref, f32[32,128]{1,0:T(8,128)S(1)} %copy-done.13, bf16[128,1536]{1,0:T(8,128)(2,1)S(1)} %bitcast.16, bf16[128,1536]{1,0:T(8,128)(2,1)S(1)} %bitcast.20, ...), custom_call_target="tpu_custom_call" | custom-call | flops 100000000 | bytes 1000000 | tf_op jit(solution)/shard_map/pallas_call | solution.py:453
  98.4 0.6 collective-permute-start.4
  99.1 1.8 %collective-permute-start.5 = (s16[104,1536]{1,0:T(8,128)(2,1)}, s16[104,1536]{1,0:T(8,128)(2,1)S(1)}, u32[]{:S(2)}, u32[]{:S(2)}) collective-permute-start(s16[104,1536]{1,0:T(8,128)(2,1)} %get-tuple-element.35), channel_id=1, source_target_pairs={{0,240},{16,0},{32,16},{48,32},{64,48},{80,64},{96,80},{112,96},{1... | collective-permute-start | bytes 958472 | tf_op jit(solution)/shard_map/ppermute | solution.py:468
  100.9 0.8 shard_map.173
  101.7 6.2 %all-to-all-start.2 = ((bf16[16,48,128]{2,1,0:T(8,128)(2,1)}), bf16[16,48,128]{2,1,0:T(8,128)(2,1)S(1)}, u32[]{:S(2)}, u32[]{:S(2)}) async-start(bf16[16,48,128]{2,1,0:T(8,128)(2,1)} %shard_map.173), calls=%async_computation.2 | async-start | bytes 393216 | tf_op jit(solution)/shard_map/all_to_all | solution.py:476
  108.0 1.1 copy-done.6
  109.1 0.8 shard_map.170
  109.9 2.0 %collective-permute-start.6 = (s16[72,1536]{1,0:T(8,128)(2,1)S(1)}, s16[72,1536]{1,0:T(8,128)(2,1)S(1)}, u32[]{:S(2)}, u32[]{:S(2)}) collective-permute-start(s16[72,1536]{1,0:T(8,128)(2,1)S(1)} %get-tuple-element.36), channel_id=1, source_target_pairs={{0,1},{1,2},{2,3},{3,4},{4,5},{5,6},{6,7},{7,8},{8,9},{9,10},{10,1... | collective-permute-start | bytes 663560 | tf_op jit(solution)/shard_map/ppermute | solution.py:468
  111.8 4.6 %collective-permute-start.7 = (s16[72,1536]{1,0:T(8,128)(2,1)S(1)}, s16[72,1536]{1,0:T(8,128)(2,1)S(1)}, u32[]{:S(2)}, u32[]{:S(2)}) collective-permute-start(s16[72,1536]{1,0:T(8,128)(2,1)S(1)} %get-tuple-element.37), channel_id=1, source_target_pairs={{0,15},{1,0},{2,1},{3,2},{4,3},{5,4},{6,5},{7,6},{8,7},{9,8},{10,9... | collective-permute-start | bytes 663560 | tf_op jit(solution)/shard_map/ppermute | solution.py:468
  116.5 2.4 %shard_map.169 = (bf16[128,1536]{1,0:T(8,128)(2,1)}, f32[256,1536]{1,0:T(8,128)S(1)}) custom-call(s32[9]{0:T(128)S(1)} %dynamic-slice_reduce_fusion.live_ref, f32[32,128]{1,0:T(8,128)S(1)} %copy-done.13, bf16[128,1536]{1,0:T(8,128)(2,1)S(1)} %bitcast.17, bf16[128,1536]{1,0:T(8,128)(2,1)S(1)} %bitcast.21, bf16[128,1536]{1,0:T(8,128)(2,1)S(1)} %bitcast.24, ...), custom_call_target="tpu_custom_call" | custom-call | flops 150000000 | bytes 1000000 | tf_op jit(solution)/shard_map/pallas_call | solution.py:453
  118.9 0.4 collective-permute-done.6.left_ref
  119.3 0.9 collective-permute-done.7.right_ref
  120.2 1.4 %shard_map.171 = (bf16[128,1536]{1,0:T(8,128)(2,1)}, bf16[128,1536]{1,0:T(8,128)(2,1)}) custom-call(bf16[128,64]{1,0:T(8,128)(2,1)S(1)} %copy-done.15, f32[256,1536]{1,0:T(8,128)S(1)} %get-tuple-element.32.own_ref, s16[72,1536]{1,0:T(8,128)(2,1)S(1)} %collective-permute-done.6.left_ref, s16[72,1536]{1,0:T(8,128)(2,1)S(1)} %collective-permute-done.7.right_ref, ...), custom_call_target="tpu_custom_call" | custom-call | flops 50000000 | bytes 1000000 | tf_op jit(solution)/shard_map/pallas_call | solution.py:453
  121.6 0.7 shard_map.174
  (37 shorter events, 0.8 us)
Async XLA Ops:
  0.6 86.7 %copy-start = (s32[16,16,9]{1,0,2:T(8,128)S(1)}, s32[16,16,9]{1,0,2:T(8,128)}, u32[]{:S(2)}) copy-start(s32[16,16,9]{1,0,2:T(8,128)} %param.21) | copy-start | bytes 27652
  0.6 67.2 %copy-start.17 = (bf16[2,32,128]{2,1,0:T(8,128)(2,1)S(1)}, bf16[2,32,128]{2,1,0:T(8,128)(2,1)}, u32[]{:S(2)}) copy-start(bf16[2,32,128]{2,1,0:T(8,128)(2,1)} %constant.29.clone.select_ref) | copy-start | bytes 49156
  0.7 67.2 %copy-start.4 = (bf16[2,8,8,1536]{3,2,1,0:T(8,128)(2,1)S(1)}, bf16[2,8,8,1536]{3,2,1,0:T(8,128)(2,1)}, u32[]{:S(2)}) copy-start(bf16[2,8,8,1536]{3,2,1,0:T(8,128)(2,1)} %param.15) | copy-start | bytes 1179652
  0.7 67.2 %copy-start.3 = (bf16[2,8,8,1536]{3,2,1,0:T(8,128)(2,1)S(1)}, bf16[2,8,8,1536]{3,2,1,0:T(8,128)(2,1)}, u32[]{:S(2)}) copy-start(bf16[2,8,8,1536]{3,2,1,0:T(8,128)(2,1)} %param.14) | copy-start | bytes 1179652
  0.7 84.5 %copy-start.14 = (bf16[2,48,192]{2,1,0:T(8,128)(2,1)S(1)}, bf16[2,48,192]{2,1,0:T(8,128)(2,1)}, u32[]{:S(2)}) copy-start(bf16[2,48,192]{2,1,0:T(8,128)(2,1)} %constant.30.clone.select_ref) | copy-start | bytes 110596
  60.0 27.7 %copy-start.1 = (bf16[2,8,8,1536]{3,2,1,0:T(8,128)(2,1)S(1)}, bf16[2,8,8,1536]{3,2,1,0:T(8,128)(2,1)}, u32[]{:S(2)}) copy-start(bf16[2,8,8,1536]{3,2,1,0:T(8,128)(2,1)} %param.13) | copy-start | bytes 1179652
  60.0 27.7 %copy-start.2 = (bf16[2,8,8,1536]{3,2,1,0:T(8,128)(2,1)S(1)}, bf16[2,8,8,1536]{3,2,1,0:T(8,128)(2,1)}, u32[]{:S(2)}) copy-start(bf16[2,8,8,1536]{3,2,1,0:T(8,128)(2,1)} %param.16) | copy-start | bytes 1179652
  60.0 27.7 %copy-start.13 = (f32[32,128]{1,0:T(8,128)S(1)}, f32[32,128]{1,0:T(8,128)}, u32[]{:S(2)}) copy-start(f32[32,128]{1,0:T(8,128)} %get-tuple-element.24.stats_ref) | copy-start | bytes 49156
  60.8 40.1 %all-to-all-start.1 = ((s16[16,56,128]{2,1,0:T(8,128)(2,1)}), s16[16,56,128]{2,1,0:T(8,128)(2,1)S(1)}, u32[]{:S(2)}, u32[]{:S(2)}) async-start(s16[16,56,128]{2,1,0:T(8,128)(2,1)} %shard_map.172), calls=%async_computation.1 | async-start | bytes 458752 | tf_op jit(solution)/shard_map/all_to_all | solution.py:476
  68.2 16.9 %collective-permute-start = (bf16[64,1536]{1,0:T(8,128)(2,1)S(1)}, bf16[64,1536]{1,0:T(8,128)(2,1)S(1)}, u32[]{:S(2)}, u32[]{:S(2)}) collective-permute-start(bf16[64,1536]{1,0:T(8,128)(2,1)S(1)} %get-tuple-element.25), channel_id=1, source_target_pairs={{0,1},{1,2},{2,3},{3,4},{4,5},{5,6},{6,7},{7,8},{8,9},{9,10},{10,1... | collective-permute-start | bytes 589832 | tf_op jit(solution)/shard_map/ppermute | solution.py:468
  71.3 13.8 %collective-permute-start.1 = (bf16[64,1536]{1,0:T(8,128)(2,1)S(1)}, bf16[64,1536]{1,0:T(8,128)(2,1)S(1)}, u32[]{:S(2)}, u32[]{:S(2)}) collective-permute-start(bf16[64,1536]{1,0:T(8,128)(2,1)S(1)} %get-tuple-element.26), channel_id=1, source_target_pairs={{0,15},{1,0},{2,1},{3,2},{4,3},{5,4},{6,5},{7,6},{8,7},{9,8},{10,9... | collective-permute-start | bytes 589832 | tf_op jit(solution)/shard_map/ppermute | solution.py:468
  86.4 4.4 %collective-permute-start.2 = (bf16[96,1536]{1,0:T(8,128)(2,1)}, bf16[96,1536]{1,0:T(8,128)(2,1)S(1)}, u32[]{:S(2)}, u32[]{:S(2)}) collective-permute-start(bf16[96,1536]{1,0:T(8,128)(2,1)} %get-tuple-element.27), channel_id=1, source_target_pairs={{0,16},{16,32},{32,48},{48,64},{64,80},{80,96},{96,112},{112,128},... | collective-permute-start | bytes 884744 | tf_op jit(solution)/shard_map/ppermute | solution.py:468
  86.8 6.4 %collective-permute-start.3 = (bf16[96,1536]{1,0:T(8,128)(2,1)S(1)}, bf16[96,1536]{1,0:T(8,128)(2,1)S(1)}, u32[]{:S(2)}, u32[]{:S(2)}) collective-permute-start(bf16[96,1536]{1,0:T(8,128)(2,1)S(1)} %get-tuple-element.28), channel_id=1, source_target_pairs={{0,240},{16,0},{32,16},{48,32},{64,48},{80,64},{96,80},{112,96},{1... | collective-permute-start | bytes 884744 | tf_op jit(solution)/shard_map/ppermute | solution.py:468
  87.7 20.3 %copy-start.16 = (bf16[64,96]{1,0:T(8,128)(2,1)S(1)}, bf16[64,96]{1,0:T(8,128)(2,1)}, u32[]{:S(2)}) copy-start(bf16[64,96]{1,0:T(8,128)(2,1)} %constant.31.clone.select_ref) | copy-start | bytes 36868
  89.2 0.9 copy-start.5
  90.7 0.7 copy-start.9
  93.2 0.7 copy-start.11
  93.9 1.0 copy-start.10
  94.9 1.0 copy-start.12
  98.4 18.0 %copy-start.7 = (bf16[32,1536]{1,0:T(8,128)(2,1)S(1)}, bf16[32,1536]{1,0:T(8,128)(2,1)}, u32[]{:S(2)}) copy-start(bf16[32,1536]{1,0:T(8,128)(2,1)} %text_key_ref.1) | copy-start | bytes 294916
  98.4 18.0 %copy-start.8 = (bf16[32,1536]{1,0:T(8,128)(2,1)S(1)}, bf16[32,1536]{1,0:T(8,128)(2,1)}, u32[]{:S(2)}) copy-start(bf16[32,1536]{1,0:T(8,128)(2,1)} %text_value_ref.1) | copy-start | bytes 294916
  98.4 9.5 %collective-permute-start.4 = (s16[104,1536]{1,0:T(8,128)(2,1)}, s16[104,1536]{1,0:T(8,128)(2,1)S(1)}, u32[]{:S(2)}, u32[]{:S(2)}) collective-permute-start(s16[104,1536]{1,0:T(8,128)(2,1)} %get-tuple-element.34), channel_id=1, source_target_pairs={{0,16},{16,32},{32,48},{48,64},{64,80},{80,96},{96,112},{112,128},... | collective-permute-start | bytes 958472 | tf_op jit(solution)/shard_map/ppermute | solution.py:468
  99.1 8.8 %collective-permute-start.5 = (s16[104,1536]{1,0:T(8,128)(2,1)}, s16[104,1536]{1,0:T(8,128)(2,1)S(1)}, u32[]{:S(2)}, u32[]{:S(2)}) collective-permute-start(s16[104,1536]{1,0:T(8,128)(2,1)} %get-tuple-element.35), channel_id=1, source_target_pairs={{0,240},{16,0},{32,16},{48,32},{64,48},{80,64},{96,80},{112,96},{1... | collective-permute-start | bytes 958472 | tf_op jit(solution)/shard_map/ppermute | solution.py:468
  101.7 19.9 %all-to-all-start.2 = ((bf16[16,48,128]{2,1,0:T(8,128)(2,1)}), bf16[16,48,128]{2,1,0:T(8,128)(2,1)S(1)}, u32[]{:S(2)}, u32[]{:S(2)}) async-start(bf16[16,48,128]{2,1,0:T(8,128)(2,1)} %shard_map.173), calls=%async_computation.2 | async-start | bytes 393216 | tf_op jit(solution)/shard_map/all_to_all | solution.py:476
  107.9 1.1 copy-start.6
  109.9 10.3 %copy-start.15 = (bf16[128,64]{1,0:T(8,128)(2,1)S(1)}, bf16[128,64]{1,0:T(8,128)(2,1)}, u32[]{:S(2)}) copy-start(bf16[128,64]{1,0:T(8,128)(2,1)} %constant.32.clone.select_ref) | copy-start | bytes 49156
  109.9 9.4 %collective-permute-start.6 = (s16[72,1536]{1,0:T(8,128)(2,1)S(1)}, s16[72,1536]{1,0:T(8,128)(2,1)S(1)}, u32[]{:S(2)}, u32[]{:S(2)}) collective-permute-start(s16[72,1536]{1,0:T(8,128)(2,1)S(1)} %get-tuple-element.36), channel_id=1, source_target_pairs={{0,1},{1,2},{2,3},{3,4},{4,5},{5,6},{6,7},{7,8},{8,9},{9,10},{10,1... | collective-permute-start | bytes 663560 | tf_op jit(solution)/shard_map/ppermute | solution.py:468
  111.8 8.4 %collective-permute-start.7 = (s16[72,1536]{1,0:T(8,128)(2,1)S(1)}, s16[72,1536]{1,0:T(8,128)(2,1)S(1)}, u32[]{:S(2)}, u32[]{:S(2)}) collective-permute-start(s16[72,1536]{1,0:T(8,128)(2,1)S(1)} %get-tuple-element.37), channel_id=1, source_target_pairs={{0,15},{1,0},{2,1},{3,2},{4,3},{5,4},{6,5},{7,6},{8,7},{9,8},{10,9... | collective-permute-start | bytes 663560 | tf_op jit(solution)/shard_map/ppermute | solution.py:468

commit v7 on v6

--- a/solution.py
+++ b/solution.py
@@ -15,6 +15,8 @@
 TILE = 8
 HALO = 2
 HA = ("ha_0", "ha_1")
+WA = ("wa_0", "wa_1")
+NEAR = (*HA, "wa_1")
 F32 = jnp.float32
 BF16 = jnp.bfloat16
 SCALE = 1.0 / math.sqrt(HDIM)
@@ -132,6 +134,11 @@
         at = slice(part * SIDE, (part + 1) * SIDE)
         left_ref[at, :] = nn(select_ref[0], rows).astype(BF16)
         right_ref[at, :] = nn(select_ref[1], rows).astype(BF16)
+
+
+def place(part, row, rows):
+    piece, within = divmod(row, rows)
+    return 4 * (piece // 2) + 2 * part + piece % 2, within
 
 
 def text_kernel(
@@ -174,12 +181,12 @@
 
     def store(h, q, g, k, probs, score_grad):
         for part, grad in enumerate((nn(score_grad, q) * SCALE, nn(probs, g))):
-            for at in range(0, text, 16):
-                chip, within = divmod(h * text + at, piece)
-                to = 2 * chip + part
-                code, level = coded(grad[at : at + 16])
-                grad_ref[to * sent + within : to * sent + within + 16, :] = code
-                levels_ref[to * 8 + within // 16 : to * 8 + within // 16 + 1, :] = level
+            code, level = coded(grad)
+            for at in range(0, text, 8):
+                to, within = place(part, h * text + at, piece)
+                grad_ref[to * sent + within : to * sent + within + 8, :] = code[at : at + 8]
+                row = to * 8 + within // 8
+                levels_ref[row : row + 1, :] = level
 
     backward(load, store, None)
     for to in range(pieces):
@@ -193,8 +200,8 @@
     for n in range(count):
         levels = wide(parts_ref[n, sent - 8 :, :])
         blocks = [
-            decoded(parts_ref[n, 16 * b : 16 * b + 16, :], levels[b : b + 1])
-            for b in range((sent - 8) // 16)
+            decoded(parts_ref[n, 8 * b : 8 * b + 8, :], levels[b : b + 1])
+            for b in range((sent - 8) // 8)
         ]
         total = total + jnp.concatenate(blocks, axis=0)
     code, level = coded(total)
@@ -239,14 +246,15 @@
 
 
 def own_kernel(
+    ready,
     live_ref,
-    stats_ref,
     query_ref,
     out_grad_ref,
     keys_ref,
     values_ref,
     text_key_ref,
     text_value_ref,
+    stats_ref,
     part_ref,
     query_grad_ref,
     own_ref,
@@ -256,6 +264,7 @@
     live = jnp.where(rows < OWN, live_ref[4].astype(F32), 1.0)
 
     def load(h):
+        ready(h)
         cols = columns(h)
         k = jnp.concatenate([keys_ref[:, cols], text_key_ref[:, cols]], axis=0)
         v = jnp.concatenate([values_ref[:, cols], text_value_ref[:, cols]], axis=0)
@@ -405,24 +414,24 @@
     rows = parts_ref.shape[1]
     for part, out in enumerate((key_ref, value_ref)):
         for h in range(HEADS):
-            for at in range(0, text, 16):
-                chip, within = divmod(h * text + at, rows)
-                piece = parts_ref[2 * chip + part, within : within + 16, :]
-                out[at : at + 16, h * HDIM : (h + 1) * HDIM] = piece
-
-
-def call(kernel, outs, ins, us=1.0, smem=0, fetch=False, scratch=()):
+            for at in range(0, text, 8):
+                to, within = place(part, h * text + at, rows)
+                piece = parts_ref[to, within : within + 8, :]
+                out[at : at + 8, h * HDIM : (h + 1) * HDIM] = piece
+
+
+def call(kernel, outs, ins, us=1.0, smem=0, fetch=0, scratch=()):
     groups = HEADS // GROUP
     step = GROUP * HDIM
 
     def body(*refs):
         n = len(ins)
         outputs = refs[n : n + len(outs)]
-        buffers = refs[n + len(outs) : 2 * n + len(outs)]
-        semaphores, *rest = refs[2 * n + len(outs) :]
+        near_refs = refs[n + len(outs) : n + len(outs) + fetch]
+        semaphores, *rest = refs[n + len(outs) + fetch :]
         small, wide = [], [[] for _ in range(groups)]
-        for i, (far, near) in enumerate(zip(refs[:n], buffers)):
-            if ins[i].ndim == 2 and ins[i].shape[1] == groups * step:
+        for i, (far, near) in enumerate(zip(refs[smem : smem + fetch], near_refs)):
+            if near.ndim == 2 and near.shape[1] == groups * step:
                 for m in range(groups):
                     at = (slice(None), slice(m * step, (m + 1) * step))
                     copy = pltpu.make_async_copy(far.at[at], near.at[at], semaphores.at[i, m])
@@ -440,16 +449,18 @@
                 for copy in wide[h // GROUP]:
                     copy.wait()
 
-        kernel(ready, *buffers, *outputs, *rest)
+        kernel(ready, *refs[:smem], *near_refs, *refs[smem + fetch : n], *outputs, *rest)
 
     here = pl.BlockSpec(memory_space=pltpu.VMEM)
     scalars = pl.BlockSpec(memory_space=pltpu.SMEM)
     if not fetch:
         function, specs, scratch, limit = kernel, [scalars] * smem + [here] * (len(ins) - smem), [*scratch], 16
     else:
-        function, specs, limit = body, [pl.BlockSpec(memory_space=pltpu.HBM)] * len(ins), 56
-        buffers = [pltpu.VMEM(a.shape, a.dtype) for a in ins]
-        scratch = [*buffers, pltpu.SemaphoreType.DMA((len(ins), groups)), *scratch]
+        function, limit = body, 56
+        far = pl.BlockSpec(memory_space=pltpu.HBM)
+        specs = [scalars] * smem + [far] * fetch + [here] * (len(ins) - smem - fetch)
+        buffers = [pltpu.VMEM(a.shape, a.dtype) for a in ins[smem : smem + fetch]]
+        scratch = [*buffers, pltpu.SemaphoreType.DMA((fetch, groups)), *scratch]
     return pl.pallas_call(
         function,
         out_shape=[jax.ShapeDtypeStruct(shape, dtype) for shape, dtype in outs],
@@ -488,10 +499,10 @@
     v = values.reshape(OWN, width)
     anchor = jnp.zeros((), jnp.int32)
     live = lax.dynamic_slice(
-        window_table, (lax.axis_index(HA), lax.axis_index("wa"), anchor), (1, 1, 9)
+        window_table, (lax.axis_index(HA), lax.axis_index(WA), anchor), (1, 1, 9)
     ).reshape(9)
 
-    count = lax.axis_size(HA)
+    count = lax.axis_size(NEAR)
     piece = 2 * HEADS * text // count
     sent = piece + 8
     words, stats = call(
@@ -499,15 +510,15 @@
         [((count * sent, HDIM), I16), ((32, HDIM), F32)],
         [by_query(log_norm), by_query(delta_rows), q, g, text_keys, text_values],
         us=3,
-        fetch=True,
+        fetch=6,
         scratch=[pltpu.VMEM((count * 8, HDIM), F32)],
     )
-    words = exchanged(words.reshape(count, sent, HDIM), HA)
-    tiles = lax.axis_size("wa")
+    words = exchanged(words.reshape(count, sent, HDIM), NEAR)
+    tiles = lax.axis_size("wa_0")
     (words,) = call(over_chips_kernel, [((tiles, sent, HDIM), I16)], [words])
-    words = exchanged(words, "wa")
+    words = exchanged(words, "wa_0")
     (words,) = call(over_tiles_kernel, [((count, piece, HDIM), BF16)], [words])
-    words = exchanged(words, HA)
+    words = exchanged(words, NEAR)
     text_key_grad, text_value_grad = call(
         words_kernel, [((text, width), BF16)] * 2, [words]
     )
@@ -515,8 +526,8 @@
     left, right = call(
         sides_kernel, [((2 * SIDE, width), BF16)] * 2, [jnp.asarray(SIDES, BF16), k, v]
     )
-    from_right = shifted(left, "wa", -1)
-    from_left = shifted(right, "wa", 1)
+    from_right = shifted(left, WA, -1)
+    from_left = shifted(right, WA, 1)
     top, bottom = call(
         ends_kernel,
         [((2 * ENDS, width), BF16)] * 2,
@@ -546,14 +557,15 @@
         [((2 * SIDE + 8, width), I16)] * 2,
         [jnp.asarray(back[OWN:], BF16), side_grad, above, below],
     )
-    after = shifted(left_grad, "wa", -1)
-    before = shifted(right_grad, "wa", 1)
+    after = shifted(left_grad, WA, -1)
+    before = shifted(right_grad, WA, 1)
     query_grad, own = call(
         own_kernel,
         [((OWN, width), BF16), ((2 * OWN, width), F32)],
-        [live, stats, q, g, k, v, text_keys, text_values, part],
+        [live, q, g, k, v, text_keys, text_values, stats, part],
         us=3,
         smem=1,
+        fetch=6,
     )
     back = np.concatenate([SIDES[0].T, SIDES[1].T], axis=1)
     key_grad, value_grad = call(
@@ -572,27 +584,27 @@
 
 def solution(mesh):
     split = Mesh(
-        mesh.devices.reshape(mesh.shape["group"], 8, 2, mesh.shape["wa"]),
-        ("group", "ha_0", "ha_1", "wa"),
+        mesh.devices.reshape(mesh.shape["group"], 8, 2, mesh.shape["wa"] // 2, 2),
+        ("group", "ha_0", "ha_1", "wa_0", "wa_1"),
     )
     return jax.shard_map(
         local,
         mesh=split,
         in_specs=(
-            P("group", HA, "wa", None),
-            P("group", HA, "wa", None),
-            P("group", HA, "wa", None),
-            P("group", HA, "wa", None),
-            P(None, "group", HA, "wa"),
-            P(None, "group", HA, "wa"),
+            P("group", HA, WA, None),
+            P("group", HA, WA, None),
+            P("group", HA, WA, None),
+            P("group", HA, WA, None),
+            P(None, "group", HA, WA),
+            P(None, "group", HA, WA),
             P("group", None),
             P("group", None),
             P(),
         ),
         out_specs=(
-            P("group", HA, "wa", None),
-            P("group", HA, "wa", None),
-            P("group", HA, "wa", None),
+            P("group", HA, WA, None),
+            P("group", HA, WA, None),
+            P("group", HA, WA, None),
             P("group", None),
             P("group", None),
         ),

time: 123 us -> 120 us (0.976)
  blocking collectives: 56.1 us -> 0 us
  starting transfers between devices: 29.7 us -> 80 us
  waiting for transfers between devices: 14.1 us -> 17.5 us
  local copies, waits for them, and re-layouts: 5.76 us -> 2.72 us
  Pallas kernels: 15.9 us -> 17.2 us
    all_to_all x1 -> x0, blocking collectives: 56.1 us -> none  [exchanged(): return lax.all_to_all(pieces, axis, 0, 0, tiled=True)]
    all_to_all x2 -> x3, starting transfers between devices: 13.3 us -> 59.4 us  [exchanged(): return lax.all_to_all(pieces, axis, 0, 0, tiled=True)]
    all_to_all x2 -> x3, waiting for transfers between devices: 0.01 us -> 10.7 us  [exchanged(): return lax.all_to_all(pieces, axis, 0, 0, tiled=True)]
    ppermute x8, waiting for transfers between devices: 14.1 us -> 6.72 us  [shifted(): lax.ppermute(value, axis, [(i, (i + steps) % count) for i in range(count)])]
    ppermute x8, starting transfers between devices: 16.5 us -> 20.6 us  [shifted(): lax.ppermute(value, axis, [(i, (i + steps) % count) for i in range(count)])]
    unnamed x36 -> x26, local copies, waits for them, and re-layouts: 5.42 us -> 2.38 us
    pallas_call x11, Pallas kernels: 15.9 us -> 17.2 us  [call(): pl.pallas_call(function, out_shape=[jax.ShapeDtypeStruct(shape, dtype) fo...]
  transfers between devices with their start and end apart: 10 -> 11, of which waited for: 5 -> 4; matrix products, arithmetic and copies ran while one was open for 0% -> 0% of each run, Pallas kernels for 9% -> 11%
where the time goes in v7:
time: 120 us; the launch traced here: 118 us
  starting transfers between devices  80 us (67%)
  waiting for transfers between devices  17.5 us (15%)
  Pallas kernels  17.2 us (14%)
  local copies, waits for them, and re-layouts  2.72 us (2%)
    all_to_all x3, starting transfers between devices, exchanged(): return lax.all_to_all(pieces, axis, 0, 0, tiled=True)  59.4 us
    ppermute x8, starting transfers between devices, shifted(): lax.ppermute(value, axis, [(i, (i + steps) % count) for i in range(count)])  20.6 us
    pallas_call x11, Pallas kernels, call(): pl.pallas_call(function, out_shape=[jax.ShapeDtypeStruct(shape, dtype) fo...  17.2 us
    all_to_all x3, waiting for transfers between devices, exchanged(): return lax.all_to_all(pieces, axis, 0, 0, tiled=True)  10.7 us
    ppermute x8, waiting for transfers between devices, shifted(): lax.ppermute(value, axis, [(i, (i + steps) % count) for i in range(count)])  6.72 us
  transfers between devices with their start and end apart: 11, of which 4 were waited for; matrix products, arithmetic and copies ran while one was open for 0% of the time, Pallas kernels for 11%

profile of v7, /device:TPU:65, one launch (start us, length us, event | category | flops | bytes accessed | tf_op | source)
XLA Modules:
  0.0 118.3 jit_solution(12534652907096205419)
XLA Ops:
  0.6 0.0 copy-start
  0.6 0.0 copy-start.11
  0.7 0.0 copy-start.8
  0.7 3.2 %shard_map.164 = (s16[1024,128]{1,0:T(8,128)(2,1)}, f32[32,128]{1,0:T(8,128)}) custom-call(f32[128,12]{1,0:T(8,128)} %bitcast.29, f32[128,12]{1,0:T(8,128)} %bitcast.30, bf16[128,1536]{1,0:T(8,128)(2,1)} %bitcast.14, bf16[128,1536]{1,0:T(8,128)(2,1)} %bitcast.18, bf16[32,1536]{1,0:T(8,128)(2,1)} %refs_5_.3, bf16[32,1536]{1,0:T(8,128)(2,1)} %refs_6_.1), custom_call_target="tpu_custom_call" | custom-call | flops 150000000 | bytes 1000000 | tf_op jit(solution)/shard_map/pallas_call | solution.py:464
  3.9 45.2 %all-to-all-start = ((s16[32,32,128]{2,1,0:T(8,128)(2,1)}), s16[32,32,128]{2,1,0:T(8,128)(2,1)S(1)}, u32[]{:S(2)}, u32[]{:S(2)}) async-start(s16[32,32,128]{2,1,0:T(8,128)(2,1)} %bitcast.28), calls=%async_computation | async-start | bytes 524288 | tf_op jit(solution)/shard_map/all_to_all | solution.py:487
  49.2 0.3 shard_map.165
  49.6 3.3 %collective-permute-start = (bf16[64,1536]{1,0:T(8,128)(2,1)S(1)}, bf16[64,1536]{1,0:T(8,128)(2,1)S(1)}, u32[]{:S(2)}, u32[]{:S(2)}) collective-permute-start(bf16[64,1536]{1,0:T(8,128)(2,1)S(1)} %get-tuple-element.25), channel_id=1, source_target_pairs={{0,1},{1,2},{2,3},{3,4},{4,5},{5,6},{6,7},{7,8},{8,9},{9,10},{10,1... | collective-permute-start | bytes 589832 | tf_op jit(solution)/shard_map/ppermute | solution.py:479
  52.9 7.4 %collective-permute-start.1 = (bf16[64,1536]{1,0:T(8,128)(2,1)S(1)}, bf16[64,1536]{1,0:T(8,128)(2,1)S(1)}, u32[]{:S(2)}, u32[]{:S(2)}) collective-permute-start(bf16[64,1536]{1,0:T(8,128)(2,1)S(1)} %get-tuple-element.26), channel_id=1, source_target_pairs={{0,15},{1,0},{2,1},{3,2},{4,3},{5,4},{6,5},{7,6},{8,7},{9,8},{10,9... | collective-permute-start | bytes 589832 | tf_op jit(solution)/shard_map/ppermute | solution.py:479
  60.3 0.5 all-to-all-done.parts_ref
  60.7 0.8 shard_map.172
  61.5 7.6 %all-to-all-start.1 = ((s16[8,32,128]{2,1,0:T(8,128)(2,1)}), s16[8,32,128]{2,1,0:T(8,128)(2,1)S(1)}, u32[]{:S(2)}, u32[]{:S(2)}) async-start(s16[8,32,128]{2,1,0:T(8,128)(2,1)} %shard_map.172), calls=%async_computation.1 | async-start | bytes 131072 | tf_op jit(solution)/shard_map/all_to_all | solution.py:487
  69.2 0.5 shard_map.166
  69.7 1.7 %collective-permute-start.2 = (bf16[96,1536]{1,0:T(8,128)(2,1)S(1)}, bf16[96,1536]{1,0:T(8,128)(2,1)S(1)}, u32[]{:S(2)}, u32[]{:S(2)}) collective-permute-start(bf16[96,1536]{1,0:T(8,128)(2,1)S(1)} %get-tuple-element.27), channel_id=1, source_target_pairs={{0,16},{16,32},{32,48},{48,64},{64,80},{80,96},{96,112},{112,128},... | collective-permute-start | bytes 884744 | tf_op jit(solution)/shard_map/ppermute | solution.py:479
  71.4 10.3 %all-to-all-done.1.parts_ref = s16[8,32,128]{2,1,0:T(8,128)(2,1)S(1)} async-done(((s16[8,32,128]{2,1,0:T(8,128)(2,1)}), s16[8,32,128]{2,1,0:T(8,128)(2,1)S(1)}, u32[]{:S(2)}, u32[]{:S(2)}) %all-to-all-start.1) | async-done | bytes 65568 | tf_op jit(solution)/shard_map/all_to_all | solution.py:487
  81.6 0.7 shard_map.173
  82.4 6.6 %all-to-all-start.2 = ((bf16[32,24,128]{2,1,0:T(8,128)(2,1)}), bf16[32,24,128]{2,1,0:T(8,128)(2,1)S(1)}, u32[]{:S(2)}, u32[]{:S(2)}) async-start(bf16[32,24,128]{2,1,0:T(8,128)(2,1)} %shard_map.173), calls=%async_computation.2 | async-start | bytes 393216 | tf_op jit(solution)/shard_map/all_to_all | solution.py:487
  88.9 0.3 dynamic-slice_reduce_fusion.live_ref.refs_0_
  89.3 0.0 copy-start.10
  89.3 1.5 %shard_map.167 = (f32[128,1536]{1,0:T(8,128)S(1)}, f32[128,1536]{1,0:T(8,128)S(1)}) custom-call(s32[9]{0:T(128)S(1)} %dynamic-slice_reduce_fusion.live_ref.refs_0_, f32[32,128]{1,0:T(8,128)S(1)} %copy-done.7, bf16[128,1536]{1,0:T(8,128)(2,1)S(1)} %bitcast.16, bf16[128,1536]{1,0:T(8,128)(2,1)S(1)} %bitcast.20, ...), custom_call_target="tpu_custom_call" | custom-call | flops 100000000 | bytes 1000000 | tf_op jit(solution)/shard_map/pallas_call | solution.py:464
  90.8 1.8 %shard_map.168 = (s16[104,1536]{1,0:T(8,128)(2,1)S(1)}, s16[104,1536]{1,0:T(8,128)(2,1)S(1)}, f32[128,1536]{1,0:T(8,128)S(1)}) custom-call(s32[9]{0:T(128)S(1)} %dynamic-slice_reduce_fusion.live_ref.refs_0_, f32[32,128]{1,0:T(8,128)S(1)} %copy-done.7, bf16[128,1536]{1,0:T(8,128)(2,1)S(1)} %bitcast.17, bf16[128,1536]{1,0:T(8,128)(2,1)S(1)} %bitcast.21, ...), custom_call_target="tpu_custom_call" | custom-call | flops 100000000 | bytes 1000000 | tf_op jit(solution)/shard_map/pallas_call | solution.py:464
  92.7 0.9 copy-done.6
  93.6 1.7 %collective-permute-start.4 = (s16[104,1536]{1,0:T(8,128)(2,1)S(1)}, s16[104,1536]{1,0:T(8,128)(2,1)S(1)}, u32[]{:S(2)}, u32[]{:S(2)}) collective-permute-start(s16[104,1536]{1,0:T(8,128)(2,1)S(1)} %get-tuple-element.34), channel_id=1, source_target_pairs={{0,16},{16,32},{32,48},{48,64},{64,80},{80,96},{96,112},{112,128},... | collective-permute-start | bytes 958472 | tf_op jit(solution)/shard_map/ppermute | solution.py:479
  95.2 4.1 %collective-permute-done.4.above_ref = s16[104,1536]{1,0:T(8,128)(2,1)S(1)} collective-permute-done((s16[104,1536]{1,0:T(8,128)(2,1)S(1)}, s16[104,1536]{1,0:T(8,128)(2,1)S(1)}, u32[]{:S(2)}, u32[]{:S(2)}) %collective-permute-start.4) | collective-permute-done | bytes 319520 | tf_op jit(solution)/shard_map/ppermute | solution.py:479
  99.4 2.6 %collective-permute-done.5.below_ref = s16[104,1536]{1,0:T(8,128)(2,1)S(1)} collective-permute-done((s16[104,1536]{1,0:T(8,128)(2,1)S(1)}, s16[104,1536]{1,0:T(8,128)(2,1)S(1)}, u32[]{:S(2)}, u32[]{:S(2)}) %collective-permute-start.5) | collective-permute-done | bytes 319520 | tf_op jit(solution)/shard_map/ppermute | solution.py:479
  102.0 0.8 shard_map.170
  102.8 0.0 copy-start.9
  102.8 2.9 %collective-permute-start.6 = (s16[72,1536]{1,0:T(8,128)(2,1)S(1)}, s16[72,1536]{1,0:T(8,128)(2,1)S(1)}, u32[]{:S(2)}, u32[]{:S(2)}) collective-permute-start(s16[72,1536]{1,0:T(8,128)(2,1)S(1)} %get-tuple-element.36), channel_id=1, source_target_pairs={{0,1},{1,2},{2,3},{3,4},{4,5},{5,6},{6,7},{7,8},{8,9},{9,10},{10,1... | collective-permute-start | bytes 663560 | tf_op jit(solution)/shard_map/ppermute | solution.py:479
  105.6 3.7 %collective-permute-start.7 = (s16[72,1536]{1,0:T(8,128)(2,1)S(1)}, s16[72,1536]{1,0:T(8,128)(2,1)S(1)}, u32[]{:S(2)}, u32[]{:S(2)}) collective-permute-start(s16[72,1536]{1,0:T(8,128)(2,1)S(1)} %get-tuple-element.37), channel_id=1, source_target_pairs={{0,15},{1,0},{2,1},{3,2},{4,3},{5,4},{6,5},{7,6},{8,7},{9,8},{10,9... | collective-permute-start | bytes 663560 | tf_op jit(solution)/shard_map/ppermute | solution.py:479
  109.3 5.4 %shard_map.169 = (bf16[128,1536]{1,0:T(8,128)(2,1)}, f32[256,1536]{1,0:T(8,128)}) custom-call(s32[9]{0:T(128)} %copy-done.12, bf16[128,1536]{1,0:T(8,128)(2,1)} %bitcast.15, bf16[128,1536]{1,0:T(8,128)(2,1)} %bitcast.19, bf16[128,1536]{1,0:T(8,128)(2,1)} %bitcast.22, bf16[128,1536]{1,0:T(8,128)(2,1)} %bitcast.25, bf16[32,1536]{1,0:T(8,128)(2,1)} %refs_5_.3, ...), custom_call_target="tpu_custom_call" | custom-call | flops 150000000 | bytes 1000000 | tf_op jit(solution)/shard_map/pallas_call | solution.py:464
  114.8 1.4 %copy-done.5 = f32[256,1536]{1,0:T(8,128)S(1)} copy-done((f32[256,1536]{1,0:T(8,128)S(1)}, f32[256,1536]{1,0:T(8,128)}, u32[]{:S(2)}) %copy-start.5) | copy-done | bytes 1572888
  116.2 1.4 %shard_map.171 = (bf16[128,1536]{1,0:T(8,128)(2,1)}, bf16[128,1536]{1,0:T(8,128)(2,1)}) custom-call(bf16[128,64]{1,0:T(8,128)(2,1)S(1)} %copy-done.9, f32[256,1536]{1,0:T(8,128)S(1)} %copy-done.5, s16[72,1536]{1,0:T(8,128)(2,1)S(1)} %collective-permute-done.6.left_ref, s16[72,1536]{1,0:T(8,128)(2,1)S(1)} %collective-permute-done.7.right_ref, ...), custom_call_target="tpu_custom_call" | custom-call | flops 50000000 | bytes 1000000 | tf_op jit(solution)/shard_map/pallas_call | solution.py:464
  117.6 0.7 shard_map.174
  (28 shorter events, 0.1 us)
Async XLA Ops:
  0.6 88.3 %copy-start = (s32[16,16,9]{1,0,2:T(8,128)S(1)}, s32[16,16,9]{1,0,2:T(8,128)}, u32[]{:S(2)}) copy-start(s32[16,16,9]{1,0,2:T(8,128)} %param.21) | copy-start | bytes 27652
  0.6 48.5 %copy-start.11 = (bf16[2,32,128]{2,1,0:T(8,128)(2,1)S(1)}, bf16[2,32,128]{2,1,0:T(8,128)(2,1)}, u32[]{:S(2)}) copy-start(bf16[2,32,128]{2,1,0:T(8,128)(2,1)} %constant.30.clone.select_ref) | copy-start | bytes 49156
  0.7 68.5 %copy-start.8 = (bf16[2,48,192]{2,1,0:T(8,128)(2,1)S(1)}, bf16[2,48,192]{2,1,0:T(8,128)(2,1)}, u32[]{:S(2)}) copy-start(bf16[2,48,192]{2,1,0:T(8,128)(2,1)} %constant.31.clone.select_ref) | copy-start | bytes 110596
  0.7 48.5 %copy-start.4 = (bf16[2,8,8,1536]{3,2,1,0:T(8,128)(2,1)S(1)}, bf16[2,8,8,1536]{3,2,1,0:T(8,128)(2,1)}, u32[]{:S(2)}) copy-start(bf16[2,8,8,1536]{3,2,1,0:T(8,128)(2,1)} %param.15) | copy-start | bytes 1179652
  0.7 48.5 %copy-start.3 = (bf16[2,8,8,1536]{3,2,1,0:T(8,128)(2,1)S(1)}, bf16[2,8,8,1536]{3,2,1,0:T(8,128)(2,1)}, u32[]{:S(2)}) copy-start(bf16[2,8,8,1536]{3,2,1,0:T(8,128)(2,1)} %param.14) | copy-start | bytes 1179652
  3.9 56.8 %all-to-all-start = ((s16[32,32,128]{2,1,0:T(8,128)(2,1)}), s16[32,32,128]{2,1,0:T(8,128)(2,1)S(1)}, u32[]{:S(2)}, u32[]{:S(2)}) async-start(s16[32,32,128]{2,1,0:T(8,128)(2,1)} %bitcast.28), calls=%async_computation | async-start | bytes 524288 | tf_op jit(solution)/shard_map/all_to_all | solution.py:487
  49.2 40.1 %copy-start.1 = (bf16[2,8,8,1536]{3,2,1,0:T(8,128)(2,1)S(1)}, bf16[2,8,8,1536]{3,2,1,0:T(8,128)(2,1)}, u32[]{:S(2)}) copy-start(bf16[2,8,8,1536]{3,2,1,0:T(8,128)(2,1)} %param.13) | copy-start | bytes 1179652
  49.2 40.1 %copy-start.2 = (bf16[2,8,8,1536]{3,2,1,0:T(8,128)(2,1)S(1)}, bf16[2,8,8,1536]{3,2,1,0:T(8,128)(2,1)}, u32[]{:S(2)}) copy-start(bf16[2,8,8,1536]{3,2,1,0:T(8,128)(2,1)} %param.16) | copy-start | bytes 1179652
  49.2 40.1 %copy-start.7 = (f32[32,128]{1,0:T(8,128)S(1)}, f32[32,128]{1,0:T(8,128)}, u32[]{:S(2)}) copy-start(f32[32,128]{1,0:T(8,128)} %get-tuple-element.24.stats_ref.refs_7_) | copy-start | bytes 49156
  49.6 19.5 %collective-permute-start = (bf16[64,1536]{1,0:T(8,128)(2,1)S(1)}, bf16[64,1536]{1,0:T(8,128)(2,1)S(1)}, u32[]{:S(2)}, u32[]{:S(2)}) collective-permute-start(bf16[64,1536]{1,0:T(8,128)(2,1)S(1)} %get-tuple-element.25), channel_id=1, source_target_pairs={{0,1},{1,2},{2,3},{3,4},{4,5},{5,6},{6,7},{7,8},{8,9},{9,10},{10,1... | collective-permute-start | bytes 589832 | tf_op jit(solution)/shard_map/ppermute | solution.py:479
  52.9 16.2 %collective-permute-start.1 = (bf16[64,1536]{1,0:T(8,128)(2,1)S(1)}, bf16[64,1536]{1,0:T(8,128)(2,1)S(1)}, u32[]{:S(2)}, u32[]{:S(2)}) collective-permute-start(bf16[64,1536]{1,0:T(8,128)(2,1)S(1)} %get-tuple-element.26), channel_id=1, source_target_pairs={{0,15},{1,0},{2,1},{3,2},{4,3},{5,4},{6,5},{7,6},{8,7},{9,8},{10,9... | collective-permute-start | bytes 589832 | tf_op jit(solution)/shard_map/ppermute | solution.py:479
  61.5 20.1 %all-to-all-start.1 = ((s16[8,32,128]{2,1,0:T(8,128)(2,1)}), s16[8,32,128]{2,1,0:T(8,128)(2,1)S(1)}, u32[]{:S(2)}, u32[]{:S(2)}) async-start(s16[8,32,128]{2,1,0:T(8,128)(2,1)} %shard_map.172), calls=%async_computation.1 | async-start | bytes 131072 | tf_op jit(solution)/shard_map/all_to_all | solution.py:487
  69.7 21.2 %collective-permute-start.2 = (bf16[96,1536]{1,0:T(8,128)(2,1)S(1)}, bf16[96,1536]{1,0:T(8,128)(2,1)S(1)}, u32[]{:S(2)}, u32[]{:S(2)}) collective-permute-start(bf16[96,1536]{1,0:T(8,128)(2,1)S(1)} %get-tuple-element.27), channel_id=1, source_target_pairs={{0,16},{16,32},{32,48},{48,64},{64,80},{80,96},{96,112},{112,128},... | collective-permute-start | bytes 884744 | tf_op jit(solution)/shard_map/ppermute | solution.py:479
  71.4 19.5 %collective-permute-start.3 = (bf16[96,1536]{1,0:T(8,128)(2,1)S(1)}, bf16[96,1536]{1,0:T(8,128)(2,1)S(1)}, u32[]{:S(2)}, u32[]{:S(2)}) collective-permute-start(bf16[96,1536]{1,0:T(8,128)(2,1)S(1)} %get-tuple-element.28), channel_id=1, source_target_pairs={{0,240},{16,0},{32,16},{48,32},{64,48},{80,64},{96,80},{112,96},{1... | collective-permute-start | bytes 884744 | tf_op jit(solution)/shard_map/ppermute | solution.py:479
  82.4 35.2 %all-to-all-start.2 = ((bf16[32,24,128]{2,1,0:T(8,128)(2,1)}), bf16[32,24,128]{2,1,0:T(8,128)(2,1)S(1)}, u32[]{:S(2)}, u32[]{:S(2)}) async-start(bf16[32,24,128]{2,1,0:T(8,128)(2,1)} %shard_map.173), calls=%async_computation.2 | async-start | bytes 393216 | tf_op jit(solution)/shard_map/all_to_all | solution.py:487
  89.3 3.4 %copy-start.12 = (s32[9]{0:T(128)}, s32[9]{0:T(128)S(1)}, u32[]{:S(2)}) copy-start(s32[9]{0:T(128)S(1)} %dynamic-slice_reduce_fusion.live_ref.refs_0_) | copy-start | bytes 112
  89.3 12.6 %copy-start.10 = (bf16[64,96]{1,0:T(8,128)(2,1)S(1)}, bf16[64,96]{1,0:T(8,128)(2,1)}, u32[]{:S(2)}) copy-start(bf16[64,96]{1,0:T(8,128)(2,1)} %constant.32.clone.select_ref) | copy-start | bytes 36868
  92.7 0.9 copy-start.6
  93.6 5.8 %collective-permute-start.4 = (s16[104,1536]{1,0:T(8,128)(2,1)S(1)}, s16[104,1536]{1,0:T(8,128)(2,1)S(1)}, u32[]{:S(2)}, u32[]{:S(2)}) collective-permute-start(s16[104,1536]{1,0:T(8,128)(2,1)S(1)} %get-tuple-element.34), channel_id=1, source_target_pairs={{0,16},{16,32},{32,48},{48,64},{64,80},{80,96},{96,112},{112,128},... | collective-permute-start | bytes 958472 | tf_op jit(solution)/shard_map/ppermute | solution.py:479
  95.2 6.7 %collective-permute-start.5 = (s16[104,1536]{1,0:T(8,128)(2,1)S(1)}, s16[104,1536]{1,0:T(8,128)(2,1)S(1)}, u32[]{:S(2)}, u32[]{:S(2)}) collective-permute-start(s16[104,1536]{1,0:T(8,128)(2,1)S(1)} %get-tuple-element.35), channel_id=1, source_target_pairs={{0,240},{16,0},{32,16},{48,32},{64,48},{80,64},{96,80},{112,96},{1... | collective-permute-start | bytes 958472 | tf_op jit(solution)/shard_map/ppermute | solution.py:479
  102.8 12.0 %copy-start.9 = (bf16[128,64]{1,0:T(8,128)(2,1)S(1)}, bf16[128,64]{1,0:T(8,128)(2,1)}, u32[]{:S(2)}) copy-start(bf16[128,64]{1,0:T(8,128)(2,1)} %constant.33.clone.select_ref) | copy-start | bytes 49156
  102.8 12.0 %collective-permute-start.6 = (s16[72,1536]{1,0:T(8,128)(2,1)S(1)}, s16[72,1536]{1,0:T(8,128)(2,1)S(1)}, u32[]{:S(2)}, u32[]{:S(2)}) collective-permute-start(s16[72,1536]{1,0:T(8,128)(2,1)S(1)} %get-tuple-element.36), channel_id=1, source_target_pairs={{0,1},{1,2},{2,3},{3,4},{4,5},{5,6},{6,7},{7,8},{8,9},{9,10},{10,1... | collective-permute-start | bytes 663560 | tf_op jit(solution)/shard_map/ppermute | solution.py:479
  105.6 9.1 %collective-permute-start.7 = (s16[72,1536]{1,0:T(8,128)(2,1)S(1)}, s16[72,1536]{1,0:T(8,128)(2,1)S(1)}, u32[]{:S(2)}, u32[]{:S(2)}) collective-permute-start(s16[72,1536]{1,0:T(8,128)(2,1)S(1)} %get-tuple-element.37), channel_id=1, source_target_pairs={{0,15},{1,0},{2,1},{3,2},{4,3},{5,4},{6,5},{7,6},{8,7},{9,8},{10,9... | collective-permute-start | bytes 663560 | tf_op jit(solution)/shard_map/ppermute | solution.py:479
  114.8 1.4 %copy-start.5 = (f32[256,1536]{1,0:T(8,128)S(1)}, f32[256,1536]{1,0:T(8,128)}, u32[]{:S(2)}) copy-start(f32[256,1536]{1,0:T(8,128)} %get-tuple-element.32.own_ref) | copy-start | bytes 4718596

commit v8 on v7

--- a/solution.py
+++ b/solution.py
@@ -246,7 +246,6 @@
 
 
 def own_kernel(
-    ready,
     live_ref,
     query_ref,
     out_grad_ref,
@@ -264,7 +263,6 @@
     live = jnp.where(rows < OWN, live_ref[4].astype(F32), 1.0)
 
     def load(h):
-        ready(h)
         cols = columns(h)
         k = jnp.concatenate([keys_ref[:, cols], text_key_ref[:, cols]], axis=0)
         v = jnp.concatenate([values_ref[:, cols], text_value_ref[:, cols]], axis=0)
@@ -273,8 +271,7 @@
 
     def store(h, q, g, k, probs, score_grad):
         cols = columns(h)
-        query_grad = part_ref[:, cols] + tn(score_grad, k)
-        query_grad_ref[:, cols] = (query_grad * SCALE).astype(BF16)
+        query_grad_ref[:, cols] = part_ref[:, cols] + tn(score_grad, k)
         own_ref[:OWN, cols] = nn(score_grad[:OWN], q) * SCALE
         own_ref[OWN:, cols] = nn(probs[:OWN], g)
 
@@ -309,7 +306,6 @@
         (stats_ref, query_ref, out_grad_ref, top_ref, bottom_ref, part_ref),
         (top_grad_ref, bottom_grad_ref, query_grad_ref),
         jnp.concatenate(lives, axis=0),
-        True,
     )
 
 
@@ -327,13 +323,12 @@
     lives = jnp.where(rows < SIDE, live_ref[3].astype(F32), live_ref[5].astype(F32))
     two_halves(
         (stats_ref, query_ref, out_grad_ref, left_ref, right_ref, None),
-        (side_grad_ref.at[: 2 * SIDE], side_grad_ref.at[2 * SIDE :], query_grad_ref),
+        (side_grad_ref.at[: 2 * SIDE + 8], side_grad_ref.at[2 * SIDE + 8 :], query_grad_ref),
         lives,
-        False,
-    )
-
-
-def two_halves(given, made, live, code):
+    )
+
+
+def two_halves(given, made, live):
     stats_ref, query_ref, out_grad_ref, first_ref, second_ref, part_ref = given
     first_grad_ref, second_grad_ref, query_grad_ref = made
     rows = first_ref.shape[0] // 2
@@ -350,18 +345,17 @@
     def store(h, q, g, k, probs, score_grad):
         cols = columns(h)
         query_grad = tn(score_grad, k)
-        query_grad_ref[:, cols] = query_grad if part_ref is None else part_ref[:, cols] + query_grad
+        if part_ref is not None:
+            query_grad = ((part_ref[:, cols] + query_grad) * SCALE).astype(BF16)
+        query_grad_ref[:, cols] = query_grad
         grads = (nn(score_grad, q) * SCALE, nn(probs, g))
         for n, ref in enumerate((first_grad_ref, second_grad_ref)):
             levels = []
             for at, grad in ((slice(0, rows), grads[0]), (slice(rows, 2 * rows), grads[1])):
-                block = grad[n * rows : (n + 1) * rows]
-                if code:
-                    block, level = coded(block)
-                    levels.append(level)
-                ref[at, cols] = block
-            if code:
-                ref[2 * rows :, cols] = levels_of(levels)
+                code, level = coded(grad[n * rows : (n + 1) * rows])
+                ref[at, cols] = code
+                levels.append(level)
+            ref[2 * rows :, cols] = levels_of(levels)
 
     backward(load, store, live)
 
@@ -380,7 +374,8 @@
         bands = [received(ref, part, ENDS) for ref in (above_ref, below_ref)]
         more = picked(select_ref[...], jnp.concatenate(bands, axis=0))
         for n, out in enumerate((left_out_ref, right_out_ref)):
-            here = sides_ref[(2 * n + part) * SIDE : (2 * n + part + 1) * SIDE, :]
+            rows = 2 * SIDE + 8
+            here = received(sides_ref.at[n * rows : (n + 1) * rows], part, SIDE)
             code, level = coded(here + more[n * SIDE : (n + 1) * SIDE])
             out[side, :] = code
             levels[n].append(level)
@@ -537,14 +532,21 @@
     from_above = shifted(bottom, HA, 1)
     side_grad, part = call(
         side_kernel,
-        [((4 * SIDE, width), F32), ((OWN, width), F32)],
+        [((4 * SIDE + 16, width), I16), ((OWN, width), F32)],
         [live, stats, q, g, from_left, from_right],
         us=2,
         smem=1,
     )
-    top_grad, bottom_grad, part = call(
+    part, own = call(
+        own_kernel,
+        [((OWN, width), F32), ((2 * OWN, width), F32)],
+        [live, q, g, k, v, text_keys, text_values, stats, part],
+        us=3,
+        smem=1,
+    )
+    top_grad, bottom_grad, query_grad = call(
         band_kernel,
-        [((2 * ENDS + 8, width), I16)] * 2 + [((OWN, width), F32)],
+        [((2 * ENDS + 8, width), I16)] * 2 + [((OWN, width), BF16)],
         [live, stats, q, g, from_above, from_below, part],
         us=2,
         smem=1,
@@ -559,14 +561,6 @@
     )
     after = shifted(left_grad, WA, -1)
     before = shifted(right_grad, WA, 1)
-    query_grad, own = call(
-        own_kernel,
-        [((OWN, width), BF16), ((2 * OWN, width), F32)],
-        [live, q, g, k, v, text_keys, text_values, stats, part],
-        us=3,
-        smem=1,
-        fetch=6,
-    )
     back = np.concatenate([SIDES[0].T, SIDES[1].T], axis=1)
     key_grad, value_grad = call(
         sum_kernel,

time: 120 us -> 118 us (0.983); the launches traced: 118 us -> 118 us
  waiting for transfers between devices: 17.5 us -> 21.5 us
  local copies, waits for them, and re-layouts: 2.72 us -> 0.41 us
  Pallas kernels: 17.2 us -> 15.2 us
    ppermute x8, waiting for transfers between devices: 6.72 us -> 11.4 us  [shifted(): lax.ppermute(value, axis, [(i, (i + steps) % count) for i in range(count)])]
    unnamed x26 -> x24, local copies, waits for them, and re-layouts: 2.38 us -> 0.07 us
    pallas_call x11, Pallas kernels: 17.2 us -> 15.2 us  [call(): pl.pallas_call(function, out_shape=[jax.ShapeDtypeStruct(shape, dtype) fo...]
  transfers between devices with their start and end apart: 11 -> 11, of which waited for: 4 -> 6; matrix products, arithmetic and copies ran while one was open for 0% -> 0% of each run, Pallas kernels for 11% -> 10%
where the time goes in v8:
time: 118 us
  starting transfers between devices  80 us (68%)
  waiting for transfers between devices  21.5 us (18%)
  Pallas kernels  15.2 us (13%)
    all_to_all x3, starting transfers between devices, exchanged(): return lax.all_to_all(pieces, axis, 0, 0, tiled=True)  59.4 us
    ppermute x8, starting transfers between devices, shifted(): lax.ppermute(value, axis, [(i, (i + steps) % count) for i in range(count)])  20.6 us
    pallas_call x11, Pallas kernels, call(): pl.pallas_call(function, out_shape=[jax.ShapeDtypeStruct(shape, dtype) fo...  15.2 us
    ppermute x8, waiting for transfers between devices, shifted(): lax.ppermute(value, axis, [(i, (i + steps) % count) for i in range(count)])  11.4 us
    all_to_all x3, waiting for transfers between devices, exchanged(): return lax.all_to_all(pieces, axis, 0, 0, tiled=True)  10 us
  transfers between devices with their start and end apart: 11, of which 6 were waited for; matrix products, arithmetic and copies ran while one was open for 0% of the time, Pallas kernels for 10%

profile of v8, /device:TPU:65, one launch (start us, length us, event | category | flops | bytes accessed | tf_op | source)
XLA Modules:
  0.0 117.9 jit_solution(7189882842954315142)
XLA Ops:
  0.6 0.0 copy-start
  0.6 0.0 copy-start.11
  0.7 0.0 copy-start.8
  0.7 3.2 %shard_map.164 = (s16[1024,128]{1,0:T(8,128)(2,1)}, f32[32,128]{1,0:T(8,128)}) custom-call(f32[128,12]{1,0:T(8,128)} %bitcast.29, f32[128,12]{1,0:T(8,128)} %bitcast.30, bf16[128,1536]{1,0:T(8,128)(2,1)} %bitcast.14, bf16[128,1536]{1,0:T(8,128)(2,1)} %bitcast.18, bf16[32,1536]{1,0:T(8,128)(2,1)} %text_key_ref.1, bf16[32,1536]{1,0:T(8,128)(2,1)} %text_value_ref.1), custom_call_target="tpu_custom_call" | custom-call | flops 150000000 | bytes 1000000 | tf_op jit(solution)/shard_map/pallas_call | solution.py:459
  3.9 45.2 %all-to-all-start = ((s16[32,32,128]{2,1,0:T(8,128)(2,1)}), s16[32,32,128]{2,1,0:T(8,128)(2,1)S(1)}, u32[]{:S(2)}, u32[]{:S(2)}) async-start(s16[32,32,128]{2,1,0:T(8,128)(2,1)} %bitcast.28), calls=%async_computation | async-start | bytes 524288 | tf_op jit(solution)/shard_map/all_to_all | solution.py:482
  49.2 0.3 shard_map.165
  49.6 3.3 %collective-permute-start = (bf16[64,1536]{1,0:T(8,128)(2,1)S(1)}, bf16[64,1536]{1,0:T(8,128)(2,1)S(1)}, u32[]{:S(2)}, u32[]{:S(2)}) collective-permute-start(bf16[64,1536]{1,0:T(8,128)(2,1)S(1)} %get-tuple-element.25), channel_id=1, source_target_pairs={{0,1},{1,2},{2,3},{3,4},{4,5},{5,6},{6,7},{7,8},{8,9},{9,10},{10,1... | collective-permute-start | bytes 589832 | tf_op jit(solution)/shard_map/ppermute | solution.py:474
  52.9 7.4 %collective-permute-start.1 = (bf16[64,1536]{1,0:T(8,128)(2,1)S(1)}, bf16[64,1536]{1,0:T(8,128)(2,1)S(1)}, u32[]{:S(2)}, u32[]{:S(2)}) collective-permute-start(bf16[64,1536]{1,0:T(8,128)(2,1)S(1)} %get-tuple-element.26), channel_id=1, source_target_pairs={{0,15},{1,0},{2,1},{3,2},{4,3},{5,4},{6,5},{7,6},{8,7},{9,8},{10,9... | collective-permute-start | bytes 589832 | tf_op jit(solution)/shard_map/ppermute | solution.py:474
  60.3 0.5 all-to-all-done.parts_ref
  60.7 0.8 shard_map.172
  61.5 7.6 %all-to-all-start.1 = ((s16[8,32,128]{2,1,0:T(8,128)(2,1)}), s16[8,32,128]{2,1,0:T(8,128)(2,1)S(1)}, u32[]{:S(2)}, u32[]{:S(2)}) async-start(s16[8,32,128]{2,1,0:T(8,128)(2,1)} %shard_map.172), calls=%async_computation.1 | async-start | bytes 131072 | tf_op jit(solution)/shard_map/all_to_all | solution.py:482
  69.2 1.2 %shard_map.166 = (bf16[96,1536]{1,0:T(8,128)(2,1)S(1)}, bf16[96,1536]{1,0:T(8,128)(2,1)}) custom-call(bf16[2,48,192]{2,1,0:T(8,128)(2,1)S(1)} %copy-done.8, bf16[128,1536]{1,0:T(8,128)(2,1)S(1)} %bitcast.23, bf16[128,1536]{1,0:T(8,128)(2,1)S(1)} %bitcast.26, bf16[64,1536]{1,0:T(8,128)(2,1)S(1)} %collective-permute-done.left_ref, ...), custom_call_target="tpu_custom_call" | custom-call | flops 50000000 | bytes 1000000 | tf_op jit(solution)/shard_map/pallas_call | solution.py:459
  70.4 1.7 %collective-permute-start.2 = (bf16[96,1536]{1,0:T(8,128)(2,1)}, bf16[96,1536]{1,0:T(8,128)(2,1)S(1)}, u32[]{:S(2)}, u32[]{:S(2)}) collective-permute-start(bf16[96,1536]{1,0:T(8,128)(2,1)} %get-tuple-element.27), channel_id=1, source_target_pairs={{0,16},{16,32},{32,48},{48,64},{64,80},{80,96},{96,112},{112,128},... | collective-permute-start | bytes 884744 | tf_op jit(solution)/shard_map/ppermute | solution.py:474
  72.1 9.6 %all-to-all-done.1.parts_ref = s16[8,32,128]{2,1,0:T(8,128)(2,1)S(1)} async-done(((s16[8,32,128]{2,1,0:T(8,128)(2,1)}), s16[8,32,128]{2,1,0:T(8,128)(2,1)S(1)}, u32[]{:S(2)}, u32[]{:S(2)}) %all-to-all-start.1) | async-done | bytes 65568 | tf_op jit(solution)/shard_map/all_to_all | solution.py:482
  81.6 0.7 shard_map.173
  82.3 6.6 %all-to-all-start.2 = ((bf16[32,24,128]{2,1,0:T(8,128)(2,1)}), bf16[32,24,128]{2,1,0:T(8,128)(2,1)S(1)}, u32[]{:S(2)}, u32[]{:S(2)}) async-start(bf16[32,24,128]{2,1,0:T(8,128)(2,1)} %shard_map.173), calls=%async_computation.2 | async-start | bytes 393216 | tf_op jit(solution)/shard_map/all_to_all | solution.py:482
  88.9 0.3 dynamic-slice_reduce_fusion.live_ref
  89.3 1.6 %shard_map.167 = (s16[144,1536]{1,0:T(8,128)(2,1)S(1)}, f32[128,1536]{1,0:T(8,128)S(1)}) custom-call(s32[9]{0:T(128)S(1)} %dynamic-slice_reduce_fusion.live_ref, f32[32,128]{1,0:T(8,128)S(1)} %copy-done.7, bf16[128,1536]{1,0:T(8,128)(2,1)S(1)} %bitcast.15, bf16[128,1536]{1,0:T(8,128)(2,1)S(1)} %bitcast.19, ...), custom_call_target="tpu_custom_call" | custom-call | flops 100000000 | bytes 1000000 | tf_op jit(solution)/shard_map/pallas_call | solution.py:459
  90.9 1.7 %shard_map.168 = (f32[128,1536]{1,0:T(8,128)S(1)}, f32[256,1536]{1,0:T(8,128)S(1)}) custom-call(s32[9]{0:T(128)S(1)} %dynamic-slice_reduce_fusion.live_ref, bf16[128,1536]{1,0:T(8,128)(2,1)S(1)} %bitcast.16, bf16[128,1536]{1,0:T(8,128)(2,1)S(1)} %bitcast.20, bf16[128,1536]{1,0:T(8,128)(2,1)S(1)} %bitcast.24, bf16[128,1536]{1,0:T(8,128)(2,1)S(1)} %bitcast.27, ...), custom_call_target="tpu_custom_call" | custom-call | flops 150000000 | bytes 1000000 | tf_op jit(solution)/shard_map/pallas_call | solution.py:459
  92.6 0.0 copy-start.10
  92.6 0.0 copy-start.9
  92.7 2.5 %shard_map.169 = (s16[104,1536]{1,0:T(8,128)(2,1)S(1)}, s16[104,1536]{1,0:T(8,128)(2,1)S(1)}, bf16[128,1536]{1,0:T(8,128)(2,1)}) custom-call(s32[9]{0:T(128)S(1)} %dynamic-slice_reduce_fusion.live_ref, f32[32,128]{1,0:T(8,128)S(1)} %copy-done.7, bf16[128,1536]{1,0:T(8,128)(2,1)S(1)} %bitcast.17, bf16[128,1536]{1,0:T(8,128)(2,1)S(1)} %bitcast.21, ...), custom_call_target="tpu_custom_call" | custom-call | flops 100000000 | bytes 1000000 | tf_op jit(solution)/shard_map/pallas_call | solution.py:459
  95.2 1.7 %collective-permute-start.4 = (s16[104,1536]{1,0:T(8,128)(2,1)S(1)}, s16[104,1536]{1,0:T(8,128)(2,1)S(1)}, u32[]{:S(2)}, u32[]{:S(2)}) collective-permute-start(s16[104,1536]{1,0:T(8,128)(2,1)S(1)} %get-tuple-element.34), channel_id=1, source_target_pairs={{0,16},{16,32},{32,48},{48,64},{64,80},{80,96},{96,112},{112,128},... | collective-permute-start | bytes 958472 | tf_op jit(solution)/shard_map/ppermute | solution.py:474
  96.9 3.9 %collective-permute-done.4.above_ref = s16[104,1536]{1,0:T(8,128)(2,1)S(1)} collective-permute-done((s16[104,1536]{1,0:T(8,128)(2,1)S(1)}, s16[104,1536]{1,0:T(8,128)(2,1)S(1)}, u32[]{:S(2)}, u32[]{:S(2)}) %collective-permute-start.4) | collective-permute-done | bytes 319520 | tf_op jit(solution)/shard_map/ppermute | solution.py:474
  100.8 2.6 %collective-permute-done.5.below_ref = s16[104,1536]{1,0:T(8,128)(2,1)S(1)} collective-permute-done((s16[104,1536]{1,0:T(8,128)(2,1)S(1)}, s16[104,1536]{1,0:T(8,128)(2,1)S(1)}, u32[]{:S(2)}, u32[]{:S(2)}) %collective-permute-start.5) | collective-permute-done | bytes 319520 | tf_op jit(solution)/shard_map/ppermute | solution.py:474
  103.4 1.0 shard_map.170
  104.4 3.0 %collective-permute-start.6 = (s16[72,1536]{1,0:T(8,128)(2,1)S(1)}, s16[72,1536]{1,0:T(8,128)(2,1)S(1)}, u32[]{:S(2)}, u32[]{:S(2)}) collective-permute-start(s16[72,1536]{1,0:T(8,128)(2,1)S(1)} %get-tuple-element.36), channel_id=1, source_target_pairs={{0,1},{1,2},{2,3},{3,4},{4,5},{5,6},{6,7},{7,8},{8,9},{9,10},{10,1... | collective-permute-start | bytes 663560 | tf_op jit(solution)/shard_map/ppermute | solution.py:474
  107.4 3.6 %collective-permute-start.7 = (s16[72,1536]{1,0:T(8,128)(2,1)S(1)}, s16[72,1536]{1,0:T(8,128)(2,1)S(1)}, u32[]{:S(2)}, u32[]{:S(2)}) collective-permute-start(s16[72,1536]{1,0:T(8,128)(2,1)S(1)} %get-tuple-element.37), channel_id=1, source_target_pairs={{0,15},{1,0},{2,1},{3,2},{4,3},{5,4},{6,5},{7,6},{8,7},{9,8},{10,9... | collective-permute-start | bytes 663560 | tf_op jit(solution)/shard_map/ppermute | solution.py:474
  111.0 3.2 %collective-permute-done.6.left_ref = s16[72,1536]{1,0:T(8,128)(2,1)S(1)} collective-permute-done((s16[72,1536]{1,0:T(8,128)(2,1)S(1)}, s16[72,1536]{1,0:T(8,128)(2,1)S(1)}, u32[]{:S(2)}, u32[]{:S(2)}) %collective-permute-start.6) | collective-permute-done | bytes 221216 | tf_op jit(solution)/shard_map/ppermute | solution.py:474
  114.1 1.7 %collective-permute-done.7.right_ref = s16[72,1536]{1,0:T(8,128)(2,1)S(1)} collective-permute-done((s16[72,1536]{1,0:T(8,128)(2,1)S(1)}, s16[72,1536]{1,0:T(8,128)(2,1)S(1)}, u32[]{:S(2)}, u32[]{:S(2)}) %collective-permute-start.7) | collective-permute-done | bytes 221216 | tf_op jit(solution)/shard_map/ppermute | solution.py:474
  115.8 1.4 %shard_map.171 = (bf16[128,1536]{1,0:T(8,128)(2,1)}, bf16[128,1536]{1,0:T(8,128)(2,1)}) custom-call(bf16[128,64]{1,0:T(8,128)(2,1)S(1)} %copy-done.9, f32[256,1536]{1,0:T(8,128)S(1)} %get-tuple-element.32.own_ref, s16[72,1536]{1,0:T(8,128)(2,1)S(1)} %collective-permute-done.6.left_ref, s16[72,1536]{1,0:T(8,128)(2,1)S(1)} %collective-permute-done.7.right_ref, ...), custom_call_target="tpu_custom_call" | custom-call | flops 50000000 | bytes 1000000 | tf_op jit(solution)/shard_map/pallas_call | solution.py:459
  117.2 0.7 shard_map.174
  (26 shorter events, 0.1 us)
Async XLA Ops:
  0.6 88.3 %copy-start = (s32[16,16,9]{1,0,2:T(8,128)S(1)}, s32[16,16,9]{1,0,2:T(8,128)}, u32[]{:S(2)}) copy-start(s32[16,16,9]{1,0,2:T(8,128)} %param.21) | copy-start | bytes 27652
  0.6 48.5 %copy-start.11 = (bf16[2,32,128]{2,1,0:T(8,128)(2,1)S(1)}, bf16[2,32,128]{2,1,0:T(8,128)(2,1)}, u32[]{:S(2)}) copy-start(bf16[2,32,128]{2,1,0:T(8,128)(2,1)} %constant.30.clone.select_ref) | copy-start | bytes 49156
  0.7 68.5 %copy-start.8 = (bf16[2,48,192]{2,1,0:T(8,128)(2,1)S(1)}, bf16[2,48,192]{2,1,0:T(8,128)(2,1)}, u32[]{:S(2)}) copy-start(bf16[2,48,192]{2,1,0:T(8,128)(2,1)} %constant.31.clone.select_ref) | copy-start | bytes 110596
  0.7 48.5 %copy-start.4 = (bf16[2,8,8,1536]{3,2,1,0:T(8,128)(2,1)S(1)}, bf16[2,8,8,1536]{3,2,1,0:T(8,128)(2,1)}, u32[]{:S(2)}) copy-start(bf16[2,8,8,1536]{3,2,1,0:T(8,128)(2,1)} %param.15) | copy-start | bytes 1179652
  0.7 48.5 %copy-start.3 = (bf16[2,8,8,1536]{3,2,1,0:T(8,128)(2,1)S(1)}, bf16[2,8,8,1536]{3,2,1,0:T(8,128)(2,1)}, u32[]{:S(2)}) copy-start(bf16[2,8,8,1536]{3,2,1,0:T(8,128)(2,1)} %param.14) | copy-start | bytes 1179652
  3.9 56.8 %all-to-all-start = ((s16[32,32,128]{2,1,0:T(8,128)(2,1)}), s16[32,32,128]{2,1,0:T(8,128)(2,1)S(1)}, u32[]{:S(2)}, u32[]{:S(2)}) async-start(s16[32,32,128]{2,1,0:T(8,128)(2,1)} %bitcast.28), calls=%async_computation | async-start | bytes 524288 | tf_op jit(solution)/shard_map/all_to_all | solution.py:482
  49.2 40.1 %copy-start.1 = (bf16[2,8,8,1536]{3,2,1,0:T(8,128)(2,1)S(1)}, bf16[2,8,8,1536]{3,2,1,0:T(8,128)(2,1)}, u32[]{:S(2)}) copy-start(bf16[2,8,8,1536]{3,2,1,0:T(8,128)(2,1)} %param.13) | copy-start | bytes 1179652
  49.2 40.1 %copy-start.2 = (bf16[2,8,8,1536]{3,2,1,0:T(8,128)(2,1)S(1)}, bf16[2,8,8,1536]{3,2,1,0:T(8,128)(2,1)}, u32[]{:S(2)}) copy-start(bf16[2,8,8,1536]{3,2,1,0:T(8,128)(2,1)} %param.16) | copy-start | bytes 1179652
  49.2 40.1 %copy-start.7 = (f32[32,128]{1,0:T(8,128)S(1)}, f32[32,128]{1,0:T(8,128)}, u32[]{:S(2)}) copy-start(f32[32,128]{1,0:T(8,128)} %get-tuple-element.24.stats_ref) | copy-start | bytes 49156
  49.6 19.6 %collective-permute-start = (bf16[64,1536]{1,0:T(8,128)(2,1)S(1)}, bf16[64,1536]{1,0:T(8,128)(2,1)S(1)}, u32[]{:S(2)}, u32[]{:S(2)}) collective-permute-start(bf16[64,1536]{1,0:T(8,128)(2,1)S(1)} %get-tuple-element.25), channel_id=1, source_target_pairs={{0,1},{1,2},{2,3},{3,4},{4,5},{5,6},{6,7},{7,8},{8,9},{9,10},{10,1... | collective-permute-start | bytes 589832 | tf_op jit(solution)/shard_map/ppermute | solution.py:474
  52.9 16.3 %collective-permute-start.1 = (bf16[64,1536]{1,0:T(8,128)(2,1)S(1)}, bf16[64,1536]{1,0:T(8,128)(2,1)S(1)}, u32[]{:S(2)}, u32[]{:S(2)}) collective-permute-start(bf16[64,1536]{1,0:T(8,128)(2,1)S(1)} %get-tuple-element.26), channel_id=1, source_target_pairs={{0,15},{1,0},{2,1},{3,2},{4,3},{5,4},{6,5},{7,6},{8,7},{9,8},{10,9... | collective-permute-start | bytes 589832 | tf_op jit(solution)/shard_map/ppermute | solution.py:474
  61.5 20.1 %all-to-all-start.1 = ((s16[8,32,128]{2,1,0:T(8,128)(2,1)}), s16[8,32,128]{2,1,0:T(8,128)(2,1)S(1)}, u32[]{:S(2)}, u32[]{:S(2)}) async-start(s16[8,32,128]{2,1,0:T(8,128)(2,1)} %shard_map.172), calls=%async_computation.1 | async-start | bytes 131072 | tf_op jit(solution)/shard_map/all_to_all | solution.py:482
  69.1 21.8 %copy-start.5 = (bf16[32,1536]{1,0:T(8,128)(2,1)S(1)}, bf16[32,1536]{1,0:T(8,128)(2,1)}, u32[]{:S(2)}) copy-start(bf16[32,1536]{1,0:T(8,128)(2,1)} %text_key_ref.1) | copy-start | bytes 294916
  69.1 21.8 %copy-start.6 = (bf16[32,1536]{1,0:T(8,128)(2,1)S(1)}, bf16[32,1536]{1,0:T(8,128)(2,1)}, u32[]{:S(2)}) copy-start(bf16[32,1536]{1,0:T(8,128)(2,1)} %text_value_ref.1) | copy-start | bytes 294916
  70.4 22.2 %collective-permute-start.2 = (bf16[96,1536]{1,0:T(8,128)(2,1)}, bf16[96,1536]{1,0:T(8,128)(2,1)S(1)}, u32[]{:S(2)}, u32[]{:S(2)}) collective-permute-start(bf16[96,1536]{1,0:T(8,128)(2,1)} %get-tuple-element.27), channel_id=1, source_target_pairs={{0,16},{16,32},{32,48},{48,64},{64,80},{80,96},{96,112},{112,128},... | collective-permute-start | bytes 884744 | tf_op jit(solution)/shard_map/ppermute | solution.py:474
  72.1 20.6 %collective-permute-start.3 = (bf16[96,1536]{1,0:T(8,128)(2,1)S(1)}, bf16[96,1536]{1,0:T(8,128)(2,1)S(1)}, u32[]{:S(2)}, u32[]{:S(2)}) collective-permute-start(bf16[96,1536]{1,0:T(8,128)(2,1)S(1)} %get-tuple-element.28), channel_id=1, source_target_pairs={{0,240},{16,0},{32,16},{48,32},{64,48},{80,64},{96,80},{112,96},{1... | collective-permute-start | bytes 884744 | tf_op jit(solution)/shard_map/ppermute | solution.py:474
  82.3 34.9 %all-to-all-start.2 = ((bf16[32,24,128]{2,1,0:T(8,128)(2,1)}), bf16[32,24,128]{2,1,0:T(8,128)(2,1)S(1)}, u32[]{:S(2)}, u32[]{:S(2)}) async-start(bf16[32,24,128]{2,1,0:T(8,128)(2,1)} %shard_map.173), calls=%async_computation.2 | async-start | bytes 393216 | tf_op jit(solution)/shard_map/all_to_all | solution.py:482
  92.6 10.8 %copy-start.10 = (bf16[64,96]{1,0:T(8,128)(2,1)S(1)}, bf16[64,96]{1,0:T(8,128)(2,1)}, u32[]{:S(2)}) copy-start(bf16[64,96]{1,0:T(8,128)(2,1)} %constant.32.clone.select_ref) | copy-start | bytes 36868
  92.6 23.2 %copy-start.9 = (bf16[128,64]{1,0:T(8,128)(2,1)S(1)}, bf16[128,64]{1,0:T(8,128)(2,1)}, u32[]{:S(2)}) copy-start(bf16[128,64]{1,0:T(8,128)(2,1)} %constant.33.clone.select_ref) | copy-start | bytes 49156
  95.2 5.6 %collective-permute-start.4 = (s16[104,1536]{1,0:T(8,128)(2,1)S(1)}, s16[104,1536]{1,0:T(8,128)(2,1)S(1)}, u32[]{:S(2)}, u32[]{:S(2)}) collective-permute-start(s16[104,1536]{1,0:T(8,128)(2,1)S(1)} %get-tuple-element.34), channel_id=1, source_target_pairs={{0,16},{16,32},{32,48},{48,64},{64,80},{80,96},{96,112},{112,128},... | collective-permute-start | bytes 958472 | tf_op jit(solution)/shard_map/ppermute | solution.py:474
  96.8 6.6 %collective-permute-start.5 = (s16[104,1536]{1,0:T(8,128)(2,1)S(1)}, s16[104,1536]{1,0:T(8,128)(2,1)S(1)}, u32[]{:S(2)}, u32[]{:S(2)}) collective-permute-start(s16[104,1536]{1,0:T(8,128)(2,1)S(1)} %get-tuple-element.35), channel_id=1, source_target_pairs={{0,240},{16,0},{32,16},{48,32},{64,48},{80,64},{96,80},{112,96},{1... | collective-permute-start | bytes 958472 | tf_op jit(solution)/shard_map/ppermute | solution.py:474
  104.4 9.7 %collective-permute-start.6 = (s16[72,1536]{1,0:T(8,128)(2,1)S(1)}, s16[72,1536]{1,0:T(8,128)(2,1)S(1)}, u32[]{:S(2)}, u32[]{:S(2)}) collective-permute-start(s16[72,1536]{1,0:T(8,128)(2,1)S(1)} %get-tuple-element.36), channel_id=1, source_target_pairs={{0,1},{1,2},{2,3},{3,4},{4,5},{5,6},{6,7},{7,8},{8,9},{9,10},{10,1... | collective-permute-start | bytes 663560 | tf_op jit(solution)/shard_map/ppermute | solution.py:474
  107.4 8.4 %collective-permute-start.7 = (s16[72,1536]{1,0:T(8,128)(2,1)S(1)}, s16[72,1536]{1,0:T(8,128)(2,1)S(1)}, u32[]{:S(2)}, u32[]{:S(2)}) collective-permute-start(s16[72,1536]{1,0:T(8,128)(2,1)S(1)} %get-tuple-element.37), channel_id=1, source_target_pairs={{0,15},{1,0},{2,1},{3,2},{4,3},{5,4},{6,5},{7,6},{8,7},{9,8},{10,9... | collective-permute-start | bytes 663560 | tf_op jit(solution)/shard_map/ppermute | solution.py:474

commit v9 on v8

--- a/solution.py
+++ b/solution.py
@@ -256,7 +256,8 @@
     stats_ref,
     part_ref,
     query_grad_ref,
-    own_ref,
+    own_key_ref,
+    own_value_ref,
 ):
     text = text_key_ref.shape[0]
     rows = lax.broadcasted_iota(jnp.int32, (OWN + text, HDIM), 0)
@@ -272,8 +273,8 @@
     def store(h, q, g, k, probs, score_grad):
         cols = columns(h)
         query_grad_ref[:, cols] = part_ref[:, cols] + tn(score_grad, k)
-        own_ref[:OWN, cols] = nn(score_grad[:OWN], q) * SCALE
-        own_ref[OWN:, cols] = nn(probs[:OWN], g)
+        own_key_ref[:, cols] = nn(score_grad[:OWN], q) * SCALE
+        own_value_ref[:, cols] = nn(probs[:OWN], g)
 
     backward(load, store, live)
 
@@ -383,25 +384,26 @@
     right_out_ref[2 * SIDE :, :] = levels_of(levels[1])
 
 
-def sum_kernel(
-    select_ref, own_ref, left_ref, right_ref, above_ref, below_ref, key_ref, value_ref
-):
+def bands_kernel(above_ref, below_ref, own_key_ref, own_value_ref, key_ref, value_ref):
     edge = HALO * TILE
-    for part, out in enumerate((key_ref, value_ref)):
+    refs = ((own_key_ref, key_ref), (own_value_ref, value_ref))
+    for part, (own_ref, out_ref) in enumerate(refs):
         above, below = received(above_ref, part, ENDS), received(below_ref, part, ENDS)
-        sides = [received(ref, part, SIDE) for ref in (left_ref, right_ref)]
-        rows = jnp.concatenate(sides, axis=0)
-        total = own_ref[part * OWN : (part + 1) * OWN, :] + picked(select_ref[...], rows)
         for frame in range(FRAMES):
             at = frame * BAND
-            top = frame * TILE * TILE
-            bottom = top + TILE * TILE - edge
-            end = top + TILE * TILE
-            out[top : top + edge, :] = (
-                total[top : top + edge] + above[at : at + edge]
-            ).astype(BF16)
-            out[top + edge : bottom, :] = total[top + edge : bottom].astype(BF16)
-            out[bottom:end, :] = (total[bottom:end] + below[at : at + edge]).astype(BF16)
+            top, end = frame * TILE * TILE, (frame + 1) * TILE * TILE
+            bottom = end - edge
+            out_ref[top : top + edge, :] = own_ref[top : top + edge, :] + above[at : at + edge]
+            out_ref[top + edge : bottom, :] = own_ref[top + edge : bottom, :]
+            out_ref[bottom:end, :] = own_ref[bottom:end, :] + below[at : at + edge]
+
+
+def sum_kernel(select_ref, own_key_ref, own_value_ref, left_ref, right_ref, key_ref, value_ref):
+    refs = ((own_key_ref, key_ref), (own_value_ref, value_ref))
+    for part, (own_ref, out_ref) in enumerate(refs):
+        sides = [received(ref, part, SIDE) for ref in (left_ref, right_ref)]
+        total = own_ref[...] + picked(select_ref[...], jnp.concatenate(sides, axis=0))
+        out_ref[...] = total.astype(BF16)
 
 
 def words_kernel(parts_ref, key_ref, value_ref):
@@ -537,9 +539,9 @@
         us=2,
         smem=1,
     )
-    part, own = call(
+    part, own_key, own_value = call(
         own_kernel,
-        [((OWN, width), F32), ((2 * OWN, width), F32)],
+        [((OWN, width), F32)] * 3,
         [live, q, g, k, v, text_keys, text_values, stats, part],
         us=3,
         smem=1,
@@ -561,11 +563,14 @@
     )
     after = shifted(left_grad, WA, -1)
     before = shifted(right_grad, WA, 1)
+    own_key, own_value = call(
+        bands_kernel, [((OWN, width), F32)] * 2, [above, below, own_key, own_value]
+    )
     back = np.concatenate([SIDES[0].T, SIDES[1].T], axis=1)
     key_grad, value_grad = call(
         sum_kernel,
         [((OWN, width), BF16)] * 2,
-        [jnp.asarray(back, BF16), own, before, after, above, below],
+        [jnp.asarray(back, BF16), own_key, own_value, before, after],
     )
     return (
         query_grad.reshape(shape),

time: 118 us -> 119 us (level)
    pallas_call x11 -> x12, Pallas kernels: 15.2 us -> 14.6 us  [call(): pl.pallas_call(function, out_shape=[jax.ShapeDtypeStruct(shape, dtype) fo...]
  transfers between devices with their start and end apart: 11 -> 11, of which waited for: 6 -> 6; matrix products, arithmetic and copies ran while one was open for 0% -> 0% of each run, Pallas kernels for 10% -> 9%
where the time goes in v9:
time: 119 us
  starting transfers between devices  80.3 us (67%)
  waiting for transfers between devices  22.1 us (19%)
  Pallas kernels  14.6 us (12%)
    all_to_all x3, starting transfers between devices, exchanged(): return lax.all_to_all(pieces, axis, 0, 0, tiled=True)  59.7 us
    ppermute x8, starting transfers between devices, shifted(): lax.ppermute(value, axis, [(i, (i + steps) % count) for i in range(count)])  20.6 us
    pallas_call x12, Pallas kernels, call(): pl.pallas_call(function, out_shape=[jax.ShapeDtypeStruct(shape, dtype) fo...  14.6 us
    ppermute x8, waiting for transfers between devices, shifted(): lax.ppermute(value, axis, [(i, (i + steps) % count) for i in range(count)])  11.3 us
    all_to_all x3, waiting for transfers between devices, exchanged(): return lax.all_to_all(pieces, axis, 0, 0, tiled=True)  10.7 us
  transfers between devices with their start and end apart: 11, of which 6 were waited for; matrix products, arithmetic and copies ran while one was open for 0% of the time, Pallas kernels for 9%

profile of v9, /device:TPU:65, one launch (start us, length us, event | category | flops | bytes accessed | tf_op | source)
XLA Modules:
  0.0 118.6 jit_solution(201157340174094997)
XLA Ops:
  0.6 0.0 copy-start
  0.7 3.2 %shard_map.164 = (s16[1024,128]{1,0:T(8,128)(2,1)}, f32[32,128]{1,0:T(8,128)}) custom-call(f32[128,12]{1,0:T(8,128)} %bitcast.29, f32[128,12]{1,0:T(8,128)} %bitcast.30, bf16[128,1536]{1,0:T(8,128)(2,1)} %bitcast.14, bf16[128,1536]{1,0:T(8,128)(2,1)} %bitcast.18, bf16[32,1536]{1,0:T(8,128)(2,1)} %text_key_ref.1, bf16[32,1536]{1,0:T(8,128)(2,1)} %text_value_ref.1), custom_call_target="tpu_custom_call" | custom-call | flops 150000000 | bytes 1000000 | tf_op jit(solution)/shard_map/pallas_call | solution.py:461
  3.9 45.4 %all-to-all-start = ((s16[32,32,128]{2,1,0:T(8,128)(2,1)}), s16[32,32,128]{2,1,0:T(8,128)(2,1)S(1)}, u32[]{:S(2)}, u32[]{:S(2)}) async-start(s16[32,32,128]{2,1,0:T(8,128)(2,1)} %bitcast.28), calls=%async_computation | async-start | bytes 524288 | tf_op jit(solution)/shard_map/all_to_all | solution.py:484
  49.3 0.3 shard_map.165
  49.6 3.3 %collective-permute-start = (bf16[64,1536]{1,0:T(8,128)(2,1)S(1)}, bf16[64,1536]{1,0:T(8,128)(2,1)S(1)}, u32[]{:S(2)}, u32[]{:S(2)}) collective-permute-start(bf16[64,1536]{1,0:T(8,128)(2,1)S(1)} %get-tuple-element.28), channel_id=1, source_target_pairs={{0,1},{1,2},{2,3},{3,4},{4,5},{5,6},{6,7},{7,8},{8,9},{9,10},{10,1... | collective-permute-start | bytes 589832 | tf_op jit(solution)/shard_map/ppermute | solution.py:476
  53.0 7.4 %collective-permute-start.1 = (bf16[64,1536]{1,0:T(8,128)(2,1)S(1)}, bf16[64,1536]{1,0:T(8,128)(2,1)S(1)}, u32[]{:S(2)}, u32[]{:S(2)}) collective-permute-start(bf16[64,1536]{1,0:T(8,128)(2,1)S(1)} %get-tuple-element.29), channel_id=1, source_target_pairs={{0,15},{1,0},{2,1},{3,2},{4,3},{5,4},{6,5},{7,6},{8,7},{9,8},{10,9... | collective-permute-start | bytes 589832 | tf_op jit(solution)/shard_map/ppermute | solution.py:476
  60.3 0.5 all-to-all-done.parts_ref
  60.8 0.8 shard_map.173
  61.6 7.7 %all-to-all-start.1 = ((s16[8,32,128]{2,1,0:T(8,128)(2,1)}), s16[8,32,128]{2,1,0:T(8,128)(2,1)S(1)}, u32[]{:S(2)}, u32[]{:S(2)}) async-start(s16[8,32,128]{2,1,0:T(8,128)(2,1)} %shard_map.173), calls=%async_computation.1 | async-start | bytes 131072 | tf_op jit(solution)/shard_map/all_to_all | solution.py:484
  69.4 0.5 shard_map.166
  69.9 0.0 copy-start.1
  69.9 1.7 %collective-permute-start.2 = (bf16[96,1536]{1,0:T(8,128)(2,1)S(1)}, bf16[96,1536]{1,0:T(8,128)(2,1)S(1)}, u32[]{:S(2)}, u32[]{:S(2)}) collective-permute-start(bf16[96,1536]{1,0:T(8,128)(2,1)S(1)} %get-tuple-element.30), channel_id=1, source_target_pairs={{0,16},{16,32},{32,48},{48,64},{64,80},{80,96},{96,112},{112,128},... | collective-permute-start | bytes 884744 | tf_op jit(solution)/shard_map/ppermute | solution.py:476
  71.6 10.2 %all-to-all-done.1.parts_ref = s16[8,32,128]{2,1,0:T(8,128)(2,1)S(1)} async-done(((s16[8,32,128]{2,1,0:T(8,128)(2,1)}), s16[8,32,128]{2,1,0:T(8,128)(2,1)S(1)}, u32[]{:S(2)}, u32[]{:S(2)}) %all-to-all-start.1) | async-done | bytes 65568 | tf_op jit(solution)/shard_map/all_to_all | solution.py:484
  81.9 0.7 shard_map.174
  82.6 6.6 %all-to-all-start.2 = ((bf16[32,24,128]{2,1,0:T(8,128)(2,1)}), bf16[32,24,128]{2,1,0:T(8,128)(2,1)S(1)}, u32[]{:S(2)}, u32[]{:S(2)}) async-start(bf16[32,24,128]{2,1,0:T(8,128)(2,1)} %shard_map.174), calls=%async_computation.2 | async-start | bytes 393216 | tf_op jit(solution)/shard_map/all_to_all | solution.py:484
  89.2 0.3 dynamic-slice_reduce_fusion.live_ref
  89.5 0.3 copy-done.7
  89.9 1.6 %shard_map.167 = (s16[144,1536]{1,0:T(8,128)(2,1)S(1)}, f32[128,1536]{1,0:T(8,128)S(1)}) custom-call(s32[9]{0:T(128)S(1)} %dynamic-slice_reduce_fusion.live_ref, f32[32,128]{1,0:T(8,128)S(1)} %copy-done.7, bf16[128,1536]{1,0:T(8,128)(2,1)S(1)} %bitcast.15, bf16[128,1536]{1,0:T(8,128)(2,1)S(1)} %bitcast.19, ...), custom_call_target="tpu_custom_call" | custom-call | flops 100000000 | bytes 1000000 | tf_op jit(solution)/shard_map/pallas_call | solution.py:461
  91.5 1.7 %shard_map.168 = (f32[128,1536]{1,0:T(8,128)S(1)}, f32[128,1536]{1,0:T(8,128)S(1)}, f32[128,1536]{1,0:T(8,128)S(1)}) custom-call(s32[9]{0:T(128)S(1)} %dynamic-slice_reduce_fusion.live_ref, bf16[128,1536]{1,0:T(8,128)(2,1)S(1)} %bitcast.16, bf16[128,1536]{1,0:T(8,128)(2,1)S(1)} %bitcast.20, bf16[128,1536]{1,0:T(8,128)(2,1)S(1)} %bitcast.24, ...), custom_call_target="tpu_custom_call" | custom-call | flops 150000000 | bytes 1000000 | tf_op jit(solution)/shard_map/pallas_call | solution.py:461
  93.2 0.0 copy-start.10
  93.2 2.5 %shard_map.169 = (s16[104,1536]{1,0:T(8,128)(2,1)S(1)}, s16[104,1536]{1,0:T(8,128)(2,1)S(1)}, bf16[128,1536]{1,0:T(8,128)(2,1)}) custom-call(s32[9]{0:T(128)S(1)} %dynamic-slice_reduce_fusion.live_ref, f32[32,128]{1,0:T(8,128)S(1)} %copy-done.7, bf16[128,1536]{1,0:T(8,128)(2,1)S(1)} %bitcast.17, bf16[128,1536]{1,0:T(8,128)(2,1)S(1)} %bitcast.21, ...), custom_call_target="tpu_custom_call" | custom-call | flops 100000000 | bytes 1000000 | tf_op jit(solution)/shard_map/pallas_call | solution.py:461
  95.7 1.7 %collective-permute-start.4 = (s16[104,1536]{1,0:T(8,128)(2,1)S(1)}, s16[104,1536]{1,0:T(8,128)(2,1)S(1)}, u32[]{:S(2)}, u32[]{:S(2)}) collective-permute-start(s16[104,1536]{1,0:T(8,128)(2,1)S(1)} %get-tuple-element.35), channel_id=1, source_target_pairs={{0,16},{16,32},{32,48},{48,64},{64,80},{80,96},{96,112},{112,128},... | collective-permute-start | bytes 958472 | tf_op jit(solution)/shard_map/ppermute | solution.py:476
  97.4 3.9 %collective-permute-done.4.above_ref = s16[104,1536]{1,0:T(8,128)(2,1)S(1)} collective-permute-done((s16[104,1536]{1,0:T(8,128)(2,1)S(1)}, s16[104,1536]{1,0:T(8,128)(2,1)S(1)}, u32[]{:S(2)}, u32[]{:S(2)}) %collective-permute-start.4) | collective-permute-done | bytes 319520 | tf_op jit(solution)/shard_map/ppermute | solution.py:476
  101.3 2.6 %collective-permute-done.5.below_ref = s16[104,1536]{1,0:T(8,128)(2,1)S(1)} collective-permute-done((s16[104,1536]{1,0:T(8,128)(2,1)S(1)}, s16[104,1536]{1,0:T(8,128)(2,1)S(1)}, u32[]{:S(2)}, u32[]{:S(2)}) %collective-permute-start.5) | collective-permute-done | bytes 319520 | tf_op jit(solution)/shard_map/ppermute | solution.py:476
  104.0 1.0 shard_map.171
  104.9 3.0 %collective-permute-start.6 = (s16[72,1536]{1,0:T(8,128)(2,1)S(1)}, s16[72,1536]{1,0:T(8,128)(2,1)S(1)}, u32[]{:S(2)}, u32[]{:S(2)}) collective-permute-start(s16[72,1536]{1,0:T(8,128)(2,1)S(1)} %get-tuple-element.42), channel_id=1, source_target_pairs={{0,1},{1,2},{2,3},{3,4},{4,5},{5,6},{6,7},{7,8},{8,9},{9,10},{10,1... | collective-permute-start | bytes 663560 | tf_op jit(solution)/shard_map/ppermute | solution.py:476
  107.9 3.6 %collective-permute-start.7 = (s16[72,1536]{1,0:T(8,128)(2,1)S(1)}, s16[72,1536]{1,0:T(8,128)(2,1)S(1)}, u32[]{:S(2)}, u32[]{:S(2)}) collective-permute-start(s16[72,1536]{1,0:T(8,128)(2,1)S(1)} %get-tuple-element.43), channel_id=1, source_target_pairs={{0,15},{1,0},{2,1},{3,2},{4,3},{5,4},{6,5},{7,6},{8,7},{9,8},{10,9... | collective-permute-start | bytes 663560 | tf_op jit(solution)/shard_map/ppermute | solution.py:476
  111.5 0.2 shard_map.170
  111.7 2.9 %collective-permute-done.6.left_ref = s16[72,1536]{1,0:T(8,128)(2,1)S(1)} collective-permute-done((s16[72,1536]{1,0:T(8,128)(2,1)S(1)}, s16[72,1536]{1,0:T(8,128)(2,1)S(1)}, u32[]{:S(2)}, u32[]{:S(2)}) %collective-permute-start.6) | collective-permute-done | bytes 221216 | tf_op jit(solution)/shard_map/ppermute | solution.py:476
  114.7 1.8 %collective-permute-done.7.right_ref = s16[72,1536]{1,0:T(8,128)(2,1)S(1)} collective-permute-done((s16[72,1536]{1,0:T(8,128)(2,1)S(1)}, s16[72,1536]{1,0:T(8,128)(2,1)S(1)}, u32[]{:S(2)}, u32[]{:S(2)}) %collective-permute-start.7) | collective-permute-done | bytes 221216 | tf_op jit(solution)/shard_map/ppermute | solution.py:476
  116.5 1.4 %shard_map.172 = (bf16[128,1536]{1,0:T(8,128)(2,1)}, bf16[128,1536]{1,0:T(8,128)(2,1)}) custom-call(bf16[128,64]{1,0:T(8,128)(2,1)S(1)} %copy-done.9, f32[128,1536]{1,0:T(8,128)S(1)} %get-tuple-element.39.own_key_ref, f32[128,1536]{1,0:T(8,128)S(1)} %get-tuple-element.40.own_value_ref, s16[72,1536]{1,0:T(8,128)(2,1)S(1)} %collective-permute-done.6.left_ref, ...), custom_call_target="tpu_custom_call" | custom-call | flops 50000000 | bytes 1000000 | tf_op jit(solution)/shard_map/pallas_call | solution.py:461
  117.8 0.7 shard_map.175
  (27 shorter events, 0.1 us)
Async XLA Ops:
  0.6 88.5 %copy-start = (s32[16,16,9]{1,0,2:T(8,128)S(1)}, s32[16,16,9]{1,0,2:T(8,128)}, u32[]{:S(2)}) copy-start(s32[16,16,9]{1,0,2:T(8,128)} %param.21) | copy-start | bytes 27652
  0.6 48.6 %copy-start.4 = (bf16[2,8,8,1536]{3,2,1,0:T(8,128)(2,1)S(1)}, bf16[2,8,8,1536]{3,2,1,0:T(8,128)(2,1)}, u32[]{:S(2)}) copy-start(bf16[2,8,8,1536]{3,2,1,0:T(8,128)(2,1)} %param.15) | copy-start | bytes 1179652
  3.9 45.4 %copy-start.3 = (bf16[2,8,8,1536]{3,2,1,0:T(8,128)(2,1)S(1)}, bf16[2,8,8,1536]{3,2,1,0:T(8,128)(2,1)}, u32[]{:S(2)}) copy-start(bf16[2,8,8,1536]{3,2,1,0:T(8,128)(2,1)} %param.14) | copy-start | bytes 1179652
  3.9 45.4 %copy-start.11 = (bf16[2,32,128]{2,1,0:T(8,128)(2,1)S(1)}, bf16[2,32,128]{2,1,0:T(8,128)(2,1)}, u32[]{:S(2)}) copy-start(bf16[2,32,128]{2,1,0:T(8,128)(2,1)} %constant.30.clone.select_ref) | copy-start | bytes 49156
  3.9 56.9 %all-to-all-start = ((s16[32,32,128]{2,1,0:T(8,128)(2,1)}), s16[32,32,128]{2,1,0:T(8,128)(2,1)S(1)}, u32[]{:S(2)}, u32[]{:S(2)}) async-start(s16[32,32,128]{2,1,0:T(8,128)(2,1)} %bitcast.28), calls=%async_computation | async-start | bytes 524288 | tf_op jit(solution)/shard_map/all_to_all | solution.py:484
  49.6 19.7 %collective-permute-start = (bf16[64,1536]{1,0:T(8,128)(2,1)S(1)}, bf16[64,1536]{1,0:T(8,128)(2,1)S(1)}, u32[]{:S(2)}, u32[]{:S(2)}) collective-permute-start(bf16[64,1536]{1,0:T(8,128)(2,1)S(1)} %get-tuple-element.28), channel_id=1, source_target_pairs={{0,1},{1,2},{2,3},{3,4},{4,5},{5,6},{6,7},{7,8},{8,9},{9,10},{10,1... | collective-permute-start | bytes 589832 | tf_op jit(solution)/shard_map/ppermute | solution.py:476
  53.0 16.4 %collective-permute-start.1 = (bf16[64,1536]{1,0:T(8,128)(2,1)S(1)}, bf16[64,1536]{1,0:T(8,128)(2,1)S(1)}, u32[]{:S(2)}, u32[]{:S(2)}) collective-permute-start(bf16[64,1536]{1,0:T(8,128)(2,1)S(1)} %get-tuple-element.29), channel_id=1, source_target_pairs={{0,15},{1,0},{2,1},{3,2},{4,3},{5,4},{6,5},{7,6},{8,7},{9,8},{10,9... | collective-permute-start | bytes 589832 | tf_op jit(solution)/shard_map/ppermute | solution.py:476
  61.6 7.8 %copy-start.8 = (bf16[2,48,192]{2,1,0:T(8,128)(2,1)S(1)}, bf16[2,48,192]{2,1,0:T(8,128)(2,1)}, u32[]{:S(2)}) copy-start(bf16[2,48,192]{2,1,0:T(8,128)(2,1)} %constant.31.clone.select_ref) | copy-start | bytes 110596
  61.6 20.3 %all-to-all-start.1 = ((s16[8,32,128]{2,1,0:T(8,128)(2,1)}), s16[8,32,128]{2,1,0:T(8,128)(2,1)S(1)}, u32[]{:S(2)}, u32[]{:S(2)}) async-start(s16[8,32,128]{2,1,0:T(8,128)(2,1)} %shard_map.173), calls=%async_computation.1 | async-start | bytes 131072 | tf_op jit(solution)/shard_map/all_to_all | solution.py:484
  69.4 20.1 %copy-start.2 = (bf16[2,8,8,1536]{3,2,1,0:T(8,128)(2,1)S(1)}, bf16[2,8,8,1536]{3,2,1,0:T(8,128)(2,1)}, u32[]{:S(2)}) copy-start(bf16[2,8,8,1536]{3,2,1,0:T(8,128)(2,1)} %param.16) | copy-start | bytes 1179652
  69.9 19.6 %copy-start.1 = (bf16[2,8,8,1536]{3,2,1,0:T(8,128)(2,1)S(1)}, bf16[2,8,8,1536]{3,2,1,0:T(8,128)(2,1)}, u32[]{:S(2)}) copy-start(bf16[2,8,8,1536]{3,2,1,0:T(8,128)(2,1)} %param.13) | copy-start | bytes 1179652
  69.9 23.3 %collective-permute-start.2 = (bf16[96,1536]{1,0:T(8,128)(2,1)S(1)}, bf16[96,1536]{1,0:T(8,128)(2,1)S(1)}, u32[]{:S(2)}, u32[]{:S(2)}) collective-permute-start(bf16[96,1536]{1,0:T(8,128)(2,1)S(1)} %get-tuple-element.30), channel_id=1, source_target_pairs={{0,16},{16,32},{32,48},{48,64},{64,80},{80,96},{96,112},{112,128},... | collective-permute-start | bytes 884744 | tf_op jit(solution)/shard_map/ppermute | solution.py:476
  71.6 21.6 %collective-permute-start.3 = (bf16[96,1536]{1,0:T(8,128)(2,1)S(1)}, bf16[96,1536]{1,0:T(8,128)(2,1)S(1)}, u32[]{:S(2)}, u32[]{:S(2)}) collective-permute-start(bf16[96,1536]{1,0:T(8,128)(2,1)S(1)} %get-tuple-element.31), channel_id=1, source_target_pairs={{0,240},{16,0},{32,16},{48,32},{64,48},{80,64},{96,80},{112,96},{1... | collective-permute-start | bytes 884744 | tf_op jit(solution)/shard_map/ppermute | solution.py:476
  82.6 35.3 %all-to-all-start.2 = ((bf16[32,24,128]{2,1,0:T(8,128)(2,1)}), bf16[32,24,128]{2,1,0:T(8,128)(2,1)S(1)}, u32[]{:S(2)}, u32[]{:S(2)}) async-start(bf16[32,24,128]{2,1,0:T(8,128)(2,1)} %shard_map.174), calls=%async_computation.2 | async-start | bytes 393216 | tf_op jit(solution)/shard_map/all_to_all | solution.py:484
  89.1 0.7 copy-start.7
  89.9 1.6 %copy-start.5 = (bf16[32,1536]{1,0:T(8,128)(2,1)S(1)}, bf16[32,1536]{1,0:T(8,128)(2,1)}, u32[]{:S(2)}) copy-start(bf16[32,1536]{1,0:T(8,128)(2,1)} %text_key_ref.1) | copy-start | bytes 294916
  89.9 1.6 %copy-start.6 = (bf16[32,1536]{1,0:T(8,128)(2,1)S(1)}, bf16[32,1536]{1,0:T(8,128)(2,1)}, u32[]{:S(2)}) copy-start(bf16[32,1536]{1,0:T(8,128)(2,1)} %text_value_ref.1) | copy-start | bytes 294916
  93.2 10.8 %copy-start.10 = (bf16[64,96]{1,0:T(8,128)(2,1)S(1)}, bf16[64,96]{1,0:T(8,128)(2,1)}, u32[]{:S(2)}) copy-start(bf16[64,96]{1,0:T(8,128)(2,1)} %constant.32.clone.select_ref) | copy-start | bytes 36868
  95.7 5.6 %collective-permute-start.4 = (s16[104,1536]{1,0:T(8,128)(2,1)S(1)}, s16[104,1536]{1,0:T(8,128)(2,1)S(1)}, u32[]{:S(2)}, u32[]{:S(2)}) collective-permute-start(s16[104,1536]{1,0:T(8,128)(2,1)S(1)} %get-tuple-element.35), channel_id=1, source_target_pairs={{0,16},{16,32},{32,48},{48,64},{64,80},{80,96},{96,112},{112,128},... | collective-permute-start | bytes 958472 | tf_op jit(solution)/shard_map/ppermute | solution.py:476
  97.4 6.6 %collective-permute-start.5 = (s16[104,1536]{1,0:T(8,128)(2,1)S(1)}, s16[104,1536]{1,0:T(8,128)(2,1)S(1)}, u32[]{:S(2)}, u32[]{:S(2)}) collective-permute-start(s16[104,1536]{1,0:T(8,128)(2,1)S(1)} %get-tuple-element.36), channel_id=1, source_target_pairs={{0,240},{16,0},{32,16},{48,32},{64,48},{80,64},{96,80},{112,96},{1... | collective-permute-start | bytes 958472 | tf_op jit(solution)/shard_map/ppermute | solution.py:476
  104.9 9.7 %collective-permute-start.6 = (s16[72,1536]{1,0:T(8,128)(2,1)S(1)}, s16[72,1536]{1,0:T(8,128)(2,1)S(1)}, u32[]{:S(2)}, u32[]{:S(2)}) collective-permute-start(s16[72,1536]{1,0:T(8,128)(2,1)S(1)} %get-tuple-element.42), channel_id=1, source_target_pairs={{0,1},{1,2},{2,3},{3,4},{4,5},{5,6},{6,7},{7,8},{8,9},{9,10},{10,1... | collective-permute-start | bytes 663560 | tf_op jit(solution)/shard_map/ppermute | solution.py:476
  107.9 8.5 %collective-permute-start.7 = (s16[72,1536]{1,0:T(8,128)(2,1)S(1)}, s16[72,1536]{1,0:T(8,128)(2,1)S(1)}, u32[]{:S(2)}, u32[]{:S(2)}) collective-permute-start(s16[72,1536]{1,0:T(8,128)(2,1)S(1)} %get-tuple-element.43), channel_id=1, source_target_pairs={{0,15},{1,0},{2,1},{3,2},{4,3},{5,4},{6,5},{7,6},{8,7},{9,8},{10,9... | collective-permute-start | bytes 663560 | tf_op jit(solution)/shard_map/ppermute | solution.py:476
  111.5 5.0 %copy-start.9 = (bf16[128,64]{1,0:T(8,128)(2,1)S(1)}, bf16[128,64]{1,0:T(8,128)(2,1)}, u32[]{:S(2)}) copy-start(bf16[128,64]{1,0:T(8,128)(2,1)} %constant.33.clone.select_ref) | copy-start | bytes 49156

commit v10 on v8

--- a/solution.py
+++ b/solution.py
@@ -256,7 +256,8 @@
     stats_ref,
     part_ref,
     query_grad_ref,
-    own_ref,
+    own_key_ref,
+    own_value_ref,
 ):
     text = text_key_ref.shape[0]
     rows = lax.broadcasted_iota(jnp.int32, (OWN + text, HDIM), 0)
@@ -272,8 +273,8 @@
     def store(h, q, g, k, probs, score_grad):
         cols = columns(h)
         query_grad_ref[:, cols] = part_ref[:, cols] + tn(score_grad, k)
-        own_ref[:OWN, cols] = nn(score_grad[:OWN], q) * SCALE
-        own_ref[OWN:, cols] = nn(probs[:OWN], g)
+        own_key_ref[:, cols] = nn(score_grad[:OWN], q) * SCALE
+        own_value_ref[:, cols] = nn(probs[:OWN], g)
 
     backward(load, store, live)
 
@@ -384,14 +385,23 @@
 
 
 def sum_kernel(
-    select_ref, own_ref, left_ref, right_ref, above_ref, below_ref, key_ref, value_ref
+    select_ref,
+    own_key_ref,
+    own_value_ref,
+    left_ref,
+    right_ref,
+    above_ref,
+    below_ref,
+    key_ref,
+    value_ref,
 ):
+    own_refs = (own_key_ref, own_value_ref)
     edge = HALO * TILE
     for part, out in enumerate((key_ref, value_ref)):
         above, below = received(above_ref, part, ENDS), received(below_ref, part, ENDS)
         sides = [received(ref, part, SIDE) for ref in (left_ref, right_ref)]
         rows = jnp.concatenate(sides, axis=0)
-        total = own_ref[part * OWN : (part + 1) * OWN, :] + picked(select_ref[...], rows)
+        total = own_refs[part][...] + picked(select_ref[...], rows)
         for frame in range(FRAMES):
             at = frame * BAND
             top = frame * TILE * TILE
@@ -537,9 +547,9 @@
         us=2,
         smem=1,
     )
-    part, own = call(
+    part, own_key, own_value = call(
         own_kernel,
-        [((OWN, width), F32), ((2 * OWN, width), F32)],
+        [((OWN, width), F32)] * 3,
         [live, q, g, k, v, text_keys, text_values, stats, part],
         us=3,
         smem=1,
@@ -565,7 +575,7 @@
     key_grad, value_grad = call(
         sum_kernel,
         [((OWN, width), BF16)] * 2,
-        [jnp.asarray(back, BF16), own, before, after, above, below],
+        [jnp.asarray(back, BF16), own_key, own_value, before, after, above, below],
     )
     return (
         query_grad.reshape(shape),

time: 118 us -> 119 us (level)
  transfers between devices with their start and end apart: 11 -> 11, of which waited for: 6 -> 6; matrix products, arithmetic and copies ran while one was open for 0% -> 0% of each run, Pallas kernels for 10% -> 9%
where the time goes in v10:
time: 119 us
  starting transfers between devices  80.3 us (67%)
  waiting for transfers between devices  22.3 us (19%)
  Pallas kernels  14.4 us (12%)
    all_to_all x3, starting transfers between devices, exchanged(): return lax.all_to_all(pieces, axis, 0, 0, tiled=True)  59.7 us
    ppermute x8, starting transfers between devices, shifted(): lax.ppermute(value, axis, [(i, (i + steps) % count) for i in range(count)])  20.6 us
    pallas_call x11, Pallas kernels, call(): pl.pallas_call(function, out_shape=[jax.ShapeDtypeStruct(shape, dtype) fo...  14.4 us
    ppermute x8, waiting for transfers between devices, shifted(): lax.ppermute(value, axis, [(i, (i + steps) % count) for i in range(count)])  11.5 us
    all_to_all x3, waiting for transfers between devices, exchanged(): return lax.all_to_all(pieces, axis, 0, 0, tiled=True)  10.7 us
  transfers between devices with their start and end apart: 11, of which 6 were waited for; matrix products, arithmetic and copies ran while one was open for 0% of the time, Pallas kernels for 9%

profile of v10, /device:TPU:65, one launch (start us, length us, event | category | flops | bytes accessed | tf_op | source)
XLA Modules:
  0.0 118.6 jit_solution(7415345653264259598)
XLA Ops:
  0.6 0.0 copy-start
  0.7 3.2 %shard_map.164 = (s16[1024,128]{1,0:T(8,128)(2,1)}, f32[32,128]{1,0:T(8,128)}) custom-call(f32[128,12]{1,0:T(8,128)} %bitcast.29, f32[128,12]{1,0:T(8,128)} %bitcast.30, bf16[128,1536]{1,0:T(8,128)(2,1)} %bitcast.14, bf16[128,1536]{1,0:T(8,128)(2,1)} %bitcast.18, bf16[32,1536]{1,0:T(8,128)(2,1)} %text_key_ref.1, bf16[32,1536]{1,0:T(8,128)(2,1)} %text_value_ref.1), custom_call_target="tpu_custom_call" | custom-call | flops 150000000 | bytes 1000000 | tf_op jit(solution)/shard_map/pallas_call | solution.py:469
  3.9 0.0 copy-start.11
  3.9 45.4 %all-to-all-start = ((s16[32,32,128]{2,1,0:T(8,128)(2,1)}), s16[32,32,128]{2,1,0:T(8,128)(2,1)S(1)}, u32[]{:S(2)}, u32[]{:S(2)}) async-start(s16[32,32,128]{2,1,0:T(8,128)(2,1)} %bitcast.28), calls=%async_computation | async-start | bytes 524288 | tf_op jit(solution)/shard_map/all_to_all | solution.py:492
  49.3 0.3 shard_map.165
  49.6 3.3 %collective-permute-start = (bf16[64,1536]{1,0:T(8,128)(2,1)S(1)}, bf16[64,1536]{1,0:T(8,128)(2,1)S(1)}, u32[]{:S(2)}, u32[]{:S(2)}) collective-permute-start(bf16[64,1536]{1,0:T(8,128)(2,1)S(1)} %get-tuple-element.26), channel_id=1, source_target_pairs={{0,1},{1,2},{2,3},{3,4},{4,5},{5,6},{6,7},{7,8},{8,9},{9,10},{10,1... | collective-permute-start | bytes 589832 | tf_op jit(solution)/shard_map/ppermute | solution.py:484
  52.9 7.4 %collective-permute-start.1 = (bf16[64,1536]{1,0:T(8,128)(2,1)S(1)}, bf16[64,1536]{1,0:T(8,128)(2,1)S(1)}, u32[]{:S(2)}, u32[]{:S(2)}) collective-permute-start(bf16[64,1536]{1,0:T(8,128)(2,1)S(1)} %get-tuple-element.27), channel_id=1, source_target_pairs={{0,15},{1,0},{2,1},{3,2},{4,3},{5,4},{6,5},{7,6},{8,7},{9,8},{10,9... | collective-permute-start | bytes 589832 | tf_op jit(solution)/shard_map/ppermute | solution.py:484
  60.3 0.5 all-to-all-done.parts_ref
  60.8 0.8 shard_map.172
  61.6 7.7 %all-to-all-start.1 = ((s16[8,32,128]{2,1,0:T(8,128)(2,1)}), s16[8,32,128]{2,1,0:T(8,128)(2,1)S(1)}, u32[]{:S(2)}, u32[]{:S(2)}) async-start(s16[8,32,128]{2,1,0:T(8,128)(2,1)} %shard_map.172), calls=%async_computation.1 | async-start | bytes 131072 | tf_op jit(solution)/shard_map/all_to_all | solution.py:492
  69.4 0.5 shard_map.166
  69.9 0.0 copy-start.1
  69.9 1.7 %collective-permute-start.2 = (bf16[96,1536]{1,0:T(8,128)(2,1)S(1)}, bf16[96,1536]{1,0:T(8,128)(2,1)S(1)}, u32[]{:S(2)}, u32[]{:S(2)}) collective-permute-start(bf16[96,1536]{1,0:T(8,128)(2,1)S(1)} %get-tuple-element.28), channel_id=1, source_target_pairs={{0,16},{16,32},{32,48},{48,64},{64,80},{80,96},{96,112},{112,128},... | collective-permute-start | bytes 884744 | tf_op jit(solution)/shard_map/ppermute | solution.py:484
  71.6 10.2 %all-to-all-done.1.parts_ref = s16[8,32,128]{2,1,0:T(8,128)(2,1)S(1)} async-done(((s16[8,32,128]{2,1,0:T(8,128)(2,1)}), s16[8,32,128]{2,1,0:T(8,128)(2,1)S(1)}, u32[]{:S(2)}, u32[]{:S(2)}) %all-to-all-start.1) | async-done | bytes 65568 | tf_op jit(solution)/shard_map/all_to_all | solution.py:492
  81.9 0.7 shard_map.173
  82.6 6.6 %all-to-all-start.2 = ((bf16[32,24,128]{2,1,0:T(8,128)(2,1)}), bf16[32,24,128]{2,1,0:T(8,128)(2,1)S(1)}, u32[]{:S(2)}, u32[]{:S(2)}) async-start(bf16[32,24,128]{2,1,0:T(8,128)(2,1)} %shard_map.173), calls=%async_computation.2 | async-start | bytes 393216 | tf_op jit(solution)/shard_map/all_to_all | solution.py:492
  89.2 0.3 dynamic-slice_reduce_fusion.live_ref
  89.5 0.3 copy-done.7
  89.9 1.6 %shard_map.167 = (s16[144,1536]{1,0:T(8,128)(2,1)S(1)}, f32[128,1536]{1,0:T(8,128)S(1)}) custom-call(s32[9]{0:T(128)S(1)} %dynamic-slice_reduce_fusion.live_ref, f32[32,128]{1,0:T(8,128)S(1)} %copy-done.7, bf16[128,1536]{1,0:T(8,128)(2,1)S(1)} %bitcast.15, bf16[128,1536]{1,0:T(8,128)(2,1)S(1)} %bitcast.19, ...), custom_call_target="tpu_custom_call" | custom-call | flops 100000000 | bytes 1000000 | tf_op jit(solution)/shard_map/pallas_call | solution.py:469
  91.5 1.7 %shard_map.168 = (f32[128,1536]{1,0:T(8,128)S(1)}, f32[128,1536]{1,0:T(8,128)S(1)}, f32[128,1536]{1,0:T(8,128)S(1)}) custom-call(s32[9]{0:T(128)S(1)} %dynamic-slice_reduce_fusion.live_ref, bf16[128,1536]{1,0:T(8,128)(2,1)S(1)} %bitcast.16, bf16[128,1536]{1,0:T(8,128)(2,1)S(1)} %bitcast.20, bf16[128,1536]{1,0:T(8,128)(2,1)S(1)} %bitcast.24, ...), custom_call_target="tpu_custom_call" | custom-call | flops 150000000 | bytes 1000000 | tf_op jit(solution)/shard_map/pallas_call | solution.py:469
  93.2 0.0 copy-start.10
  93.2 2.5 %shard_map.169 = (s16[104,1536]{1,0:T(8,128)(2,1)S(1)}, s16[104,1536]{1,0:T(8,128)(2,1)S(1)}, bf16[128,1536]{1,0:T(8,128)(2,1)}) custom-call(s32[9]{0:T(128)S(1)} %dynamic-slice_reduce_fusion.live_ref, f32[32,128]{1,0:T(8,128)S(1)} %copy-done.7, bf16[128,1536]{1,0:T(8,128)(2,1)S(1)} %bitcast.17, bf16[128,1536]{1,0:T(8,128)(2,1)S(1)} %bitcast.21, ...), custom_call_target="tpu_custom_call" | custom-call | flops 100000000 | bytes 1000000 | tf_op jit(solution)/shard_map/pallas_call | solution.py:469
  95.7 1.7 %collective-permute-start.4 = (s16[104,1536]{1,0:T(8,128)(2,1)S(1)}, s16[104,1536]{1,0:T(8,128)(2,1)S(1)}, u32[]{:S(2)}, u32[]{:S(2)}) collective-permute-start(s16[104,1536]{1,0:T(8,128)(2,1)S(1)} %get-tuple-element.36), channel_id=1, source_target_pairs={{0,16},{16,32},{32,48},{48,64},{64,80},{80,96},{96,112},{112,128},... | collective-permute-start | bytes 958472 | tf_op jit(solution)/shard_map/ppermute | solution.py:484
  97.4 3.9 %collective-permute-done.4.above_ref = s16[104,1536]{1,0:T(8,128)(2,1)S(1)} collective-permute-done((s16[104,1536]{1,0:T(8,128)(2,1)S(1)}, s16[104,1536]{1,0:T(8,128)(2,1)S(1)}, u32[]{:S(2)}, u32[]{:S(2)}) %collective-permute-start.4) | collective-permute-done | bytes 319520 | tf_op jit(solution)/shard_map/ppermute | solution.py:484
  101.4 2.6 %collective-permute-done.5.below_ref = s16[104,1536]{1,0:T(8,128)(2,1)S(1)} collective-permute-done((s16[104,1536]{1,0:T(8,128)(2,1)S(1)}, s16[104,1536]{1,0:T(8,128)(2,1)S(1)}, u32[]{:S(2)}, u32[]{:S(2)}) %collective-permute-start.5) | collective-permute-done | bytes 319520 | tf_op jit(solution)/shard_map/ppermute | solution.py:484
  104.0 0.9 shard_map.170
  104.9 3.0 %collective-permute-start.6 = (s16[72,1536]{1,0:T(8,128)(2,1)S(1)}, s16[72,1536]{1,0:T(8,128)(2,1)S(1)}, u32[]{:S(2)}, u32[]{:S(2)}) collective-permute-start(s16[72,1536]{1,0:T(8,128)(2,1)S(1)} %get-tuple-element.38), channel_id=1, source_target_pairs={{0,1},{1,2},{2,3},{3,4},{4,5},{5,6},{6,7},{7,8},{8,9},{9,10},{10,1... | collective-permute-start | bytes 663560 | tf_op jit(solution)/shard_map/ppermute | solution.py:484
  107.9 3.6 %collective-permute-start.7 = (s16[72,1536]{1,0:T(8,128)(2,1)S(1)}, s16[72,1536]{1,0:T(8,128)(2,1)S(1)}, u32[]{:S(2)}, u32[]{:S(2)}) collective-permute-start(s16[72,1536]{1,0:T(8,128)(2,1)S(1)} %get-tuple-element.39), channel_id=1, source_target_pairs={{0,15},{1,0},{2,1},{3,2},{4,3},{5,4},{6,5},{7,6},{8,7},{9,8},{10,9... | collective-permute-start | bytes 663560 | tf_op jit(solution)/shard_map/ppermute | solution.py:484
  111.5 3.1 %collective-permute-done.6.left_ref = s16[72,1536]{1,0:T(8,128)(2,1)S(1)} collective-permute-done((s16[72,1536]{1,0:T(8,128)(2,1)S(1)}, s16[72,1536]{1,0:T(8,128)(2,1)S(1)}, u32[]{:S(2)}, u32[]{:S(2)}) %collective-permute-start.6) | collective-permute-done | bytes 221216 | tf_op jit(solution)/shard_map/ppermute | solution.py:484
  114.7 1.8 %collective-permute-done.7.right_ref = s16[72,1536]{1,0:T(8,128)(2,1)S(1)} collective-permute-done((s16[72,1536]{1,0:T(8,128)(2,1)S(1)}, s16[72,1536]{1,0:T(8,128)(2,1)S(1)}, u32[]{:S(2)}, u32[]{:S(2)}) %collective-permute-start.7) | collective-permute-done | bytes 221216 | tf_op jit(solution)/shard_map/ppermute | solution.py:484
  116.5 1.4 %shard_map.171 = (bf16[128,1536]{1,0:T(8,128)(2,1)}, bf16[128,1536]{1,0:T(8,128)(2,1)}) custom-call(bf16[128,64]{1,0:T(8,128)(2,1)S(1)} %copy-done.9, f32[128,1536]{1,0:T(8,128)S(1)} %get-tuple-element.33.own_key_ref, f32[128,1536]{1,0:T(8,128)S(1)} %get-tuple-element.34.own_value_ref, s16[72,1536]{1,0:T(8,128)(2,1)S(1)} %collective-permute-done.6.left_ref, ...), custom_call_target="tpu_custom_call" | custom-call | flops 50000000 | bytes 1000000 | tf_op jit(solution)/shard_map/pallas_call | solution.py:469
  117.9 0.7 shard_map.174
  (26 shorter events, 0.1 us)
Async XLA Ops:
  0.6 88.5 %copy-start = (s32[16,16,9]{1,0,2:T(8,128)S(1)}, s32[16,16,9]{1,0,2:T(8,128)}, u32[]{:S(2)}) copy-start(s32[16,16,9]{1,0,2:T(8,128)} %param.21) | copy-start | bytes 27652
  0.6 48.6 %copy-start.4 = (bf16[2,8,8,1536]{3,2,1,0:T(8,128)(2,1)S(1)}, bf16[2,8,8,1536]{3,2,1,0:T(8,128)(2,1)}, u32[]{:S(2)}) copy-start(bf16[2,8,8,1536]{3,2,1,0:T(8,128)(2,1)} %param.15) | copy-start | bytes 1179652
  3.9 45.4 %copy-start.3 = (bf16[2,8,8,1536]{3,2,1,0:T(8,128)(2,1)S(1)}, bf16[2,8,8,1536]{3,2,1,0:T(8,128)(2,1)}, u32[]{:S(2)}) copy-start(bf16[2,8,8,1536]{3,2,1,0:T(8,128)(2,1)} %param.14) | copy-start | bytes 1179652
  3.9 45.4 %copy-start.11 = (bf16[2,32,128]{2,1,0:T(8,128)(2,1)S(1)}, bf16[2,32,128]{2,1,0:T(8,128)(2,1)}, u32[]{:S(2)}) copy-start(bf16[2,32,128]{2,1,0:T(8,128)(2,1)} %constant.30.clone.select_ref) | copy-start | bytes 49156
  3.9 56.9 %all-to-all-start = ((s16[32,32,128]{2,1,0:T(8,128)(2,1)}), s16[32,32,128]{2,1,0:T(8,128)(2,1)S(1)}, u32[]{:S(2)}, u32[]{:S(2)}) async-start(s16[32,32,128]{2,1,0:T(8,128)(2,1)} %bitcast.28), calls=%async_computation | async-start | bytes 524288 | tf_op jit(solution)/shard_map/all_to_all | solution.py:492
  49.6 19.7 %collective-permute-start = (bf16[64,1536]{1,0:T(8,128)(2,1)S(1)}, bf16[64,1536]{1,0:T(8,128)(2,1)S(1)}, u32[]{:S(2)}, u32[]{:S(2)}) collective-permute-start(bf16[64,1536]{1,0:T(8,128)(2,1)S(1)} %get-tuple-element.26), channel_id=1, source_target_pairs={{0,1},{1,2},{2,3},{3,4},{4,5},{5,6},{6,7},{7,8},{8,9},{9,10},{10,1... | collective-permute-start | bytes 589832 | tf_op jit(solution)/shard_map/ppermute | solution.py:484
  52.9 16.4 %collective-permute-start.1 = (bf16[64,1536]{1,0:T(8,128)(2,1)S(1)}, bf16[64,1536]{1,0:T(8,128)(2,1)S(1)}, u32[]{:S(2)}, u32[]{:S(2)}) collective-permute-start(bf16[64,1536]{1,0:T(8,128)(2,1)S(1)} %get-tuple-element.27), channel_id=1, source_target_pairs={{0,15},{1,0},{2,1},{3,2},{4,3},{5,4},{6,5},{7,6},{8,7},{9,8},{10,9... | collective-permute-start | bytes 589832 | tf_op jit(solution)/shard_map/ppermute | solution.py:484
  61.6 7.8 %copy-start.8 = (bf16[2,48,192]{2,1,0:T(8,128)(2,1)S(1)}, bf16[2,48,192]{2,1,0:T(8,128)(2,1)}, u32[]{:S(2)}) copy-start(bf16[2,48,192]{2,1,0:T(8,128)(2,1)} %constant.31.clone.select_ref) | copy-start | bytes 110596
  61.6 20.3 %all-to-all-start.1 = ((s16[8,32,128]{2,1,0:T(8,128)(2,1)}), s16[8,32,128]{2,1,0:T(8,128)(2,1)S(1)}, u32[]{:S(2)}, u32[]{:S(2)}) async-start(s16[8,32,128]{2,1,0:T(8,128)(2,1)} %shard_map.172), calls=%async_computation.1 | async-start | bytes 131072 | tf_op jit(solution)/shard_map/all_to_all | solution.py:492
  69.4 20.1 %copy-start.2 = (bf16[2,8,8,1536]{3,2,1,0:T(8,128)(2,1)S(1)}, bf16[2,8,8,1536]{3,2,1,0:T(8,128)(2,1)}, u32[]{:S(2)}) copy-start(bf16[2,8,8,1536]{3,2,1,0:T(8,128)(2,1)} %param.16) | copy-start | bytes 1179652
  69.9 19.6 %copy-start.1 = (bf16[2,8,8,1536]{3,2,1,0:T(8,128)(2,1)S(1)}, bf16[2,8,8,1536]{3,2,1,0:T(8,128)(2,1)}, u32[]{:S(2)}) copy-start(bf16[2,8,8,1536]{3,2,1,0:T(8,128)(2,1)} %param.13) | copy-start | bytes 1179652
  69.9 23.3 %collective-permute-start.2 = (bf16[96,1536]{1,0:T(8,128)(2,1)S(1)}, bf16[96,1536]{1,0:T(8,128)(2,1)S(1)}, u32[]{:S(2)}, u32[]{:S(2)}) collective-permute-start(bf16[96,1536]{1,0:T(8,128)(2,1)S(1)} %get-tuple-element.28), channel_id=1, source_target_pairs={{0,16},{16,32},{32,48},{48,64},{64,80},{80,96},{96,112},{112,128},... | collective-permute-start | bytes 884744 | tf_op jit(solution)/shard_map/ppermute | solution.py:484
  71.6 21.6 %collective-permute-start.3 = (bf16[96,1536]{1,0:T(8,128)(2,1)S(1)}, bf16[96,1536]{1,0:T(8,128)(2,1)S(1)}, u32[]{:S(2)}, u32[]{:S(2)}) collective-permute-start(bf16[96,1536]{1,0:T(8,128)(2,1)S(1)} %get-tuple-element.29), channel_id=1, source_target_pairs={{0,240},{16,0},{32,16},{48,32},{64,48},{80,64},{96,80},{112,96},{1... | collective-permute-start | bytes 884744 | tf_op jit(solution)/shard_map/ppermute | solution.py:484
  82.6 35.3 %all-to-all-start.2 = ((bf16[32,24,128]{2,1,0:T(8,128)(2,1)}), bf16[32,24,128]{2,1,0:T(8,128)(2,1)S(1)}, u32[]{:S(2)}, u32[]{:S(2)}) async-start(bf16[32,24,128]{2,1,0:T(8,128)(2,1)} %shard_map.173), calls=%async_computation.2 | async-start | bytes 393216 | tf_op jit(solution)/shard_map/all_to_all | solution.py:492
  89.1 0.7 copy-start.7
  89.9 1.6 %copy-start.5 = (bf16[32,1536]{1,0:T(8,128)(2,1)S(1)}, bf16[32,1536]{1,0:T(8,128)(2,1)}, u32[]{:S(2)}) copy-start(bf16[32,1536]{1,0:T(8,128)(2,1)} %text_key_ref.1) | copy-start | bytes 294916
  89.9 1.6 %copy-start.6 = (bf16[32,1536]{1,0:T(8,128)(2,1)S(1)}, bf16[32,1536]{1,0:T(8,128)(2,1)}, u32[]{:S(2)}) copy-start(bf16[32,1536]{1,0:T(8,128)(2,1)} %text_value_ref.1) | copy-start | bytes 294916
  93.2 10.8 %copy-start.10 = (bf16[64,96]{1,0:T(8,128)(2,1)S(1)}, bf16[64,96]{1,0:T(8,128)(2,1)}, u32[]{:S(2)}) copy-start(bf16[64,96]{1,0:T(8,128)(2,1)} %constant.32.clone.select_ref) | copy-start | bytes 36868
  95.7 5.6 %collective-permute-start.4 = (s16[104,1536]{1,0:T(8,128)(2,1)S(1)}, s16[104,1536]{1,0:T(8,128)(2,1)S(1)}, u32[]{:S(2)}, u32[]{:S(2)}) collective-permute-start(s16[104,1536]{1,0:T(8,128)(2,1)S(1)} %get-tuple-element.36), channel_id=1, source_target_pairs={{0,16},{16,32},{32,48},{48,64},{64,80},{80,96},{96,112},{112,128},... | collective-permute-start | bytes 958472 | tf_op jit(solution)/shard_map/ppermute | solution.py:484
  97.4 6.6 %collective-permute-start.5 = (s16[104,1536]{1,0:T(8,128)(2,1)S(1)}, s16[104,1536]{1,0:T(8,128)(2,1)S(1)}, u32[]{:S(2)}, u32[]{:S(2)}) collective-permute-start(s16[104,1536]{1,0:T(8,128)(2,1)S(1)} %get-tuple-element.37), channel_id=1, source_target_pairs={{0,240},{16,0},{32,16},{48,32},{64,48},{80,64},{96,80},{112,96},{1... | collective-permute-start | bytes 958472 | tf_op jit(solution)/shard_map/ppermute | solution.py:484
  104.0 12.5 %copy-start.9 = (bf16[128,64]{1,0:T(8,128)(2,1)S(1)}, bf16[128,64]{1,0:T(8,128)(2,1)}, u32[]{:S(2)}) copy-start(bf16[128,64]{1,0:T(8,128)(2,1)} %constant.33.clone.select_ref) | copy-start | bytes 49156
  104.9 9.7 %collective-permute-start.6 = (s16[72,1536]{1,0:T(8,128)(2,1)S(1)}, s16[72,1536]{1,0:T(8,128)(2,1)S(1)}, u32[]{:S(2)}, u32[]{:S(2)}) collective-permute-start(s16[72,1536]{1,0:T(8,128)(2,1)S(1)} %get-tuple-element.38), channel_id=1, source_target_pairs={{0,1},{1,2},{2,3},{3,4},{4,5},{5,6},{6,7},{7,8},{8,9},{9,10},{10,1... | collective-permute-start | bytes 663560 | tf_op jit(solution)/shard_map/ppermute | solution.py:484
  107.9 8.5 %collective-permute-start.7 = (s16[72,1536]{1,0:T(8,128)(2,1)S(1)}, s16[72,1536]{1,0:T(8,128)(2,1)S(1)}, u32[]{:S(2)}, u32[]{:S(2)}) collective-permute-start(s16[72,1536]{1,0:T(8,128)(2,1)S(1)} %get-tuple-element.39), channel_id=1, source_target_pairs={{0,15},{1,0},{2,1},{3,2},{4,3},{5,4},{6,5},{7,6},{8,7},{9,8},{10,9... | collective-permute-start | bytes 663560 | tf_op jit(solution)/shard_map/ppermute | solution.py:484
